TPU v7x, 128 devices: a whole 4x4x4 slice. The times are simulated.
128 devices in a mesh: blk: 8 (over x, z_hi), grp: 16 (over z_lo, y, core).
Axes of the slice: x: 4, y: 4, z: 4 (z_hi: 2, z_lo: 2; z = z_hi * 2 + z_lo), core: 2. Of those that a mesh axis runs over, the one named last changes fastest.
Arguments:
- frames: bfloat16 [16384, 8, 2048], P(('blk', 'grp')), may hold values from -6 to 6
- counts: int32 [16384], P(('blk', 'grp')), may hold values from 1 to 8
- positives: int32 [16384], P(('blk', 'grp')), may hold values from 0 to 16383, as said below
- w_first: bfloat16 [2048, 4096], P(None, 'grp'), may hold values from -0.125 to 0.125
- w_second: bfloat16 [4096, 256], P('grp'), may hold values from -0.09375 to 0.09375
Outputs:
- batch_loss: float32 [], replicated
- grad_first: float32 [2048, 4096], P(None, 'grp')
- grad_second: float32 [4096, 256], P('grp')
Inputs may be any that keep to these rules, and one draw needn't show every extreme that they name: positives[positives[i]] = i and positives[i] != i for every clip i.
All inputs are finite; a program needn't handle non-finite values.
Results may differ from a plain program's by a relative error of at most 0.005.
The roundings to bfloat16 on the way count: a program that leaves them out, or rounds other values in their place, can miss the bound.
Values may be sent and summed in bfloat16 or wider, within the bound.
No kernel may reach another device: no remote copies, remote signals or barrier semaphores. Data moves between devices by JAX's collectives and lax.ppermute only.
A program may use at most 128 MiB of HBM per device.

v0:
```python
import jax
import jax.numpy as jnp
from jax import lax
from jax.sharding import Mesh
from jax.sharding import PartitionSpec as P

BLK = ("blk_0", "blk_1")
GRP = ("grp_0", "grp_1", "grp_2")
BLK_GRP = ("blk_0", "blk_1", "grp_0", "grp_1", "grp_2")


logit_sharpness_divisor = 0.05
score_top = 20.0


def in_blocks(array, dim, peers):
    shape = array.shape
    pieces = array.reshape(*shape[:dim], peers, shape[dim] // peers, *shape[dim + 1 :])
    return jnp.moveaxis(pieces, dim, 0)


def sent_and_summed(array, axis, dim):
    peers = lax.axis_size(axis)
    pieces = lax.all_to_all(in_blocks(array, dim, peers), axis, 0, 0, tiled=True)
    return jnp.sum(pieces, axis=0)


def in_order(pieces, dim):
    shape = list(pieces.shape[1:])
    shape[dim] *= pieces.shape[0]
    return jnp.moveaxis(pieces, 0, dim).reshape(shape)


def from_everyone(array, axis):
    peers = lax.axis_size(axis)
    return lax.all_to_all(
        jnp.broadcast_to(array[None], (peers, *array.shape)), axis, 0, 0, tiled=True
    )


def gather_directly(array, axis, dim):
    return in_order(from_everyone(array, axis), dim)


def shifted(block, axis, distance):
    devices = range(lax.axis_size(axis))
    route = [((i - distance) % len(devices), i) for i in devices]
    return lax.ppermute(block, axis, route)


def by_axis(array, axes):
    for axis in axes:
        array = lax.psum(array, axis)
    return array


def shards(frames, counts, positives, w_first, w_second):
    row_count = frames.shape[0]
    slot_count = frames.shape[1]
    cycle_size = lax.axis_size(BLK)
    group_size = lax.axis_size(GRP)
    complete_segment_entries = row_count * cycle_size * group_size
    group_rows = row_count * group_size
    cycle_index = lax.axis_index(BLK)
    first_row = (cycle_index * group_size + lax.axis_index(GRP)) * row_count
    row_ids = first_row + jnp.arange(row_count, dtype=jnp.int32)
    frame_mask = (jnp.arange(slot_count, dtype=jnp.int32)[None, :] < counts[:, None]).astype(
        jnp.bfloat16
    )
    summed = jnp.einsum("rf,rfc->rc", frame_mask, frames, preferred_element_type=jnp.float32)
    pooled = (summed / counts[:, None].astype(jnp.float32)).astype(jnp.bfloat16)
    pooled_all = lax.all_gather(pooled, GRP, axis=0, tiled=True)
    preact = jnp.dot(pooled_all, w_first, preferred_element_type=jnp.float32)
    hidden = jax.nn.gelu(preact).astype(jnp.bfloat16)
    raw_keys = sent_and_summed(
        jnp.dot(hidden, w_second, preferred_element_type=jnp.float32), GRP, 0
    )
    key_length = jnp.sqrt(jnp.sum(raw_keys * raw_keys, axis=1, keepdims=True) + 1e-06)
    unit_keys = raw_keys / key_length
    lower_match_vectors = unit_keys.astype(jnp.bfloat16)
    key_block = gather_directly(lower_match_vectors, GRP, 0)
    block_ids = jnp.arange(group_rows, dtype=jnp.int32)
    exp_total = jnp.zeros((row_count,), jnp.float32)
    pos_score = jnp.zeros((row_count,), jnp.float32)
    stored = []
    for hop_index in range(cycle_size):
        owner = (cycle_index - hop_index) % cycle_size
        offset = owner * group_rows
        key_ids = offset + block_ids
        cosine_logit_matrix = (
            lax.dot_general(
                lower_match_vectors,
                key_block,
                (((1,), (1,)), ((), ())),
                preferred_element_type=jnp.float32,
            )
            / logit_sharpness_divisor
        )
        self_mask = key_ids[None, :] == row_ids[:, None]
        pair_mask = key_ids[None, :] == positives[:, None]
        exp_total = exp_total + jnp.sum(
            jnp.where(self_mask, 0.0, jnp.exp(cosine_logit_matrix - score_top)), axis=1
        )
        pos_score = pos_score + jnp.sum(jnp.where(pair_mask, cosine_logit_matrix, 0.0), axis=1)
        stored.append((key_block, offset, cosine_logit_matrix, self_mask, pair_mask))
        if hop_index + 1 < cycle_size:
            key_block = shifted(key_block, BLK, 1)
    log_norm = jnp.log(exp_total) + score_top
    batch_loss = by_axis(jnp.sum(log_norm - pos_score), BLK_GRP) / complete_segment_entries
    query_gradient = jnp.zeros((row_count, lower_match_vectors.shape[1]), jnp.float32)
    every_norm = lax.all_gather(log_norm, BLK_GRP, axis=0, tiled=True)
    self_key_gradient = jnp.zeros((row_count, lower_match_vectors.shape[1]), jnp.float32)
    for key_block, offset, cosine_logit_matrix, self_mask, pair_mask in stored:
        pair_float = pair_mask.astype(jnp.float32)
        probs = jnp.where(self_mask, 0.0, jnp.exp(cosine_logit_matrix - log_norm[:, None]))
        weights = (probs - pair_float).astype(jnp.bfloat16)
        column_norm = lax.dynamic_slice_in_dim(every_norm, offset, group_rows, 0)
        mirrored = jnp.where(self_mask, 0.0, jnp.exp(cosine_logit_matrix - column_norm[None, :]))
        mirror_weights = (mirrored - pair_float).astype(jnp.bfloat16)
        query_gradient = query_gradient + jnp.dot(
            weights, key_block, preferred_element_type=jnp.float32
        )
        self_key_gradient = self_key_gradient + jnp.dot(
            mirror_weights, key_block, preferred_element_type=jnp.float32
        )
    sphere_projected_derivative = (query_gradient + self_key_gradient) / (
        complete_segment_entries * logit_sharpness_divisor
    )
    raw_grad = (
        (
            sphere_projected_derivative
            - unit_keys * jnp.sum(unit_keys * sphere_projected_derivative, axis=1, keepdims=True)
        )
        / key_length
    ).astype(jnp.bfloat16)
    group_grad = gather_directly(raw_grad, GRP, 0)
    second_grad = lax.dot_general(
        hidden, group_grad, (((0,), (0,)), ((), ())), preferred_element_type=jnp.float32
    )
    hidden_grad = lax.dot_general(
        group_grad, w_second, (((1,), (1,)), ((), ())), preferred_element_type=jnp.float32
    )
    unused, backward = jax.vjp(jax.nn.gelu, preact)
    preact_grad = backward(hidden_grad)[0].astype(jnp.bfloat16)
    first_grad = lax.dot_general(
        pooled_all, preact_grad, (((0,), (0,)), ((), ())), preferred_element_type=jnp.float32
    )
    first_grad, second_grad = lax.psum((first_grad, second_grad), BLK)
    return (batch_loss, first_grad, second_grad)


def solution(mesh):
    finer = Mesh(mesh.devices.reshape(4, 2, 2, 4, 2), ("blk_0", "blk_1", "grp_0", "grp_1", "grp_2"))
    placed = (P(BLK_GRP, None, None), P(BLK_GRP), P(BLK_GRP), P(None, GRP), P(GRP, None))
    return jax.shard_map(
        shards,
        mesh=finer,
        in_specs=placed,
        out_specs=(P(), P(None, GRP), P(GRP, None)),
        check_vma=False,
    )
```

profile of v0, /device:TPU:6, one launch (start us, length us, event | category | flops | bytes accessed | tf_op | source)
XLA Modules:
  0.0 521.7 jit_solution(11916011583549820062)
XLA Ops:
  7.2 0.8 fusion.150
  8.0 0.7 convert_element_type.96
  8.7 3.4 fusion.148
  12.1 1.1 fusion.43
  13.4 54.5 %all-gather.3.cloned.1.call-done = bf16[2048,2048]{1,0:T(8,128)(2,1)} async-done(((bf16[128,2048]{1,0:T(8,128)(2,1)}), bf16[2048,2048]{1,0:T(8,128)(2,1)}) %all-gather.3.cloned.1.call-update) | async-done | bytes 8388624 | tf_op jit(solution)/shard_map/all_gather | solution.py:72
  67.9 5.9 %fusion.179 = f32[2048,256]{1,0:T(8,128)S(1)} fusion(bf16[2048,2048]{1,0:T(8,128)(2,1)} %all-gather.3.cloned.1.call-done, bf16[2048,256]{1,0:T(8,128)(2,1)S(1)} %copy-done), kind=kOutput, calls=%fused_computation.252 | convolution fusion | flops 2147483648 | bytes 11534336 | tf_op jit(solution)/shard_map/dot_general | solution.py:73
  73.8 0.8 fusion.175
  74.5 0.5 copy-done.8
  75.1 32.5 %all_to_all.15 = f32[16,128,256]{2,1,0:T(8,128)S(1)} all-to-all(f32[16,128,256]{2,1,0:T(8,128)S(1)} %bitcast.55), channel_id=1, replica_groups=mesh['blk_0'=4,'blk_1'=2,'grp_0'=2,'grp_1'=4,'grp_2'=2] {'grp_0','grp_1'..., dimensions={0} | all-to-all | bytes 4194304 | tf_op jit(solution)/shard_map/all_to_all | solution.py:24
  108.0 19.1 %all_to_all.16 = bf16[16,128,256]{2,1,0:T(8,128)(2,1)S(1)} all-to-all(bf16[16,128,256]{2,1,0:T(8,128)(2,1)S(1)} %broadcast_in_dim.41), channel_id=1, replica_groups=mesh['blk_0'=4,'blk_1'=2,'grp_0'=2,'grp_1'=4,'grp_2'=2] {'grp_0','grp_1'..., dimensions={0} | all-to-all | bytes 2097152 | tf_op jit(solution)/shard_map/all_to_all | solution.py:36
  127.1 2.9 collective-permute-start
  129.9 23.7 %collective-permute-done = bf16[2048,256]{1,0:T(8,128)(2,1)S(1)} collective-permute-done((bf16[2048,256]{1,0:T(8,128)(2,1)S(1)}, bf16[2048,256]{1,0:T(8,128)(2,1)S(1)}, u32[]{:S(2)}, u32[]{:S(2)}) %collective-permute-start) | collective-permute-done | bytes 1048608 | tf_op jit(solution)/shard_map/ppermute | solution.py:48
  153.7 2.0 collective-permute-start.1
  155.6 23.7 %collective-permute-done.1 = bf16[2048,256]{1,0:T(8,128)(2,1)S(1)} collective-permute-done((bf16[2048,256]{1,0:T(8,128)(2,1)S(1)}, bf16[2048,256]{1,0:T(8,128)(2,1)S(1)}, u32[]{:S(2)}, u32[]{:S(2)}) %collective-permute-start.1) | collective-permute-done | bytes 1048608 | tf_op jit(solution)/shard_map/ppermute | solution.py:48
  179.4 1.1 copy-done.1
  180.4 1.1 collective-permute-start.2
  181.5 23.8 %collective-permute-done.2 = bf16[2048,256]{1,0:T(8,128)(2,1)S(1)} collective-permute-done((bf16[2048,256]{1,0:T(8,128)(2,1)S(1)}, bf16[2048,256]{1,0:T(8,128)(2,1)S(1)}, u32[]{:S(2)}, u32[]{:S(2)}) %collective-permute-start.2) | collective-permute-done | bytes 1048608 | tf_op jit(solution)/shard_map/ppermute | solution.py:48
  205.3 1.0 copy-done.3
  206.2 1.1 collective-permute-start.3
  207.3 23.0 %collective-permute-done.3 = bf16[2048,256]{1,0:T(8,128)(2,1)} collective-permute-done((bf16[2048,256]{1,0:T(8,128)(2,1)S(1)}, bf16[2048,256]{1,0:T(8,128)(2,1)}, u32[]{:S(2)}, u32[]{:S(2)}) %collective-permute-start.3) | collective-permute-done | bytes 1048608 | tf_op jit(solution)/shard_map/ppermute | solution.py:48
  230.3 2.2 collective-permute-start.4
  232.5 21.3 %collective-permute-done.4 = bf16[2048,256]{1,0:T(8,128)(2,1)} collective-permute-done((bf16[2048,256]{1,0:T(8,128)(2,1)}, bf16[2048,256]{1,0:T(8,128)(2,1)}, u32[]{:S(2)}, u32[]{:S(2)}) %collective-permute-start.4) | collective-permute-done | bytes 1048608 | tf_op jit(solution)/shard_map/ppermute | solution.py:48
  253.8 3.5 collective-permute-start.5
  259.0 18.3 %collective-permute-done.5 = bf16[2048,256]{1,0:T(8,128)(2,1)S(1)} collective-permute-done((bf16[2048,256]{1,0:T(8,128)(2,1)}, bf16[2048,256]{1,0:T(8,128)(2,1)S(1)}, u32[]{:S(2)}, u32[]{:S(2)}) %collective-permute-start.5) | collective-permute-done | bytes 1048608 | tf_op jit(solution)/shard_map/ppermute | solution.py:48
  277.3 3.7 collective-permute-start.6
  281.5 1.7 convolution_multiply_fusion.3
  283.3 1.7 convolution_multiply_fusion.2
  285.5 13.3 %collective-permute-done.6 = bf16[2048,256]{1,0:T(8,128)(2,1)S(1)} collective-permute-done((bf16[2048,256]{1,0:T(8,128)(2,1)S(1)}, bf16[2048,256]{1,0:T(8,128)(2,1)S(1)}, u32[]{:S(2)}, u32[]{:S(2)}) %collective-permute-start.6) | collective-permute-done | bytes 1048608 | tf_op jit(solution)/shard_map/ppermute | solution.py:48
  298.8 2.8 fusion.30
  301.5 0.6 subtract_reduce_fusion
  302.6 44.5 %all-gather = f32[128,1,128]{2,1,0:T(1,128)S(1)} all-gather(f32[1,1,128]{2,1,0:T(1,128)S(1)} %bitcast.59), channel_id=1, replica_groups=mesh['blk_0'=4,'blk_1'=2,'grp_0'=2,'grp_1'=4,'grp_2'=2] {'blk_0','blk_1'..., dimensions={0}, use_global_device_ids=true | all-gather | bytes 66048 | tf_op jit(solution)/shard_map/all_gather | solution.py:111
  349.1 1.7 convolution_add_fusion.10
  350.8 1.7 convolution_add_fusion.9
  354.5 1.7 convolution_add_fusion.3
  356.2 1.7 convolution_add_fusion.2
  358.4 0.5 convolution_add_fusion
  358.9 0.6 multiply_reduce_fusion
  359.7 20.1 %all_to_all.17 = bf16[16,128,256]{2,1,0:T(8,128)(2,1)S(1)} all-to-all(bf16[16,128,256]{2,1,0:T(8,128)(2,1)S(1)} %broadcast_in_dim.42), channel_id=1, replica_groups=mesh['blk_0'=4,'blk_1'=2,'grp_0'=2,'grp_1'=4,'grp_2'=2] {'grp_0','grp_1'..., dimensions={0} | all-to-all | bytes 2097152 | tf_op jit(solution)/shard_map/all_to_all | solution.py:36
  379.8 1.5 fusion.174
  381.4 9.3 %fusion.41 = f32[2048,256]{1,0:T(8,128)} fusion(bf16[2048,2048]{1,0:T(8,128)(2,1)} %all-gather.3.cloned.1.call-done, f32[2048,256]{1,0:T(8,128)} %copy-done.8, bf16[2048,256]{1,0:T(8,128)(2,1)S(1)} %bitcast.57, bf16[256,256]{1,0:T(8,128)(2,1)S(1)} %copy-done.6), kind=kOutput, calls=%fused_computation.114 | convolution fusion | flops 2426404864 | bytes 13762560 | tf_op jit(solution)/shard_map/dot_general | solution.py:145
  390.7 8.9 %psum.49 = f32[]{:T(128)} all-reduce(f32[]{:T(128)} %get-tuple-element.35), channel_id=1, replica_groups=mesh['blk_0'=4,'blk_1'=2,'grp_0'=2,'grp_1'=4,'grp_2'=2] {'blk_0'}, use_global_device_ids=true, to_apply=%region_19.20 | all-reduce | flops 1 | bytes 8 | tf_op jit(solution)/shard_map/psum | solution.py:53
  399.6 7.3 %psum.50 = f32[]{:T(128)} all-reduce(f32[]{:T(128)} %psum.49), channel_id=1, replica_groups=mesh['blk_0'=4,'blk_1'=2,'grp_0'=2,'grp_1'=4,'grp_2'=2] {'blk_1'}, use_global_device_ids=true, to_apply=%region_20.21 | all-reduce | flops 1 | bytes 8 | tf_op jit(solution)/shard_map/psum | solution.py:53
  406.8 5.7 %psum.51 = f32[]{:T(128)} all-reduce(f32[]{:T(128)} %psum.50), channel_id=1, replica_groups=mesh['blk_0'=4,'blk_1'=2,'grp_0'=2,'grp_1'=4,'grp_2'=2] {'grp_0'}, use_global_device_ids=true, to_apply=%region_21.22 | all-reduce | flops 1 | bytes 8 | tf_op jit(solution)/shard_map/psum | solution.py:53
  412.6 10.6 %psum.52 = f32[]{:T(128)} all-reduce(f32[]{:T(128)} %psum.51), channel_id=1, replica_groups=mesh['blk_0'=4,'blk_1'=2,'grp_0'=2,'grp_1'=4,'grp_2'=2] {'grp_1'}, use_global_device_ids=true, to_apply=%region_22.23 | all-reduce | flops 1 | bytes 8 | tf_op jit(solution)/shard_map/psum | solution.py:53
  423.2 3.1 psum.53
  426.9 83.0 %all-reduce.3.cloned.1.call-done = (f32[2048,256]{1,0:T(8,128)}, f32[256,256]{1,0:T(8,128)}) async-done(((f32[2048,256]{1,0:T(8,128)}, f32[256,256]{1,0:T(8,128)}), (f32[2048,256]{1,0:T(8,128)}, f32[256,256]{1,0:T(8,128)})) %all-reduce.3.cloned.1.call-update) | async-done | bytes 2359312 | tf_op jit(solution)/shard_map/psum | solution.py:148
  509.9 3.1 copy.16
  513.0 0.7 copy.17
  (49 shorter events, 8.2 us)
Async XLA Ops:
  7.2 60.7 %copy-start = (bf16[2048,256]{1,0:T(8,128)(2,1)S(1)}, bf16[2048,256]{1,0:T(8,128)(2,1)}, u32[]{:S(2)}) copy-start(bf16[2048,256]{1,0:T(8,128)(2,1)} %param.8) | copy-start | bytes 3145732
  7.2 60.7 %all-gather.3.cloned.1.call-start = ((), (), s32[]{:S(2)}) async-start(), calls=%async_computation.3 | async-start | bytes 8912896 | tf_op jit(solution)/shard_map/all_gather | solution.py:72
  13.3 60.4 %copy-start.6 = (bf16[256,256]{1,0:T(8,128)(2,1)S(1)}, bf16[256,256]{1,0:T(8,128)(2,1)}, u32[]{:S(2)}) copy-start(bf16[256,256]{1,0:T(8,128)(2,1)} %param.9) | copy-start | bytes 393220
  13.3 496.6 %all-reduce.3.cloned.1.call-start = ((), (), s32[]{:S(2)}) async-start(), calls=%async_computation.4 | async-start | bytes 4718592 | tf_op jit(solution)/shard_map/psum | solution.py:148
  73.7 1.3 copy-start.8
  127.1 26.6 %collective-permute-start = (bf16[2048,256]{1,0:T(8,128)(2,1)S(1)}, bf16[2048,256]{1,0:T(8,128)(2,1)S(1)}, u32[]{:S(2)}, u32[]{:S(2)}) collective-permute-start(bf16[2048,256]{1,0:T(8,128)(2,1)S(1)} %bitcast.51), channel_id=1, source_target_pairs={{112,0},{0,16},{16,32},{32,48},{48,64},{64,80},{80,96},{96,112},{1... | collective-permute-start | bytes 3145736 | tf_op jit(solution)/shard_map/ppermute | solution.py:48
  153.7 25.7 %collective-permute-start.1 = (bf16[2048,256]{1,0:T(8,128)(2,1)S(1)}, bf16[2048,256]{1,0:T(8,128)(2,1)S(1)}, u32[]{:S(2)}, u32[]{:S(2)}) collective-permute-start(bf16[2048,256]{1,0:T(8,128)(2,1)S(1)} %collective-permute-done), channel_id=1, source_target_pairs={{112,0},{0,16},{16,32},{32,48},{48,64},{64,80},{80,96},{96,112},{1... | collective-permute-start | bytes 3145736 | tf_op jit(solution)/shard_map/ppermute | solution.py:48
  179.4 1.1 copy-start.1
  180.4 24.8 %collective-permute-start.2 = (bf16[2048,256]{1,0:T(8,128)(2,1)S(1)}, bf16[2048,256]{1,0:T(8,128)(2,1)S(1)}, u32[]{:S(2)}, u32[]{:S(2)}) collective-permute-start(bf16[2048,256]{1,0:T(8,128)(2,1)S(1)} %collective-permute-done.1), channel_id=1, source_target_pairs={{112,0},{0,16},{16,32},{32,48},{48,64},{64,80},{80,96},{96,112},{1... | collective-permute-start | bytes 3145736 | tf_op jit(solution)/shard_map/ppermute | solution.py:48
  205.3 1.0 copy-start.3
  206.2 24.1 %collective-permute-start.3 = (bf16[2048,256]{1,0:T(8,128)(2,1)S(1)}, bf16[2048,256]{1,0:T(8,128)(2,1)}, u32[]{:S(2)}, u32[]{:S(2)}) collective-permute-start(bf16[2048,256]{1,0:T(8,128)(2,1)S(1)} %collective-permute-done.2), channel_id=1, source_target_pairs={{112,0},{0,16},{16,32},{32,48},{48,64},{64,80},{80,96},{96,112},{1... | collective-permute-start | bytes 3145736 | tf_op jit(solution)/shard_map/ppermute | solution.py:48
  230.3 23.4 %collective-permute-start.4 = (bf16[2048,256]{1,0:T(8,128)(2,1)}, bf16[2048,256]{1,0:T(8,128)(2,1)}, u32[]{:S(2)}, u32[]{:S(2)}) collective-permute-start(bf16[2048,256]{1,0:T(8,128)(2,1)} %collective-permute-done.3), channel_id=1, source_target_pairs={{112,0},{0,16},{16,32},{32,48},{48,64},{64,80},{80,96},{96,112},{1... | collective-permute-start | bytes 3145736 | tf_op jit(solution)/shard_map/ppermute | solution.py:48
  253.8 23.5 %collective-permute-start.5 = (bf16[2048,256]{1,0:T(8,128)(2,1)}, bf16[2048,256]{1,0:T(8,128)(2,1)S(1)}, u32[]{:S(2)}, u32[]{:S(2)}) collective-permute-start(bf16[2048,256]{1,0:T(8,128)(2,1)} %collective-permute-done.4), channel_id=1, source_target_pairs={{112,0},{0,16},{16,32},{32,48},{48,64},{64,80},{80,96},{96,112},{1... | collective-permute-start | bytes 3145736 | tf_op jit(solution)/shard_map/ppermute | solution.py:48
  257.3 1.2 copy-start.2
  257.8 23.3 %copy-start.4 = (bf16[2048,256]{1,0:T(8,128)(2,1)S(1)}, bf16[2048,256]{1,0:T(8,128)(2,1)}, u32[]{:S(2)}) copy-start(bf16[2048,256]{1,0:T(8,128)(2,1)} %copy-done.3) | copy-start | bytes 3145732
  277.3 21.4 %collective-permute-start.6 = (bf16[2048,256]{1,0:T(8,128)(2,1)S(1)}, bf16[2048,256]{1,0:T(8,128)(2,1)S(1)}, u32[]{:S(2)}, u32[]{:S(2)}) collective-permute-start(bf16[2048,256]{1,0:T(8,128)(2,1)S(1)} %collective-permute-done.5), channel_id=1, source_target_pairs={{112,0},{0,16},{16,32},{32,48},{48,64},{64,80},{80,96},{96,112},{1... | collective-permute-start | bytes 3145736 | tf_op jit(solution)/shard_map/ppermute | solution.py:48
  283.3 15.5 %copy-start.7 = (s32[128]{0:T(128)S(1)}, s32[128]{0:T(128)}, u32[]{:S(2)}) copy-start(s32[128]{0:T(128)} %param.7) | copy-start | bytes 1540
  359.5 20.3 %copy-start.9 = (f32[2048,256]{1,0:T(8,128)S(1)}, f32[2048,256]{1,0:T(8,128)}, u32[]{:S(2)}) copy-start(f32[2048,256]{1,0:T(8,128)} %copy-done.8) | copy-start | bytes 6291460
  509.9 3.1 copy-start.5
Sparse Core Ops, SparseCore 0:
  13.4 54.3 all-gather.2
  390.8 119.0 all-reduce.2
where the time goes:
time: 522 us
  waiting for transfers between devices  285 us (55%)
  blocking collectives  152 us (29%)
  matrix products  42.2 us (8%)
  starting transfers between devices  16.4 us (3%)
  between operations  16.1 us (3%)
  local copies, waits for them, and re-layouts  6.82 us (1%)
    ppermute x7, waiting for transfers between devices, shifted(): return lax.ppermute(block, axis, route)  147 us
    psum x1, waiting for transfers between devices, shards(): first_grad, second_grad = lax.psum((first_grad, second_grad), BLK)  83 us
    all_gather x1, waiting for transfers between devices, shards(): pooled_all = lax.all_gather(pooled, GRP, axis=0, tiled=True)  54.5 us
    all_gather x1, blocking collectives, shards(): every_norm = lax.all_gather(log_norm, BLK_GRP, axis=0, tiled=True)  44.5 us
    all_to_all x2, blocking collectives, from_everyone(): lax.all_to_all(jnp.broadcast_to(array[None], (peers, *array.shape)), axis...  39.2 us
    psum x5, blocking collectives, by_axis(): array = lax.psum(array, axis)  35.6 us
    all_to_all x1, blocking collectives, sent_and_summed(): lax.all_to_all(in_blocks(array, dim, peers), axis, 0, 0, tiled=True)  32.5 us
    ppermute x7, starting transfers between devices, shifted(): return lax.ppermute(block, axis, route)  16.3 us
  transfers between devices with their start and end apart: 9, of which 9 were waited for; matrix products, arithmetic and copies ran while one was open for 1% of the time, Pallas kernels for 0%

commit v1 on v0

v1 whole, which is shorter than its diff:
```python
import math

import jax
import jax.numpy as jnp
from jax import lax
from jax.experimental import pallas as pl
from jax.experimental.pallas import tpu as pltpu
from jax.sharding import Mesh
from jax.sharding import PartitionSpec as P


BLK = ("x", "zh")
GRP = ("zl", "y", "c")
ALL = ("x", "zh", "zl", "y", "c")
YC = ("y", "c")
ZC = ("zh", "zl", "c")
XZ = ("x", "zh", "zl")


bf16 = jnp.bfloat16
f32 = jnp.float32
i32 = jnp.int32

sharpness = 0.05
score_top = 20.0
log2e = math.log2(math.e)

ROWS = 128
HALF = 64
C = 2048
U = 256
E = 256
SLOTS = 8
TOTAL = 16384


def sds(shape, dtype):
    return jax.ShapeDtypeStruct(shape, dtype)


def kernel(body, outs, *args, grid=None, in_specs=None, out_specs=None, scratch=(), mib=24, flops=0):
    extra = {}
    if in_specs is not None:
        extra = dict(in_specs=in_specs, out_specs=out_specs)
    if grid is not None:
        extra["grid"] = grid
    return pl.pallas_call(
        body,
        out_shape=outs,
        scratch_shapes=list(scratch),
        compiler_params=pltpu.CompilerParams(vmem_limit_bytes=mib * 1024 * 1024),
        cost_estimate=pl.CostEstimate(flops=flops, bytes_accessed=0, transcendentals=0),
        **extra,
    )(*args)


def along_y(block, distance):
    return lax.ppermute(block, "y", [(i, (i + distance) % 4) for i in range(4)])


def swap(block):
    return lax.ppermute(block, "c", [(0, 1), (1, 0)])


def along_z(block):
    pairs = []
    for zz in range(4):
        pairs.append((zz * 2, ((zz + 1) % 4) * 2))
        pairs.append((zz * 2 + 1, ((zz - 1) % 4) * 2 + 1))
    return lax.ppermute(block, ZC, pairs)


def exchange(array, axis):
    return lax.all_to_all(array, axis, 0, 0, tiled=True)


def dot(a, b):
    return jnp.dot(a, b, preferred_element_type=f32)


def dot_t(a, b):
    return lax.dot_general(a, b, (((1,), (1,)), ((), ())), preferred_element_type=f32)


def join_weights(w1, w2, after, out):
    out[:C, :] = w1[...]
    out[C:, :] = w2[...]


def as_column(row):
    return jnp.broadcast_to(row, (ROWS, 128)).T


def pool_body(frames, counts, out_a, out_b, column):
    step = pl.program_id(0)

    @pl.when(step == 0)
    def _():
        column[...] = as_column(counts[...].astype(f32))

    n = column[pl.ds(pl.multiple_of(step * 32, 32), 32), 0:1]
    slot = lax.broadcasted_iota(i32, (32, 256), 1)
    row = lax.broadcasted_iota(i32, (32, 256), 0)
    low = row * SLOTS
    mask = ((slot >= low) & (slot < low + n.astype(i32))).astype(f32).astype(bf16)
    mean = (dot(mask, frames[...]) / n).astype(bf16)

    @pl.when(step < 2)
    def _():
        out_a[...] = mean

    @pl.when(step >= 2)
    def _():
        out_b[...] = mean


def gelu(v):
    k = math.sqrt(2.0 / math.pi)
    return v * (0.5 * (1.0 + jnp.tanh(k * (v + 0.044715 * (v * v * v)))))


def forward_sum(block, weights):
    total = None
    for w in weights:
        hidden = gelu(dot(block, w[:C, :])).astype(bf16)
        part = dot(hidden, w[C:, :])
        total = part if total is None else total + part
    return total


def near_body(a0, a1, a3, b0, b1, b3, own, far, mate, mate_far, near, p0, p1, p3):
    for i, piece in enumerate((a0, a1, a3, b0, b1, b3)):
        near[i * HALF : (i + 1) * HALF, :] = piece[...]
    part = forward_sum(near[...], (own, far, mate, mate_far))
    for i, out in enumerate((p0, p1, p3)):
        out[:HALF, :] = part[i * HALF : (i + 1) * HALF]
        out[HALF:, :] = part[(3 + i) * HALF : (4 + i) * HALF]


def far_body(a2, b2, own, far, mate, mate_far, block, p2):
    block[:HALF, :] = a2[...]
    block[HALF:, :] = b2[...]
    p2[...] = forward_sum(block[...], (own, far, mate, mate_far))


def keys_body(p0, p1, p2, p3, partner, raw, pay, spread):
    total = p0[...] + p1[...] + p2[...] + p3[...]
    raw[...] = total
    length = jnp.sqrt(jnp.sum(total * total, axis=1, keepdims=True) + 1e-06)
    half = (total / length).astype(bf16)
    row = partner[...]
    high = (row // 128).astype(f32)
    low = (row % 128).astype(f32)
    lane = lax.broadcasted_iota(i32, (ROWS, 128), 1)
    code = jnp.where(lane == 0, as_column(high), jnp.where(lane == 1, as_column(low), 0.0))
    code = code.astype(bf16)
    for i in range(16):
        spread[i] = half
    pay[:, :E] = half
    pay[:, E:] = code


def pair_body(own, mate, out):
    out[:ROWS, :] = own[...]
    out[ROWS:, :] = mate[...]


def pair_sum_body(own, mate, out):
    for d in range(4):
        for m in range(2):
            r = 2 * d + m
            other = 2 * d + 1 - m
            out[r : r + 1, :] = own[r : r + 1, :] + mate[other : other + 1, :]


def column_ids(base, j):
    lane = lax.broadcasted_iota(i32, (1, 256), 1)
    block = 2 * j + lane // 128
    return base + block * 1024 + lane % 128


def exp_block(scaled, exps, where, j):
    exps[...] = jnp.exp2(scaled * (log2e / sharpness) - score_top * log2e)

    @pl.when(where[2] == j)
    def _():
        row = where[0] + lax.broadcasted_iota(i32, (ROWS, 1), 0)
        same = column_ids(where[1], j) == row
        exps[:ROWS, :] = jnp.where(same, 0.0, exps[:ROWS, :])


def place_body(given, out):
    for i in range(5):
        out[i] = given[i]


def score_body(where, pay0, pay1, pay2, pay3, cols, row_out, col_out, tile, who, exps, acc):
    for d, pay in enumerate((pay0, pay1, pay2, pay3)):
        tile[d * 256 : (d + 1) * 256, :] = pay[:, :E]
        code = pay[:, E:].astype(f32)
        who[d * 256 : (d + 1) * 256, :] = code[:, 0:1] * 128.0 + code[:, 1:2]
    mates = who[...]
    found = jnp.zeros((1, 256), f32)
    for j in range(8):
        block = cols[2 * j : 2 * j + 2].reshape(256, E)
        scaled = dot_t(tile[...], block)
        ids = column_ids(where[1], j)
        exp_block(scaled, exps, where, j)
        hit = mates == ids.astype(f32)
        found = found + jnp.sum(jnp.where(hit, scaled, 0.0), axis=0, keepdims=True)
        here = exps[...]
        two = here[:, :128] + here[:, 128:]
        if j == 0:
            acc[...] = two
        else:
            acc[...] += two
        sums = jnp.sum(here, axis=0, keepdims=True)
        for i in range(16):
            col_out[i, :, j * 256 : (j + 1) * 256] = sums
    positive = jnp.sum(found) / sharpness
    for i in range(16):
        col_out[i, :, 2048:] = jnp.full((1, 128), positive, f32)
    for r in range(8):
        total = jnp.sum(acc[r * ROWS : (r + 1) * ROWS, :].T, axis=0, keepdims=True)
        row_out[r : r + 1, :] = total


def weight_body(
    where, tile, who, cols, sum0, sum1, sum2, sum3, col_sums, out, loss, scale, exps, acc
):
    sums = (sum0, sum1, sum2, sum3)
    for r in range(8):
        d, m = divmod(r, 2)
        total = None
        for s in range(4):
            at = (d - s) % 4 * 2 + m
            part = sums[s][at : at + 1, :]
            total = part if total is None else total + part
        scale[r * ROWS : (r + 1) * ROWS, :] = as_column(1.0 / total)
    mates = who[...]
    by_row = scale[:, 0:1]
    columns = col_sums[0]
    for i in range(1, 16):
        columns = columns + col_sums[i]
    logs = jnp.log(columns[:, :2048]) + score_top
    loss[...] = jnp.full((1, 128), jnp.sum(logs) - jnp.sum(columns[:, 2048:2049]), f32)
    for j in range(8):
        block = cols[2 * j : 2 * j + 2].reshape(256, E)
        scaled = dot_t(tile[...], block)
        ids = column_ids(where[1], j)
        exp_block(scaled, exps, where, j)
        here = exps[...]
        hit = (mates == ids.astype(f32)).astype(f32)
        by_col = 1.0 / columns[:, j * 256 : (j + 1) * 256]
        weights = (here * by_row - hit).astype(bf16)
        mirror = (here * by_col - hit).astype(bf16)
        part = dot(weights, block) + dot(mirror, block)
        if j == 0:
            acc[...] = part
        elif j < 7:
            acc[...] += part
        else:
            part = acc[...] + part
            for r in range(8):
                d, m = divmod(r, 2)
                at = (where[3] + d) % 4 * 2 + (where[4] + m) % 2
                out[pl.ds(at, 1)] = part[r * ROWS : (r + 1) * ROWS].reshape(1, ROWS, E)


def raw_grad_body(raw, got, out):
    total = raw[...]
    length = jnp.sqrt(jnp.sum(total * total, axis=1, keepdims=True) + 1e-06)
    unit = total / length
    grad = got[0]
    for i in range(1, 8):
        grad = grad + got[i]
    grad = grad / (TOTAL * sharpness)
    along = jnp.sum(unit * grad, axis=1, keepdims=True)
    out[...] = ((grad - unit * along) / length).astype(bf16)


def bundle_body(own, other, loss, out):
    out[:ROWS, :] = own[...]
    out[ROWS : 2 * ROWS, :] = other[...]
    value = loss[:, 0:1]
    high = value.astype(bf16).astype(f32)
    mid = (value - high).astype(bf16).astype(f32)
    low = value - high - mid
    lane = lax.broadcasted_iota(i32, (16, E), 1)
    rows = jnp.where(lane == 0, high, jnp.where(lane == 1, mid, jnp.where(lane == 2, low, 0.0)))
    out[2 * ROWS :, :] = rows.astype(bf16)


def slope_body(*refs):
    pools, w1 = refs[:8], refs[8]
    hidden, slope, joined = refs[9:]
    k = math.sqrt(2.0 / math.pi)
    low = 0
    for pool in pools:
        n = pool.shape[0]
        v = dot(pool[...], w1[...])
        t = jnp.tanh(k * (v + 0.044715 * (v * v * v)))
        hidden[:, low : low + n] = (v * (0.5 * (1.0 + t))).astype(bf16).T
        joined[low : low + n, :] = pool[...]
        slope[low : low + n, :] = 0.5 * (1.0 + t) + (0.5 * v) * (1.0 - t * t) * (
            k * (1.0 + 3 * 0.044715 * (v * v))
        )
        low += n


def head_body(*refs):
    pool, hidden, slope, w2, rings = refs[0], refs[1], refs[2], refs[3], refs[4:12]
    out, loss, grads, turned, second = refs[12:]
    step = pl.program_id(0)

    @pl.when(step == 0)
    def _():
        low = 0
        for core in range(2):
            ring = rings[core * 4 : core * 4 + 4]
            for z in range(2):
                near = [(d, h) for h in range(2) for d in (0, 1, 3)]
                for d, h in near + [(2, 0), (2, 1)]:
                    at = z * ROWS + h * HALF
                    grads[low : low + HALF, :] = ring[d][at : at + HALF, :]
                    low += HALF
        pre = (dot_t(grads[...], w2[...]) * slope[...]).astype(bf16)
        turned[...] = pre.T
        second[...] = dot(hidden[...], grads[...]).astype(bf16)
        total = jnp.zeros((1, E), f32)
        for ring in rings:
            total = total + ring[2 * ROWS : 2 * ROWS + 16, :].astype(f32)[0:1]
        loss[...] = jnp.full((1, 128), jnp.sum(total) / TOTAL, f32)

    out[0, :U, :] = dot(turned[...], pool[...]).astype(bf16)
    out[0, U:, :] = second[pl.ds(pl.multiple_of(step * 32, 32), 32), :]


def piece_body(got, out):
    total = got[0].astype(f32)
    for i in range(1, 8):
        total = total + got[i].astype(f32)
    first = total[:U, :].T.astype(bf16)
    second = total[U:, :].astype(bf16)
    for i in range(8):
        out[i, :U, :] = first
        out[i, U:, :] = second


def final_body(got, first, second):
    for i in range(2):
        first[i * 256 : (i + 1) * 256, :] = got[i, :U, :].astype(f32)
        second[i * 32 : (i + 1) * 32, :] = got[i, U:, :].astype(f32)


def step(frames, counts, positives, w_first, w_second):
    x, zh, zl = lax.axis_index("x"), lax.axis_index("zh"), lax.axis_index("zl")
    y, c = lax.axis_index("y"), lax.axis_index("c")
    base = (y * 2 + c) * ROWS
    cell = x * 4 + zh * 2 + zl
    where = jnp.stack([cell * 1024 + base, base, cell // 2, y, c]).astype(i32)
    vm = pl.BlockSpec()
    smem = pl.BlockSpec(memory_space=pltpu.SMEM)
    hbm = pl.BlockSpec(memory_space=pl.ANY)

    a0, b0 = kernel(
        pool_body,
        (sds((HALF, C), bf16), sds((HALF, C), bf16)),
        frames.reshape(ROWS * SLOTS, C),
        counts.reshape(1, ROWS),
        grid=(4,),
        in_specs=[
            pl.BlockSpec((256, C), lambda i: (i, 0)),
            pl.BlockSpec((1, ROWS), lambda i: (0, 0)),
        ],
        out_specs=[
            pl.BlockSpec((32, C), lambda i: (jnp.minimum(i, 1), 0)),
            pl.BlockSpec((32, C), lambda i: (jnp.maximum(i - 2, 0), 0)),
        ],
        scratch=[pltpu.VMEM((ROWS, 128), f32)],
        flops=10**8,
    )
    a3, b1 = along_y(a0, 1), along_y(b0, -1)
    b3, a1 = along_y(b0, 1), along_y(a0, -1)
    a2, b2 = along_y(a3, 1), along_y(b1, -1)

    w_own = kernel(
        join_weights, sds((C + U, E), bf16), w_first, w_second, a0,
        in_specs=[vm, vm, hbm], out_specs=vm,
    )
    w_far = along_z(w_own)
    w_mate = swap(w_own)
    w_mate_far = swap(w_far)
    weights = (w_own, w_far, w_mate, w_mate_far)

    key_part = sds((ROWS, E), f32)
    near, p0, p1, p3 = kernel(
        near_body,
        (sds((6 * HALF, C), bf16), key_part, key_part, key_part),
        a0, a1, a3, b0, b1, b3, *weights,
        flops=2 * 10**9,
    )
    q1, q3 = along_y(p1, 1), along_y(p3, -1)
    far, p2 = kernel(
        far_body, (sds((ROWS, C), bf16), key_part), a2, b2, *weights, flops=5 * 10**8
    )
    q2 = along_y(p2, 2)
    raw, pay, spread = kernel(
        keys_body,
        (key_part, sds((ROWS, E + 128), bf16), sds((16, ROWS, E), bf16)),
        p0, q1, q2, q3, positives.reshape(1, ROWS),
    )
    cols = exchange(spread, XZ)
    pair = kernel(pair_body, sds((2 * ROWS, E + 128), bf16), pay, swap(pay))
    pairs = [pair] + [along_y(pair, -d) for d in (1, 2, 3)]

    z_near, z_far = along_z(near), along_z(far)
    core = (near, far, z_near, z_far)
    pools = core + tuple(swap(p) for p in core)
    hidden, slope, joined = kernel(
        slope_body,
        (sds((U, 16 * ROWS), bf16), sds((16 * ROWS, U), f32), sds((16 * ROWS, C), bf16)),
        *pools, w_first,
        mib=36,
        flops=2 * 10**9,
    )

    where = kernel(place_body, sds((5,), i32), where, in_specs=[smem], out_specs=smem)
    row_sums, col_sums, tile, who = kernel(
        score_body,
        (
            sds((8, ROWS), f32),
            sds((16, 1, 2176), f32),
            sds((1024, E), bf16),
            sds((1024, 1), f32),
        ),
        where, *pairs, cols,
        in_specs=[smem] + [vm] * 5,
        out_specs=[vm, vm, vm, vm],
        scratch=[pltpu.VMEM((1024, 256), f32), pltpu.VMEM((1024, 128), f32)],
        flops=10**9,
    )
    col_sums = exchange(col_sums, XZ)
    row_sums = kernel(pair_sum_body, sds((8, ROWS), f32), row_sums, swap(row_sums))
    row_sums = [row_sums] + [along_y(row_sums, -d) for d in (1, 2, 3)]
    where = kernel(place_body, sds((5,), i32), where, in_specs=[smem], out_specs=smem)
    grads, loss = kernel(
        weight_body,
        (sds((8, ROWS, E), f32), sds((1, 128), f32)),
        where, tile, who, cols, *row_sums, col_sums,
        in_specs=[smem] + [vm] * 8,
        out_specs=[vm, vm],
        scratch=[
            pltpu.VMEM((1024, 128), f32),
            pltpu.VMEM((1024, 256), f32),
            pltpu.VMEM((1024, E), f32),
        ],
        flops=3 * 10**9,
    )
    mine = exchange(grads, YC)
    raw_grad = kernel(raw_grad_body, sds((ROWS, E), bf16), raw, mine)
    z_grad = along_z(raw_grad)
    ring0 = kernel(bundle_body, sds((2 * ROWS + 16, E), bf16), raw_grad, z_grad, loss)
    ring = [ring0] + [along_y(ring0, -d) for d in (1, 2, 3)]
    ring = ring + [swap(r) for r in ring]
    ring_spec = pl.BlockSpec((2 * ROWS + 16, E), lambda j: (0, 0))
    send, loss_all = kernel(
        head_body,
        (sds((8, U + 32, E), bf16), sds((1, 128), f32)),
        joined, hidden, slope, w_second, *ring,
        grid=(8,),
        in_specs=[
            pl.BlockSpec((16 * ROWS, 256), lambda j: (0, j)),
            pl.BlockSpec((U, 16 * ROWS), lambda j: (0, 0)),
            pl.BlockSpec((16 * ROWS, U), lambda j: (0, 0)),
            pl.BlockSpec((U, E), lambda j: (0, 0)),
        ]
        + [ring_spec] * 8,
        out_specs=[
            pl.BlockSpec((1, U + 32, E), lambda j: (j, 0, 0)),
            pl.BlockSpec((1, 128), lambda j: (0, 0)),
        ],
        scratch=[
            pltpu.VMEM((16 * ROWS, E), bf16),
            pltpu.VMEM((U, 16 * ROWS), bf16),
            pltpu.VMEM((U, E), bf16),
        ],
        flops=2 * 10**9,
    )
    got = exchange(send, BLK)
    piece = kernel(piece_body, sds((8, U + 32, E), bf16), got)
    whole = exchange(piece, BLK)
    first, second = kernel(
        final_body,
        (sds((C, U), f32), sds((U, E), f32)),
        whole,
        grid=(4,),
        in_specs=[pl.BlockSpec((2, U + 32, E), lambda j: (j, 0, 0))],
        out_specs=[
            pl.BlockSpec((512, U), lambda j: (j, 0)),
            pl.BlockSpec((64, E), lambda j: (j, 0)),
        ],
    )
    return (loss_all[0, 0], first, second)


def solution(mesh):
    finer = Mesh(mesh.devices.reshape(4, 2, 2, 4, 2), ALL)
    placed = (P(ALL, None, None), P(ALL), P(ALL), P(None, GRP), P(GRP, None))
    return jax.shard_map(
        step,
        mesh=finer,
        in_specs=placed,
        out_specs=(P(), P(None, GRP), P(GRP, None)),
        check_vma=False,
    )
```

time: 522 us -> 227 us (0.43)
  waiting for transfers between devices: 285 us -> 77.6 us
  blocking collectives: 152 us -> 43.3 us
  matrix products: 42.2 us -> 0 us
  Pallas kernels: 0 us -> 41 us
  starting transfers between devices: 16.4 us -> 46.5 us
  between operations: 16.1 us -> 0.86 us
  local copies, waits for them, and re-layouts: 6.82 us -> 14.9 us
    ppermute x7 -> x34, waiting for transfers between devices: 147 us -> 62.2 us  [the longest x18 41.1 us: along_y(): return lax.ppermute(block, 'y', [(i, (i + distance) % 4) for i in range(4)])]
    psum x1 -> x0, waiting for transfers between devices: 83 us -> none  [shards(): first_grad, second_grad = lax.psum((first_grad, second_grad), BLK)]
    all_gather x1 -> x0, waiting for transfers between devices: 54.5 us -> none  [shards(): pooled_all = lax.all_gather(pooled, GRP, axis=0, tiled=True)]
    all_gather x1 -> x0, blocking collectives: 44.5 us -> none  [shards(): every_norm = lax.all_gather(log_norm, BLK_GRP, axis=0, tiled=True)]
    dot_general x29 -> x0, matrix products: 42.2 us -> none  [the longest x1 9.26 us: shards(): lax.dot_general(pooled_all, preact_grad, (((0,), (0,)), ((), ())), prefer...]
    pallas_call x0 -> x17, Pallas kernels: none -> 41 us  [kernel(): pl.pallas_call(body, out_shape=outs, scratch_shapes=list(scratch), compil...]
    psum x5 -> x0, blocking collectives: 35.6 us -> none  [by_axis(): array = lax.psum(array, axis)]
    all_to_all x3 -> x2, blocking collectives: 71.7 us -> 43.3 us  [exchange(): return lax.all_to_all(array, axis, 0, 0, tiled=True)]
  transfers between devices with their start and end apart: 9 -> 37, of which waited for: 9 -> 19; matrix products, arithmetic and copies ran while one was open for 1% -> 0% of each run, Pallas kernels for 0% -> 13%
where the time goes in v1:
time: 227 us; the launch traced here: 224 us
  waiting for transfers between devices  77.6 us (34%)
  starting transfers between devices  46.5 us (20%)
  blocking collectives  43.3 us (19%)
  Pallas kernels  41 us (18%)
  local copies, waits for them, and re-layouts  14.9 us (7%)
    all_to_all x2, blocking collectives, exchange(): return lax.all_to_all(array, axis, 0, 0, tiled=True)  43.3 us
    ppermute x18, waiting for transfers between devices, along_y(): return lax.ppermute(block, 'y', [(i, (i + distance) % 4) for i in range(4)])  41.1 us
    pallas_call x17, Pallas kernels, kernel(): pl.pallas_call(body, out_shape=outs, scratch_shapes=list(scratch), compil...  41 us
    ppermute x18, starting transfers between devices, along_y(): return lax.ppermute(block, 'y', [(i, (i + distance) % 4) for i in range(4)])  21.2 us
    ppermute x4, waiting for transfers between devices, along_z(): return lax.ppermute(block, ZC, pairs)  18.6 us
    all_to_all x3, starting transfers between devices, exchange(): return lax.all_to_all(array, axis, 0, 0, tiled=True)  17.2 us
    all_to_all x3, waiting for transfers between devices, exchange(): return lax.all_to_all(array, axis, 0, 0, tiled=True)  15.3 us
    unnamed x36, local copies, waits for them, and re-layouts  14.9 us
  transfers between devices with their start and end apart: 37, of which 19 were waited for; matrix products, arithmetic and copies ran while one was open for 0% of the time, Pallas kernels for 13%

profile of v1, /device:TPU:6, one launch (start us, length us, event | category | flops | bytes accessed | tf_op | source)
XLA Modules:
  0.0 224.2 jit_solution(5646004571574085616)
XLA Ops:
  0.6 2.2 copy-done.2
  3.5 1.5 shard_map.76
  5.1 2.0 collective-permute-start.4
  7.1 1.7 collective-permute-start.5
  8.8 14.6 %collective-permute-done.4.far = bf16[2304,256]{1,0:T(8,128)(2,1)S(1)} collective-permute-done((bf16[2304,256]{1,0:T(8,128)(2,1)S(1)}, bf16[2304,256]{1,0:T(8,128)(2,1)S(1)}, u32[]{:S(2)}, u32[]{:S(2)}) %collective-permute-start.4) | collective-permute-done | bytes 1179680 | tf_op jit(solution)/shard_map/ppermute | solution.py:70
  23.4 3.0 %collective-permute-start = (bf16[64,2048]{1,0:T(8,128)(2,1)S(1)}, bf16[64,2048]{1,0:T(8,128)(2,1)S(1)}, u32[]{:S(2)}, u32[]{:S(2)}) collective-permute-start(bf16[64,2048]{1,0:T(8,128)(2,1)S(1)} %get-tuple-element.27.after.a0), channel_id=1, source_target_pairs={{0,6},{2,0},{4,2},{6,4},{1,7},{3,1},{5,3},{7,5},{8,14},{10,8},{12,... | collective-permute-start | bytes 786440 | tf_op jit(solution)/shard_map/ppermute | solution.py:58
  26.4 3.2 %collective-permute-start.2 = (bf16[64,2048]{1,0:T(8,128)(2,1)S(1)}, bf16[64,2048]{1,0:T(8,128)(2,1)S(1)}, u32[]{:S(2)}, u32[]{:S(2)}) collective-permute-start(bf16[64,2048]{1,0:T(8,128)(2,1)S(1)} %get-tuple-element.28.b0), channel_id=1, source_target_pairs={{0,6},{2,0},{4,2},{6,4},{1,7},{3,1},{5,3},{7,5},{8,14},{10,8},{12,... | collective-permute-start | bytes 786440 | tf_op jit(solution)/shard_map/ppermute | solution.py:58
  29.7 3.5 %collective-permute-done.a1 = bf16[64,2048]{1,0:T(8,128)(2,1)S(1)} collective-permute-done((bf16[64,2048]{1,0:T(8,128)(2,1)S(1)}, bf16[64,2048]{1,0:T(8,128)(2,1)S(1)}, u32[]{:S(2)}, u32[]{:S(2)}) %collective-permute-start) | collective-permute-done | bytes 262176 | tf_op jit(solution)/shard_map/ppermute | solution.py:58
  33.1 1.0 collective-permute-start.3
  34.2 1.9 collective-permute-done.1.a3
  36.1 2.2 collective-permute-done.2.b1
  38.3 4.2 %collective-permute-done.3.b3 = bf16[64,2048]{1,0:T(8,128)(2,1)S(1)} collective-permute-done((bf16[64,2048]{1,0:T(8,128)(2,1)S(1)}, bf16[64,2048]{1,0:T(8,128)(2,1)S(1)}, u32[]{:S(2)}, u32[]{:S(2)}) %collective-permute-start.3) | collective-permute-done | bytes 262176 | tf_op jit(solution)/shard_map/ppermute | solution.py:58
  42.5 3.1 %shard_map.78 = (bf16[384,2048]{1,0:T(8,128)(2,1)}, f32[128,256]{1,0:T(8,128)S(1)}, f32[128,256]{1,0:T(8,128)S(1)}, f32[128,256]{1,0:T(8,128)S(1)}) custom-call(bf16[64,2048]{1,0:T(8,128)(2,1)S(1)} %get-tuple-element.27.after.a0, bf16[64,2048]{1,0:T(8,128)(2,1)S(1)} %collective-permute-done.a1, bf16[64,2048]{1,0:T(8,128)(2,1)S(1)} %collective-permute-done.1.a3, ...), custom_call_target="tpu_custom_call" | custom-call | flops 2000000000 | tf_op jit(solution)/shard_map/pallas_call | solution.py:47
  45.8 3.2 %collective-permute-start.8 = (bf16[64,2048]{1,0:T(8,128)(2,1)S(1)}, bf16[64,2048]{1,0:T(8,128)(2,1)S(1)}, u32[]{:S(2)}, u32[]{:S(2)}) collective-permute-start(bf16[64,2048]{1,0:T(8,128)(2,1)S(1)} %collective-permute-done.2.b1), channel_id=1, source_target_pairs={{0,6},{2,0},{4,2},{6,4},{1,7},{3,1},{5,3},{7,5},{8,14},{10,8},{12,... | collective-permute-start | bytes 786440 | tf_op jit(solution)/shard_map/ppermute | solution.py:58
  49.0 7.1 %collective-permute-done.7.a2 = bf16[64,2048]{1,0:T(8,128)(2,1)S(1)} collective-permute-done((bf16[64,2048]{1,0:T(8,128)(2,1)S(1)}, bf16[64,2048]{1,0:T(8,128)(2,1)S(1)}, u32[]{:S(2)}, u32[]{:S(2)}) %collective-permute-start.7) | collective-permute-done | bytes 262176 | tf_op jit(solution)/shard_map/ppermute | solution.py:58
  56.2 1.3 shard_map.79
  58.3 1.6 collective-permute-start.17
  59.9 4.1 %collective-permute-done.16.p2 = f32[128,256]{1,0:T(8,128)S(1)} collective-permute-done((f32[128,256]{1,0:T(8,128)S(1)}, f32[128,256]{1,0:T(8,128)S(1)}, u32[]{:S(2)}, u32[]{:S(2)}) %collective-permute-start.16) | collective-permute-done | bytes 131104 | tf_op jit(solution)/shard_map/ppermute | solution.py:58
  64.0 2.1 collective-permute-done.17.p3
  66.2 1.2 shard_map.81
  67.4 4.8 %all-to-all-start = ((bf16[16,128,256]{2,1,0:T(8,128)(2,1)}), bf16[16,128,256]{2,1,0:T(8,128)(2,1)S(1)}, u32[]{:S(2)}, u32[]{:S(2)}) async-start(bf16[16,128,256]{2,1,0:T(8,128)(2,1)} %get-tuple-element.40), calls=%async_computation | async-start | bytes 2097152 | tf_op jit(solution)/shard_map/all_to_all | solution.py:74
  72.2 1.3 collective-permute-done.18.mate
  73.5 2.5 %collective-permute-start.19 = (bf16[256,384]{1,0:T(8,128)(2,1)S(1)}, bf16[256,384]{1,0:T(8,128)(2,1)S(1)}, u32[]{:S(2)}, u32[]{:S(2)}) collective-permute-start(bf16[256,384]{1,0:T(8,128)(2,1)S(1)} %shard_map.84.pay0), channel_id=1, source_target_pairs={{0,6},{2,0},{4,2},{6,4},{1,7},{3,1},{5,3},{7,5},{8,14},{10,8},{12,... | collective-permute-start | bytes 589832 | tf_op jit(solution)/shard_map/ppermute | solution.py:58
  77.0 1.1 shard_map.82.given.where
  78.8 5.9 %collective-permute-done.19.pay1 = bf16[256,384]{1,0:T(8,128)(2,1)S(1)} collective-permute-done((bf16[256,384]{1,0:T(8,128)(2,1)S(1)}, bf16[256,384]{1,0:T(8,128)(2,1)S(1)}, u32[]{:S(2)}, u32[]{:S(2)}) %collective-permute-start.19) | collective-permute-done | bytes 196640 | tf_op jit(solution)/shard_map/ppermute | solution.py:58
  85.3 2.9 %collective-permute-done.21.pay3 = bf16[256,384]{1,0:T(8,128)(2,1)} collective-permute-done((bf16[256,384]{1,0:T(8,128)(2,1)S(1)}, bf16[256,384]{1,0:T(8,128)(2,1)}, u32[]{:S(2)}, u32[]{:S(2)}) %collective-permute-start.21) | collective-permute-done | bytes 196640 | tf_op jit(solution)/shard_map/ppermute | solution.py:58
  88.2 5.9 %shard_map.85 = (f32[8,128]{1,0:T(8,128)S(1)}, f32[16,1,2176]{2,1,0:T(1,128)}, bf16[1024,256]{1,0:T(8,128)(2,1)S(1)}, f32[1024,1]{1,0:T(8,128)S(1)}) custom-call(s32[5]{0:T(128)S(1)} %shard_map.82.given.where, bf16[256,384]{1,0:T(8,128)(2,1)S(1)} %shard_map.84.pay0, bf16[256,384]{1,0:T(8,128)(2,1)S(1)} %collective-permute-done.19.pay1, ...), custom_call_target="tpu_custom_call" | custom-call | flops 1000000000 | tf_op jit(solution)/shard_map/pallas_call | solution.py:47
  95.7 7.2 %all-to-all-start.1 = ((f32[16,1,2176]{2,1,0:T(1,128)}), f32[16,1,2176]{2,1,0:T(1,128)S(1)}, u32[]{:S(2)}, u32[]{:S(2)}) async-start(f32[16,1,2176]{2,1,0:T(1,128)} %get-tuple-element.44), calls=%async_computation.1 | async-start | bytes 278528 | tf_op jit(solution)/shard_map/all_to_all | solution.py:74
  103.0 1.2 collective-permute-done.22.mate
  106.2 1.1 shard_map.83.where
  108.4 1.5 collective-permute-start.10
  114.0 1.0 copy-done.15
  116.1 7.1 %shard_map.87 = (f32[8,128,256]{2,1,0:T(8,128)}, f32[1,128]{1,0:T(1,128)S(1)}) custom-call(s32[5]{0:T(128)S(1)} %copy-done.13, bf16[1024,256]{1,0:T(8,128)(2,1)S(1)} %copy-done.15, f32[1024,1]{1,0:T(8,128)S(1)} %copy-done.17, bf16[16,128,256]{2,1,0:T(8,128)(2,1)S(1)} %all-to-all-done.cols, f32[8,128]{1,0:T(8,128)S(1)} %shard_map.86.sum0, ...), custom_call_target="tpu_custom_call" | custom-call | flops 3000000000 | tf_op jit(solution)/shard_map/pallas_call | solution.py:47
  123.2 5.2 %all-to-all-start.2 = ((f32[8,128,256]{2,1,0:T(8,128)}), f32[8,128,256]{2,1,0:T(8,128)S(1)}, u32[]{:S(2)}, u32[]{:S(2)}) async-start(f32[8,128,256]{2,1,0:T(8,128)} %get-tuple-element.45), calls=%async_computation.2 | async-start | bytes 2097152 | tf_op jit(solution)/shard_map/all_to_all | solution.py:74
  129.0 15.3 %all-to-all-done.2.got = f32[8,128,256]{2,1,0:T(8,128)S(1)} async-done(((f32[8,128,256]{2,1,0:T(8,128)}), f32[8,128,256]{2,1,0:T(8,128)S(1)}, u32[]{:S(2)}, u32[]{:S(2)}) %all-to-all-start.2) | async-done | bytes 1048608 | tf_op jit(solution)/shard_map/all_to_all | solution.py:74
  144.5 1.5 collective-permute-start.26
  146.1 4.0 %collective-permute-done.26.other = bf16[128,256]{1,0:T(8,128)(2,1)S(1)} collective-permute-done((bf16[128,256]{1,0:T(8,128)(2,1)S(1)}, bf16[128,256]{1,0:T(8,128)(2,1)S(1)}, u32[]{:S(2)}, u32[]{:S(2)}) %collective-permute-start.26) | collective-permute-done | bytes 65568 | tf_op jit(solution)/shard_map/ppermute | solution.py:70
  150.2 1.2 collective-permute-start.27
  151.4 1.5 collective-permute-start.28
  153.2 2.1 collective-permute-done.27.refs_5_
  155.3 2.7 %collective-permute-done.28.refs_6_ = bf16[272,256]{1,0:T(8,128)(2,1)S(1)} collective-permute-done((bf16[272,256]{1,0:T(8,128)(2,1)S(1)}, bf16[272,256]{1,0:T(8,128)(2,1)S(1)}, u32[]{:S(2)}, u32[]{:S(2)}) %collective-permute-start.28) | collective-permute-done | bytes 139296 | tf_op jit(solution)/shard_map/ppermute | solution.py:58
  158.0 1.5 collective-permute-done.29.refs_7_
  159.4 10.2 %shard_map.80 = (bf16[256,2048]{1,0:T(8,128)(2,1)S(1)}, f32[2048,256]{1,0:T(8,128)S(1)}, bf16[2048,2048]{1,0:T(8,128)(2,1)}) custom-call(bf16[384,2048]{1,0:T(8,128)(2,1)} %get-tuple-element.29.refs_0_, bf16[128,2048]{1,0:T(8,128)(2,1)S(1)} %get-tuple-element.30.refs_1_, bf16[384,2048]{1,0:T(8,128)(2,1)} %collective-permute-done.9.refs_2_, ...), custom_call_target="tpu_custom_call" | custom-call | flops 2000000000 | tf_op jit(solution)/shard_map/pallas_call | solution.py:47
  169.7 3.4 %copy-done = bf16[2048,2048]{1,0:T(8,128)(2,1)S(1)} copy-done((bf16[2048,2048]{1,0:T(8,128)(2,1)S(1)}, bf16[2048,2048]{1,0:T(8,128)(2,1)}, u32[]{:S(2)}) %copy-start) | copy-done | bytes 8388632
  173.1 5.7 %shard_map.90 = (bf16[8,288,256]{2,1,0:T(8,128)(2,1)S(1)}, f32[1,128]{1,0:T(1,128)}) custom-call(bf16[2048,2048]{1,0:T(8,128)(2,1)S(1)} %copy-done, bf16[256,2048]{1,0:T(8,128)(2,1)S(1)} %get-tuple-element.32.refs_1_, f32[2048,256]{1,0:T(8,128)S(1)} %get-tuple-element.33.refs_2_, bf16[256,256]{1,0:T(8,128)(2,1)S(1)} %copy-done.3, ...), custom_call_target="tpu_custom_call" | custom-call | flops 2000000000 | tf_op jit(solution)/shard_map/pallas_call | solution.py:47
  178.8 22.6 %all_to_all.25.got = bf16[8,288,256]{2,1,0:T(8,128)(2,1)S(1)} all-to-all(bf16[8,288,256]{2,1,0:T(8,128)(2,1)S(1)} %get-tuple-element.48), channel_id=1, replica_groups=mesh['x'=4,'zh'=2,'zl'=2,'y'=4,'c'=2] {'x','zh'}, dimensions={0} | all-to-all | bytes 2359296 | tf_op jit(solution)/shard_map/all_to_all | solution.py:74
  201.6 20.7 %all_to_all.26.got = bf16[8,288,256]{2,1,0:T(8,128)(2,1)S(1)} all-to-all(bf16[8,288,256]{2,1,0:T(8,128)(2,1)S(1)} %shard_map.91), channel_id=1, replica_groups=mesh['x'=4,'zh'=2,'zl'=2,'y'=4,'c'=2] {'x','zh'}, dimensions={0} | all-to-all | bytes 2359296 | tf_op jit(solution)/shard_map/all_to_all | solution.py:74
  222.3 1.9 shard_map.92
  (82 shorter events, 15.3 us)
Async XLA Ops:
  0.6 2.2 copy-start.2
  3.5 1.6 copy-start.1
  3.5 1.6 copy-start.3
  5.1 18.3 %collective-permute-start.4 = (bf16[2304,256]{1,0:T(8,128)(2,1)S(1)}, bf16[2304,256]{1,0:T(8,128)(2,1)S(1)}, u32[]{:S(2)}, u32[]{:S(2)}) collective-permute-start(bf16[2304,256]{1,0:T(8,128)(2,1)S(1)} %shard_map.77.own), channel_id=1, source_target_pairs={{0,8},{1,25},{8,16},{9,1},{16,24},{17,9},{24,0},{25,17},{2,10},{3,... | collective-permute-start | bytes 3538952 | tf_op jit(solution)/shard_map/ppermute | solution.py:70
  7.1 35.4 %collective-permute-start.5 = (bf16[2304,256]{1,0:T(8,128)(2,1)S(1)}, bf16[2304,256]{1,0:T(8,128)(2,1)S(1)}, u32[]{:S(2)}, u32[]{:S(2)}) collective-permute-start(bf16[2304,256]{1,0:T(8,128)(2,1)S(1)} %shard_map.77.own), channel_id=1, source_target_pairs={{0,1},{1,0},{2,3},{3,2},{4,5},{5,4},{6,7},{7,6},{8,9},{9,8},{10,11... | collective-permute-start | bytes 3538952 | tf_op jit(solution)/shard_map/ppermute | solution.py:62
  23.4 19.1 %collective-permute-start.6 = (bf16[2304,256]{1,0:T(8,128)(2,1)S(1)}, bf16[2304,256]{1,0:T(8,128)(2,1)S(1)}, u32[]{:S(2)}, u32[]{:S(2)}) collective-permute-start(bf16[2304,256]{1,0:T(8,128)(2,1)S(1)} %collective-permute-done.4.far), channel_id=1, source_target_pairs={{0,1},{1,0},{2,3},{3,2},{4,5},{5,4},{6,7},{7,6},{8,9},{9,8},{10,11... | collective-permute-start | bytes 3538952 | tf_op jit(solution)/shard_map/ppermute | solution.py:62
  23.4 9.7 %collective-permute-start = (bf16[64,2048]{1,0:T(8,128)(2,1)S(1)}, bf16[64,2048]{1,0:T(8,128)(2,1)S(1)}, u32[]{:S(2)}, u32[]{:S(2)}) collective-permute-start(bf16[64,2048]{1,0:T(8,128)(2,1)S(1)} %get-tuple-element.27.after.a0), channel_id=1, source_target_pairs={{0,6},{2,0},{4,2},{6,4},{1,7},{3,1},{5,3},{7,5},{8,14},{10,8},{12,... | collective-permute-start | bytes 786440 | tf_op jit(solution)/shard_map/ppermute | solution.py:58
  26.4 9.6 %collective-permute-start.1 = (bf16[64,2048]{1,0:T(8,128)(2,1)S(1)}, bf16[64,2048]{1,0:T(8,128)(2,1)S(1)}, u32[]{:S(2)}, u32[]{:S(2)}) collective-permute-start(bf16[64,2048]{1,0:T(8,128)(2,1)S(1)} %get-tuple-element.27.after.a0), channel_id=1, source_target_pairs={{0,2},{2,4},{4,6},{6,0},{1,3},{3,5},{5,7},{7,1},{8,10},{10,12},{12... | collective-permute-start | bytes 786440 | tf_op jit(solution)/shard_map/ppermute | solution.py:58
  26.4 11.9 %collective-permute-start.2 = (bf16[64,2048]{1,0:T(8,128)(2,1)S(1)}, bf16[64,2048]{1,0:T(8,128)(2,1)S(1)}, u32[]{:S(2)}, u32[]{:S(2)}) collective-permute-start(bf16[64,2048]{1,0:T(8,128)(2,1)S(1)} %get-tuple-element.28.b0), channel_id=1, source_target_pairs={{0,6},{2,0},{4,2},{6,4},{1,7},{3,1},{5,3},{7,5},{8,14},{10,8},{12,... | collective-permute-start | bytes 786440 | tf_op jit(solution)/shard_map/ppermute | solution.py:58
  33.1 9.3 %collective-permute-start.3 = (bf16[64,2048]{1,0:T(8,128)(2,1)S(1)}, bf16[64,2048]{1,0:T(8,128)(2,1)S(1)}, u32[]{:S(2)}, u32[]{:S(2)}) collective-permute-start(bf16[64,2048]{1,0:T(8,128)(2,1)S(1)} %get-tuple-element.28.b0), channel_id=1, source_target_pairs={{0,2},{2,4},{4,6},{6,0},{1,3},{3,5},{5,7},{7,1},{8,10},{10,12},{12... | collective-permute-start | bytes 786440 | tf_op jit(solution)/shard_map/ppermute | solution.py:58
  45.6 32.7 %collective-permute-start.9 = (bf16[384,2048]{1,0:T(8,128)(2,1)}, bf16[384,2048]{1,0:T(8,128)(2,1)}, u32[]{:S(2)}, u32[]{:S(2)}) collective-permute-start(bf16[384,2048]{1,0:T(8,128)(2,1)} %get-tuple-element.29.refs_0_), channel_id=1, source_target_pairs={{0,8},{1,25},{8,16},{9,1},{16,24},{17,9},{24,0},{25,17},{2,10},{3,... | collective-permute-start | bytes 4718600 | tf_op jit(solution)/shard_map/ppermute | solution.py:70
  45.7 10.5 %collective-permute-start.7 = (bf16[64,2048]{1,0:T(8,128)(2,1)S(1)}, bf16[64,2048]{1,0:T(8,128)(2,1)S(1)}, u32[]{:S(2)}, u32[]{:S(2)}) collective-permute-start(bf16[64,2048]{1,0:T(8,128)(2,1)S(1)} %collective-permute-done.1.a3), channel_id=1, source_target_pairs={{0,2},{2,4},{4,6},{6,0},{1,3},{3,5},{5,7},{7,1},{8,10},{10,12},{12... | collective-permute-start | bytes 786440 | tf_op jit(solution)/shard_map/ppermute | solution.py:58
  45.8 10.4 %collective-permute-start.8 = (bf16[64,2048]{1,0:T(8,128)(2,1)S(1)}, bf16[64,2048]{1,0:T(8,128)(2,1)S(1)}, u32[]{:S(2)}, u32[]{:S(2)}) collective-permute-start(bf16[64,2048]{1,0:T(8,128)(2,1)S(1)} %collective-permute-done.2.b1), channel_id=1, source_target_pairs={{0,6},{2,0},{4,2},{6,4},{1,7},{3,1},{5,3},{7,5},{8,14},{10,8},{12,... | collective-permute-start | bytes 786440 | tf_op jit(solution)/shard_map/ppermute | solution.py:58
  49.0 17.2 %copy-start.5 = (s32[128]{0:T(128)S(1)}, s32[128]{0:T(128)}, u32[]{:S(2)}) copy-start(s32[128]{0:T(128)} %param.7) | copy-start | bytes 1540
  49.0 10.9 %collective-permute-start.15 = (f32[128,256]{1,0:T(8,128)S(1)}, f32[128,256]{1,0:T(8,128)S(1)}, u32[]{:S(2)}, u32[]{:S(2)}) collective-permute-start(f32[128,256]{1,0:T(8,128)S(1)} %get-tuple-element.35), channel_id=1, source_target_pairs={{0,2},{2,4},{4,6},{6,0},{1,3},{3,5},{5,7},{7,1},{8,10},{10,12},{12... | collective-permute-start | bytes 393224 | tf_op jit(solution)/shard_map/ppermute | solution.py:58
  57.5 6.6 %collective-permute-start.16 = (f32[128,256]{1,0:T(8,128)S(1)}, f32[128,256]{1,0:T(8,128)S(1)}, u32[]{:S(2)}, u32[]{:S(2)}) collective-permute-start(f32[128,256]{1,0:T(8,128)S(1)} %get-tuple-element.36), channel_id=1, source_target_pairs={{0,4},{2,6},{4,0},{6,2},{1,5},{3,7},{5,1},{7,3},{8,12},{10,14},{12... | collective-permute-start | bytes 393224 | tf_op jit(solution)/shard_map/ppermute | solution.py:58
  58.3 7.8 %collective-permute-start.17 = (f32[128,256]{1,0:T(8,128)S(1)}, f32[128,256]{1,0:T(8,128)S(1)}, u32[]{:S(2)}, u32[]{:S(2)}) collective-permute-start(f32[128,256]{1,0:T(8,128)S(1)} %get-tuple-element.37), channel_id=1, source_target_pairs={{0,6},{2,0},{4,2},{6,4},{1,7},{3,1},{5,3},{7,5},{8,14},{10,8},{12,... | collective-permute-start | bytes 393224 | tf_op jit(solution)/shard_map/ppermute | solution.py:58
  67.4 20.8 %all-to-all-start = ((bf16[16,128,256]{2,1,0:T(8,128)(2,1)}), bf16[16,128,256]{2,1,0:T(8,128)(2,1)S(1)}, u32[]{:S(2)}, u32[]{:S(2)}) async-start(bf16[16,128,256]{2,1,0:T(8,128)(2,1)} %get-tuple-element.40), calls=%async_computation | async-start | bytes 2097152 | tf_op jit(solution)/shard_map/all_to_all | solution.py:74
  72.2 1.3 collective-permute-start.18
  73.5 11.2 %collective-permute-start.19 = (bf16[256,384]{1,0:T(8,128)(2,1)S(1)}, bf16[256,384]{1,0:T(8,128)(2,1)S(1)}, u32[]{:S(2)}, u32[]{:S(2)}) collective-permute-start(bf16[256,384]{1,0:T(8,128)(2,1)S(1)} %shard_map.84.pay0), channel_id=1, source_target_pairs={{0,6},{2,0},{4,2},{6,4},{1,7},{3,1},{5,3},{7,5},{8,14},{10,8},{12,... | collective-permute-start | bytes 589832 | tf_op jit(solution)/shard_map/ppermute | solution.py:58
  76.0 9.3 %collective-permute-start.20 = (bf16[256,384]{1,0:T(8,128)(2,1)S(1)}, bf16[256,384]{1,0:T(8,128)(2,1)S(1)}, u32[]{:S(2)}, u32[]{:S(2)}) collective-permute-start(bf16[256,384]{1,0:T(8,128)(2,1)S(1)} %shard_map.84.pay0), channel_id=1, source_target_pairs={{0,4},{2,6},{4,0},{6,2},{1,5},{3,7},{5,1},{7,3},{8,12},{10,14},{12... | collective-permute-start | bytes 589832 | tf_op jit(solution)/shard_map/ppermute | solution.py:58
  76.2 12.1 %collective-permute-start.21 = (bf16[256,384]{1,0:T(8,128)(2,1)S(1)}, bf16[256,384]{1,0:T(8,128)(2,1)}, u32[]{:S(2)}, u32[]{:S(2)}) collective-permute-start(bf16[256,384]{1,0:T(8,128)(2,1)S(1)} %shard_map.84.pay0), channel_id=1, source_target_pairs={{0,2},{2,4},{4,6},{6,0},{1,3},{3,5},{5,7},{7,1},{8,10},{10,12},{12... | collective-permute-start | bytes 589832 | tf_op jit(solution)/shard_map/ppermute | solution.py:58
  78.2 74.7 %collective-permute-start.11 = (bf16[384,2048]{1,0:T(8,128)(2,1)}, bf16[384,2048]{1,0:T(8,128)(2,1)}, u32[]{:S(2)}, u32[]{:S(2)}) collective-permute-start(bf16[384,2048]{1,0:T(8,128)(2,1)} %get-tuple-element.29.refs_0_), channel_id=1, source_target_pairs={{0,1},{1,0},{2,3},{3,2},{4,5},{5,4},{6,7},{7,6},{8,9},{9,8},{10,11... | collective-permute-start | bytes 4718600 | tf_op jit(solution)/shard_map/ppermute | solution.py:62
  78.3 81.2 %collective-permute-start.13 = (bf16[384,2048]{1,0:T(8,128)(2,1)}, bf16[384,2048]{1,0:T(8,128)(2,1)}, u32[]{:S(2)}, u32[]{:S(2)}) collective-permute-start(bf16[384,2048]{1,0:T(8,128)(2,1)} %collective-permute-done.9.refs_2_), channel_id=1, source_target_pairs={{0,1},{1,0},{2,3},{3,2},{4,5},{5,4},{6,7},{7,6},{8,9},{9,8},{10,11... | collective-permute-start | bytes 4718600 | tf_op jit(solution)/shard_map/ppermute | solution.py:62
  94.1 0.8 copy-start.14
  94.9 0.8 copy-start.16
  95.7 15.6 %all-to-all-start.1 = ((f32[16,1,2176]{2,1,0:T(1,128)}), f32[16,1,2176]{2,1,0:T(1,128)S(1)}, u32[]{:S(2)}, u32[]{:S(2)}) async-start(f32[16,1,2176]{2,1,0:T(1,128)} %get-tuple-element.44), calls=%async_computation.1 | async-start | bytes 278528 | tf_op jit(solution)/shard_map/all_to_all | solution.py:74
  103.0 1.2 collective-permute-start.22
  104.1 3.7 %collective-permute-start.23 = (f32[8,128]{1,0:T(8,128)S(1)}, f32[8,128]{1,0:T(8,128)S(1)}, u32[]{:S(2)}, u32[]{:S(2)}) collective-permute-start(f32[8,128]{1,0:T(8,128)S(1)} %shard_map.86.sum0), channel_id=1, source_target_pairs={{0,6},{2,0},{4,2},{6,4},{1,7},{3,1},{5,3},{7,5},{8,14},{10,8},{12,... | collective-permute-start | bytes 12296 | tf_op jit(solution)/shard_map/ppermute | solution.py:58
  105.0 5.1 %collective-permute-start.24 = (f32[8,128]{1,0:T(8,128)S(1)}, f32[8,128]{1,0:T(8,128)S(1)}, u32[]{:S(2)}, u32[]{:S(2)}) collective-permute-start(f32[8,128]{1,0:T(8,128)S(1)} %shard_map.86.sum0), channel_id=1, source_target_pairs={{0,4},{2,6},{4,0},{6,2},{1,5},{3,7},{5,1},{7,3},{8,12},{10,14},{12... | collective-permute-start | bytes 12296 | tf_op jit(solution)/shard_map/ppermute | solution.py:58
  105.3 5.4 %collective-permute-start.25 = (f32[8,128]{1,0:T(8,128)S(1)}, f32[8,128]{1,0:T(8,128)S(1)}, u32[]{:S(2)}, u32[]{:S(2)}) collective-permute-start(f32[8,128]{1,0:T(8,128)S(1)} %shard_map.86.sum0), channel_id=1, source_target_pairs={{0,2},{2,4},{4,6},{6,0},{1,3},{3,5},{5,7},{7,1},{8,10},{10,12},{12... | collective-permute-start | bytes 12296 | tf_op jit(solution)/shard_map/ppermute | solution.py:58
  108.4 20.5 %collective-permute-start.10 = (bf16[128,2048]{1,0:T(8,128)(2,1)S(1)}, bf16[128,2048]{1,0:T(8,128)(2,1)S(1)}, u32[]{:S(2)}, u32[]{:S(2)}) collective-permute-start(bf16[128,2048]{1,0:T(8,128)(2,1)S(1)} %get-tuple-element.30.refs_1_), channel_id=1, source_target_pairs={{0,8},{1,25},{8,16},{9,1},{16,24},{17,9},{24,0},{25,17},{2,10},{3,... | collective-permute-start | bytes 1572872 | tf_op jit(solution)/shard_map/ppermute | solution.py:70
  111.3 0.7 copy-start.7
  112.0 0.7 copy-start.9
  114.0 1.0 copy-start.15
  115.1 1.0 copy-start.17
  123.2 21.1 %all-to-all-start.2 = ((f32[8,128,256]{2,1,0:T(8,128)}), f32[8,128,256]{2,1,0:T(8,128)S(1)}, u32[]{:S(2)}, u32[]{:S(2)}) async-start(f32[8,128,256]{2,1,0:T(8,128)} %get-tuple-element.45), calls=%async_computation.2 | async-start | bytes 2097152 | tf_op jit(solution)/shard_map/all_to_all | solution.py:74
  128.4 23.0 %collective-permute-start.12 = (bf16[128,2048]{1,0:T(8,128)(2,1)S(1)}, bf16[128,2048]{1,0:T(8,128)(2,1)}, u32[]{:S(2)}, u32[]{:S(2)}) collective-permute-start(bf16[128,2048]{1,0:T(8,128)(2,1)S(1)} %get-tuple-element.30.refs_1_), channel_id=1, source_target_pairs={{0,1},{1,0},{2,3},{3,2},{4,5},{5,4},{6,7},{7,6},{8,9},{9,8},{10,11... | collective-permute-start | bytes 1572872 | tf_op jit(solution)/shard_map/ppermute | solution.py:62
  128.9 23.9 %collective-permute-start.14 = (bf16[128,2048]{1,0:T(8,128)(2,1)S(1)}, bf16[128,2048]{1,0:T(8,128)(2,1)}, u32[]{:S(2)}, u32[]{:S(2)}) collective-permute-start(bf16[128,2048]{1,0:T(8,128)(2,1)S(1)} %collective-permute-done.10.refs_3_), channel_id=1, source_target_pairs={{0,1},{1,0},{2,3},{3,2},{4,5},{5,4},{6,7},{7,6},{8,9},{9,8},{10,11... | collective-permute-start | bytes 1572872 | tf_op jit(solution)/shard_map/ppermute | solution.py:62
  144.5 5.5 %collective-permute-start.26 = (bf16[128,256]{1,0:T(8,128)(2,1)S(1)}, bf16[128,256]{1,0:T(8,128)(2,1)S(1)}, u32[]{:S(2)}, u32[]{:S(2)}) collective-permute-start(bf16[128,256]{1,0:T(8,128)(2,1)S(1)} %shard_map.88.own), channel_id=1, source_target_pairs={{0,8},{1,25},{8,16},{9,1},{16,24},{17,9},{24,0},{25,17},{2,10},{3,... | collective-permute-start | bytes 196616 | tf_op jit(solution)/shard_map/ppermute | solution.py:70
  150.2 5.1 %collective-permute-start.27 = (bf16[272,256]{1,0:T(8,128)(2,1)S(1)}, bf16[272,256]{1,0:T(8,128)(2,1)S(1)}, u32[]{:S(2)}, u32[]{:S(2)}) collective-permute-start(bf16[272,256]{1,0:T(8,128)(2,1)S(1)} %shard_map.89.refs_4_), channel_id=1, source_target_pairs={{0,6},{2,0},{4,2},{6,4},{1,7},{3,1},{5,3},{7,5},{8,14},{10,8},{12,... | collective-permute-start | bytes 417800 | tf_op jit(solution)/shard_map/ppermute | solution.py:58
  151.4 6.6 %collective-permute-start.28 = (bf16[272,256]{1,0:T(8,128)(2,1)S(1)}, bf16[272,256]{1,0:T(8,128)(2,1)S(1)}, u32[]{:S(2)}, u32[]{:S(2)}) collective-permute-start(bf16[272,256]{1,0:T(8,128)(2,1)S(1)} %shard_map.89.refs_4_), channel_id=1, source_target_pairs={{0,4},{2,6},{4,0},{6,2},{1,5},{3,7},{5,1},{7,3},{8,12},{10,14},{12... | collective-permute-start | bytes 417800 | tf_op jit(solution)/shard_map/ppermute | solution.py:58
  152.9 6.6 %collective-permute-start.29 = (bf16[272,256]{1,0:T(8,128)(2,1)S(1)}, bf16[272,256]{1,0:T(8,128)(2,1)S(1)}, u32[]{:S(2)}, u32[]{:S(2)}) collective-permute-start(bf16[272,256]{1,0:T(8,128)(2,1)S(1)} %shard_map.89.refs_4_), channel_id=1, source_target_pairs={{0,2},{2,4},{4,6},{6,0},{1,3},{3,5},{5,7},{7,1},{8,10},{10,12},{12... | collective-permute-start | bytes 417800 | tf_op jit(solution)/shard_map/ppermute | solution.py:58
  152.9 16.8 %collective-permute-start.30 = (bf16[272,256]{1,0:T(8,128)(2,1)S(1)}, bf16[272,256]{1,0:T(8,128)(2,1)S(1)}, u32[]{:S(2)}, u32[]{:S(2)}) collective-permute-start(bf16[272,256]{1,0:T(8,128)(2,1)S(1)} %shard_map.89.refs_4_), channel_id=1, source_target_pairs={{0,1},{1,0},{2,3},{3,2},{4,5},{5,4},{6,7},{7,6},{8,9},{9,8},{10,11... | collective-permute-start | bytes 417800 | tf_op jit(solution)/shard_map/ppermute | solution.py:62
  155.3 14.4 %collective-permute-start.31 = (bf16[272,256]{1,0:T(8,128)(2,1)S(1)}, bf16[272,256]{1,0:T(8,128)(2,1)S(1)}, u32[]{:S(2)}, u32[]{:S(2)}) collective-permute-start(bf16[272,256]{1,0:T(8,128)(2,1)S(1)} %collective-permute-done.27.refs_5_), channel_id=1, source_target_pairs={{0,1},{1,0},{2,3},{3,2},{4,5},{5,4},{6,7},{7,6},{8,9},{9,8},{10,11... | collective-permute-start | bytes 417800 | tf_op jit(solution)/shard_map/ppermute | solution.py:62
  158.0 11.7 %collective-permute-start.32 = (bf16[272,256]{1,0:T(8,128)(2,1)S(1)}, bf16[272,256]{1,0:T(8,128)(2,1)S(1)}, u32[]{:S(2)}, u32[]{:S(2)}) collective-permute-start(bf16[272,256]{1,0:T(8,128)(2,1)S(1)} %collective-permute-done.28.refs_6_), channel_id=1, source_target_pairs={{0,1},{1,0},{2,3},{3,2},{4,5},{5,4},{6,7},{7,6},{8,9},{9,8},{10,11... | collective-permute-start | bytes 417800 | tf_op jit(solution)/shard_map/ppermute | solution.py:62
  159.4 10.2 %collective-permute-start.33 = (bf16[272,256]{1,0:T(8,128)(2,1)S(1)}, bf16[272,256]{1,0:T(8,128)(2,1)S(1)}, u32[]{:S(2)}, u32[]{:S(2)}) collective-permute-start(bf16[272,256]{1,0:T(8,128)(2,1)S(1)} %collective-permute-done.29.refs_7_), channel_id=1, source_target_pairs={{0,1},{1,0},{2,3},{3,2},{4,5},{5,4},{6,7},{7,6},{8,9},{9,8},{10,11... | collective-permute-start | bytes 417800 | tf_op jit(solution)/shard_map/ppermute | solution.py:62
  169.7 3.4 %copy-start = (bf16[2048,2048]{1,0:T(8,128)(2,1)S(1)}, bf16[2048,2048]{1,0:T(8,128)(2,1)}, u32[]{:S(2)}) copy-start(bf16[2048,2048]{1,0:T(8,128)(2,1)} %get-tuple-element.31.refs_0_) | copy-start | bytes 25165828
  (7 other events, 4.3 us)

commit v2 on v1

v2 whole, which is shorter than its diff:
```python
import math

import jax
import jax.numpy as jnp
from jax import lax
from jax.experimental import pallas as pl
from jax.experimental.pallas import tpu as pltpu
from jax.sharding import Mesh
from jax.sharding import PartitionSpec as P


BLK = ("x", "zh")
GRP = ("zl", "y", "c")
ALL = ("x", "zh", "zl", "y", "c")
ZC = ("zh", "zl", "c")
XZ = ("x", "zh", "zl")


bf16 = jnp.bfloat16
f32 = jnp.float32
i32 = jnp.int32

sharpness = 0.05
log2e = math.log2(math.e)

ROWS = 128
HALF = 64
C = 2048
U = 256
E = 256
SLOTS = 8
TOTAL = 16384
CELLS = (0, 1, 3, 2)


def sds(shape, dtype):
    return jax.ShapeDtypeStruct(shape, dtype)


def far_sds(shape, dtype):
    return pltpu.HBM(shape, dtype)


def kept(array):
    return pltpu.with_memory_space_constraint(array, pltpu.HBM)


def kernel(body, outs, *args, grid=None, in_specs=None, out_specs=None, scratch=(), mib=24, flops=0):
    extra = {}
    if in_specs is not None:
        extra = dict(in_specs=in_specs, out_specs=out_specs)
    if grid is not None:
        extra["grid"] = grid
    return pl.pallas_call(
        body,
        out_shape=outs,
        scratch_shapes=list(scratch),
        compiler_params=pltpu.CompilerParams(vmem_limit_bytes=mib * 1024 * 1024),
        cost_estimate=pl.CostEstimate(flops=flops, bytes_accessed=0, transcendentals=0),
        **extra,
    )(*args)


def along_y(block, distance):
    return lax.ppermute(block, "y", [(i, (i + distance) % 4) for i in range(4)])


def swap(block):
    return lax.ppermute(block, "c", [(0, 1), (1, 0)])


def along_z(block):
    pairs = []
    for zz in range(4):
        pairs.append((zz * 2, ((zz + 1) % 4) * 2))
        pairs.append((zz * 2 + 1, ((zz - 1) % 4) * 2 + 1))
    return lax.ppermute(block, ZC, pairs)


def exchange(array, axis):
    return lax.all_to_all(array, axis, 0, 0, tiled=True)


def dot(a, b):
    return jnp.dot(a, b, preferred_element_type=f32)


def dot_t(a, b):
    return lax.dot_general(a, b, (((1,), (1,)), ((), ())), preferred_element_type=f32)


def as_column(row):
    return jnp.broadcast_to(row, (ROWS, 128)).T


def pool_body(frames, counts, out_a, out_b, column):
    step = pl.program_id(0)

    @pl.when(step == 0)
    def _():
        column[...] = as_column(counts[...].astype(f32))

    slot = lax.broadcasted_iota(i32, (32, 256), 1)
    row = lax.broadcasted_iota(i32, (32, 256), 0)
    low = row * SLOTS

    def half(out):
        for i in range(2):
            at = pl.multiple_of(step * HALF + i * 32, 32)
            n = column[pl.ds(at, 32), 0:1]
            mask = ((slot >= low) & (slot < low + n.astype(i32))).astype(f32).astype(bf16)
            mean = dot(mask, frames[i * 256 : (i + 1) * 256, :]) / n
            out[i * 32 : (i + 1) * 32, :] = mean.astype(bf16)

    @pl.when(step == 0)
    def _():
        half(out_a)

    @pl.when(step == 1)
    def _():
        half(out_b)


def gelu(v):
    k = math.sqrt(2.0 / math.pi)
    return v * (0.5 * (1.0 + jnp.tanh(k * (v + 0.044715 * (v * v * v)))))


def forward_sum(block, weights):
    total = None
    for w1, w2 in zip(weights[:4], weights[4:]):
        hidden = gelu(dot(block, w1[...])).astype(bf16)
        part = dot(hidden, w2[...])
        total = part if total is None else total + part
    return total


def near_body(a0, b0, a1, b1, a3, b3, *refs):
    weights, (near, ring, p0, p1, p3) = refs[:8], refs[8:]
    for i, piece in enumerate((a0, b0, a1, b1, a3, b3)):
        near[i * HALF : (i + 1) * HALF, :] = piece[...]
    ring[...] = near[ROWS:, :]
    part = forward_sum(near[...], weights)
    for i, out in enumerate((p0, p1, p3)):
        out[...] = part[i * ROWS : (i + 1) * ROWS]


def far_body(a2, b2, *refs):
    weights, (block, p2) = refs[:8], refs[8:]
    block[:HALF, :] = a2[...]
    block[HALF:, :] = b2[...]
    p2[...] = forward_sum(block[...], weights)


def keys_body(p0, p1, p2, p3, partner, raw, pay, spread):
    total = p0[...] + p1[...] + p2[...] + p3[...]
    raw[...] = total
    length = jnp.sqrt(jnp.sum(total * total, axis=1, keepdims=True) + 1e-06)
    half = (total / length).astype(bf16)
    row = partner[...]
    high = (row // 128).astype(f32)
    low = (row % 128).astype(f32)
    lane = lax.broadcasted_iota(i32, (ROWS, 128), 1)
    code = jnp.where(lane == 0, as_column(high), jnp.where(lane == 1, as_column(low), 0.0))
    code = code.astype(bf16)
    for i in range(16):
        spread[i] = half
    pay[:, :E] = half
    pay[:, E:] = code


def pair_body(own, mate, out):
    out[:ROWS, :] = own[...]
    out[ROWS:, :] = mate[...]


def pair_sum_body(own, mate, out):
    for d in range(4):
        for m in range(2):
            r = 2 * d + m
            other = 2 * d + 1 - m
            out[r : r + 1, :] = own[r : r + 1, :] + mate[other : other + 1, :]


def column_ids(base, j):
    lane = lax.broadcasted_iota(i32, (1, 256), 1)
    block = 2 * j + lane // 128
    return base + block * 1024 + lane % 128


def exp_block(scaled, ids, own_row):
    exps = jnp.exp2(scaled * (log2e / sharpness))
    row = own_row + lax.broadcasted_iota(i32, (ROWS, 1), 0)
    return jnp.concatenate([jnp.where(ids == row, 0.0, exps[:ROWS]), exps[ROWS:]], axis=0)


def place_body(given, out):
    for i in range(5):
        out[i] = given[i]


def score_body(where, pay0, pay1, pay2, pay3, cols, row_out, col_out, tile, who, acc):
    for d, pay in enumerate((pay0, pay1, pay2, pay3)):
        tile[d * 256 : (d + 1) * 256, :] = pay[:, :E]
        code = pay[:, E:].astype(f32)
        number = code[:, 0:1] * 128.0 + code[:, 1:2]
        who[d * 256 : (d + 1) * 256, :] = jnp.broadcast_to(number, (256, 128))
    found = jnp.zeros((1, 256), f32)
    for j in range(8):
        block = cols[2 * j : 2 * j + 2].reshape(256, E)
        scaled = dot_t(tile[...], block)
        ids = column_ids(where[1], j)
        here = exp_block(scaled, ids, where[0])
        ids = ids.astype(f32)
        hit = jnp.concatenate([who[...] == ids[:, :128], who[...] == ids[:, 128:]], axis=1)
        found = found + jnp.sum(jnp.where(hit, scaled, 0.0), axis=0, keepdims=True)
        two = here[:, :128] + here[:, 128:]
        if j == 0:
            acc[...] = two
        else:
            acc[...] += two
        sums = jnp.sum(here, axis=0, keepdims=True)
        for i in range(16):
            col_out[i, :, j * 256 : (j + 1) * 256] = sums
    positive = jnp.sum(found) / sharpness
    for i in range(16):
        col_out[i, :, 2048:] = jnp.full((1, 128), positive, f32)
    for r in range(8):
        total = jnp.sum(acc[r * ROWS : (r + 1) * ROWS, :].T, axis=0, keepdims=True)
        row_out[r : r + 1, :] = total


def weight_body(
    where, tile, who, cols, sum0, sum1, sum2, sum3, col_sums, own, mate, loss, scale, acc
):
    sums = (sum0, sum1, sum2, sum3)
    for r in range(8):
        d, m = divmod(r, 2)
        total = None
        for s in range(4):
            at = (d - s) % 4 * 2 + m
            part = sums[s][at : at + 1, :]
            total = part if total is None else total + part
        scale[r * ROWS : (r + 1) * ROWS, :] = as_column(1.0 / total)
    columns = col_sums[0]
    for i in range(1, 16):
        columns = columns + col_sums[i]
    logs = jnp.log(columns[:, :2048])
    loss[...] = jnp.full((1, 128), jnp.sum(logs) - jnp.sum(columns[:, 2048:2049]), f32)
    for j in range(8):
        block = cols[2 * j : 2 * j + 2].reshape(256, E)
        scaled = dot_t(tile[...], block)
        ids = column_ids(where[1], j)
        here = exp_block(scaled, ids, where[0])
        ids = ids.astype(f32)
        by_col = 1.0 / columns[:, j * 256 : (j + 1) * 256]
        sides = [], []
        for low in (0, 128):
            half = here[:, low : low + 128]
            hit = jnp.where(who[...] == ids[:, low : low + 128], 1.0, 0.0)
            sides[0].append((half * scale[...] - hit).astype(bf16))
            sides[1].append((half * by_col[:, low : low + 128] - hit).astype(bf16))
        weights = jnp.concatenate(sides[0], axis=1)
        mirror = jnp.concatenate(sides[1], axis=1)
        part = dot(weights, block) + dot(mirror, block)
        if j == 0:
            acc[...] = part
        elif j < 7:
            acc[...] += part
        else:
            part = acc[...] + part
            for r in range(8):
                d, m = divmod(r, 2)
                out = mate if m else own
                out[pl.ds((where[3] + d) % 4, 1)] = part[r * ROWS : (r + 1) * ROWS].reshape(1, ROWS, E)


def add_body(a, b, out):
    out[...] = a[...] + b[...]


def raw_grad_body(raw, got, loss, out):
    total = raw[...]
    length = jnp.sqrt(jnp.sum(total * total, axis=1, keepdims=True) + 1e-06)
    unit = total / length
    grad = got[0]
    for i in range(1, 4):
        grad = grad + got[i]
    grad = grad / (TOTAL * sharpness)
    along = jnp.sum(unit * grad, axis=1, keepdims=True)
    out[:ROWS, :] = ((grad - unit * along) / length).astype(bf16)
    value = loss[:, 0:1]
    high = value.astype(bf16).astype(f32)
    mid = (value - high).astype(bf16).astype(f32)
    low = value - high - mid
    lane = lax.broadcasted_iota(i32, (16, E), 1)
    rows = jnp.where(lane == 0, high, jnp.where(lane == 1, mid, jnp.where(lane == 2, low, 0.0)))
    out[ROWS:, :] = rows.astype(bf16)


def slope_body(*refs):
    *pools, w1, hidden, slope, joined, acc = refs
    step = pl.program_id(0)
    low = 0
    for pool in pools:
        n = pool.shape[0]
        joined[low : low + n, :] = pool[...]
        low += n
    part = dot(joined[...], w1[...])

    @pl.when(step == 0)
    def _():
        acc[...] = part

    @pl.when(step > 0)
    def _():
        acc[...] += part

    @pl.when(step == 3)
    def _():
        k = math.sqrt(2.0 / math.pi)
        n = 256
        for low in range(0, 8 * ROWS, n):
            v = acc[low : low + n, :]
            t = jnp.tanh(k * (v + 0.044715 * (v * v * v)))
            hidden[:, low : low + n] = (v * (0.5 * (1.0 + t))).astype(bf16).T
            rise = k * (1.0 + 3 * 0.044715 * (v * v))
            turn = 0.5 * (1.0 + t) + (0.5 * v) * (1.0 - t * t) * rise
            slope[:, low : low + n] = turn.T


def head_body(pool_a, pool_b, hidden_a, hidden_b, slope_a, slope_b, w2, *refs):
    rings, (out, loss, grads, turned, second) = refs[:16], refs[16:]
    step = pl.program_id(0)
    rows = 8 * ROWS

    @pl.when(step == 0)
    def _():
        low = 0
        for z in range(2):
            for core in range(2):
                for d in CELLS:
                    grads[low : low + ROWS, :] = rings[z * 8 + core * 4 + d][:ROWS, :]
                    low += ROWS
        turned[:, :rows] = (dot_t(w2[...], grads[:rows, :]) * slope_a[...]).astype(bf16)
        turned[:, rows:] = (dot_t(w2[...], grads[rows:, :]) * slope_b[...]).astype(bf16)
        total = jnp.zeros((1, E), f32)
        for ring in rings[:8]:
            total = total + ring[ROWS : ROWS + 16, :].astype(f32)[0:1]
        loss[...] = jnp.full((1, 128), jnp.sum(total) / TOTAL, f32)
        both = dot(hidden_a[...], grads[:rows, :]) + dot(hidden_b[...], grads[rows:, :])
        second[...] = both.astype(bf16)

    first = dot(turned[:, :rows], pool_a[...]) + dot(turned[:, rows:], pool_b[...])
    first = first.astype(bf16)
    for i in range(2):
        out[i, :U, :] = first[:, i * 256 : (i + 1) * 256]
        out[i, U:, :] = second[pl.ds(pl.multiple_of(step * 64 + i * 32, 32), 32), :]


def piece_body(got, out):
    total = got[0].astype(f32)
    for i in range(1, 8):
        total = total + got[i].astype(f32)
    first = total[:U, :].T.astype(bf16)
    second = total[U:, :].astype(bf16)
    for i in range(8):
        out[i, :U, :] = first
        out[i, U:, :] = second


def final_body(got, first, second):
    for i in range(2):
        first[i * 256 : (i + 1) * 256, :] = got[i, :U, :].astype(f32)
        second[i * 32 : (i + 1) * 32, :] = got[i, U:, :].astype(f32)


def step(frames, counts, positives, w_first, w_second):
    x, zh, zl = lax.axis_index("x"), lax.axis_index("zh"), lax.axis_index("zl")
    y, c = lax.axis_index("y"), lax.axis_index("c")
    base = (y * 2 + c) * ROWS
    cell = x * 4 + zh * 2 + zl
    where = jnp.stack([cell * 1024 + base, base, cell // 2, y, c]).astype(i32)
    vm = pl.BlockSpec()
    smem = pl.BlockSpec(memory_space=pltpu.SMEM)
    hbm = pl.BlockSpec(memory_space=pl.ANY)

    w1_far = along_z(w_first)
    a0, b0 = kernel(
        pool_body,
        (sds((HALF, C), bf16), sds((HALF, C), bf16)),
        kept(frames.reshape(ROWS * SLOTS, C)),
        counts.reshape(1, ROWS),
        grid=(2,),
        in_specs=[
            pl.BlockSpec((512, C), lambda i: (i, 0)),
            pl.BlockSpec((1, ROWS), lambda i: (0, 0)),
        ],
        out_specs=[
            pl.BlockSpec((HALF, C), lambda i: (0, 0)),
            pl.BlockSpec((HALF, C), lambda i: (0, 0)),
        ],
        scratch=[pltpu.VMEM((ROWS, 128), f32)],
        flops=10**8,
    )
    a3, b1 = along_y(a0, 1), along_y(b0, -1)
    b3, a1 = along_y(b0, 1), along_y(a0, -1)
    a2, b2 = along_y(a3, 1), along_y(b1, -1)

    w1 = [w_first, w1_far, swap(w_first), swap(w1_far)]
    w2_far = along_z(w_second)
    w2 = [w_second, w2_far, swap(w_second), swap(w2_far)]
    weights = w1 + w2

    key_part = sds((ROWS, E), f32)
    near, near_ring, p0, p1, p3 = kernel(
        near_body,
        (far_sds((6 * HALF, C), bf16), far_sds((4 * HALF, C), bf16)) + (key_part,) * 3,
        a0, b0, a1, b1, a3, b3, *weights,
        flops=2 * 10**9,
    )
    q1, q3 = along_y(p1, 1), along_y(p3, -1)
    far, p2 = kernel(
        far_body, (far_sds((ROWS, C), bf16), key_part), a2, b2, *weights, flops=5 * 10**8
    )
    q2 = along_y(p2, 2)
    raw, pay, spread = kernel(
        keys_body,
        (far_sds((ROWS, E), f32), sds((ROWS, E + 128), bf16), far_sds((16, ROWS, E), bf16)),
        p0, q1, q2, q3, positives.reshape(1, ROWS),
    )
    cols = exchange(spread, XZ)
    pair = kernel(pair_body, sds((2 * ROWS, E + 128), bf16), pay, swap(pay))
    pairs = [pair] + [along_y(pair, -d) for d in (1, 2, 3)]

    own = (near, far)
    beside = (along_z(a0), along_z(b0), along_z(near_ring), along_z(far))

    def rows_of(pools):
        return kernel(
            slope_body,
            (
                far_sds((U, 8 * ROWS), bf16),
                far_sds((U, 8 * ROWS), f32),
                far_sds((8 * ROWS, C), bf16),
            ),
            *[kept(p) for p in pools], kept(w_first),
            grid=(4,),
            in_specs=[pl.BlockSpec((p.shape[0], 512), lambda j: (0, j)) for p in pools]
            + [pl.BlockSpec((512, U), lambda j: (j, 0))],
            out_specs=[
                pl.BlockSpec((U, 8 * ROWS), lambda j: (0, 0)),
                pl.BlockSpec((U, 8 * ROWS), lambda j: (0, 0)),
                pl.BlockSpec((8 * ROWS, 512), lambda j: (0, j)),
            ],
            scratch=[pltpu.VMEM((8 * ROWS, U), f32)],
            flops=2 * 10**9,
        )

    hidden_a, slope_a, joined_a = rows_of(own + (swap(near), swap(far)))
    hidden_b, slope_b, joined_b = rows_of(
        beside + tuple(swap(p) for p in beside[:3]) + (swap(beside[3]),)
    )

    where = kernel(
        place_body, sds((5,), i32), where, in_specs=[smem], out_specs=smem
    )
    row_sums, col_sums, tile, who = kernel(
        score_body,
        (
            sds((8, ROWS), f32),
            far_sds((16, 1, 2176), f32),
            far_sds((1024, E), bf16),
            far_sds((1024, 128), f32),
        ),
        where, *pairs, cols,
        in_specs=[smem] + [vm] * 5,
        out_specs=[vm, vm, vm, vm],
        scratch=[pltpu.VMEM((1024, 128), f32)],
        flops=10**9,
    )
    col_sums = exchange(col_sums, XZ)
    row_sums = kernel(pair_sum_body, sds((8, ROWS), f32), row_sums, swap(row_sums))
    row_sums = [row_sums] + [along_y(row_sums, -d) for d in (1, 2, 3)]
    where = kernel(
        place_body, sds((5,), i32), where, in_specs=[smem], out_specs=smem
    )
    grads, mate_grads, loss = kernel(
        weight_body,
        (
            sds((4, ROWS, E), f32),
            sds((4, ROWS, E), f32),
            far_sds((1, 128), f32),
        ),
        where, kept(tile), kept(who), kept(cols), *row_sums, col_sums,
        in_specs=[smem] + [vm] * 8,
        out_specs=[vm, vm, vm],
        scratch=[
            pltpu.VMEM((1024, 128), f32),
            pltpu.VMEM((1024, E), f32),
        ],
        flops=3 * 10**9,
    )
    grads = kernel(add_body, far_sds((4, ROWS, E), f32), grads, swap(mate_grads))
    mine = exchange(grads, "y")
    raw_grad = kernel(raw_grad_body, sds((ROWS + 16, E), bf16), kept(raw), mine, loss)
    z_grad = along_z(raw_grad)

    def ring_of(block):
        core = [block] + [along_y(block, -d) for d in (1, 2, 3)]
        return core + [swap(r) for r in core]

    ring = ring_of(raw_grad) + ring_of(z_grad)
    ring_spec = pl.BlockSpec((ROWS + 16, E), lambda j: (0, 0))
    send, loss_all = kernel(
        head_body,
        (sds((8, U + 32, E), bf16), sds((1, 128), f32)),
        kept(joined_a), kept(joined_b), hidden_a, hidden_b, slope_a, slope_b, kept(w_second), *ring,
        grid=(4,),
        in_specs=[
            pl.BlockSpec((8 * ROWS, 512), lambda j: (0, j)),
            pl.BlockSpec((8 * ROWS, 512), lambda j: (0, j)),
            pl.BlockSpec((U, 8 * ROWS), lambda j: (0, 0)),
            pl.BlockSpec((U, 8 * ROWS), lambda j: (0, 0)),
            pl.BlockSpec((U, 8 * ROWS), lambda j: (0, 0)),
            pl.BlockSpec((U, 8 * ROWS), lambda j: (0, 0)),
            pl.BlockSpec((U, E), lambda j: (0, 0)),
        ]
        + [ring_spec] * 16,
        out_specs=[
            pl.BlockSpec((2, U + 32, E), lambda j: (j, 0, 0)),
            pl.BlockSpec((1, 128), lambda j: (0, 0)),
        ],
        scratch=[
            pltpu.VMEM((16 * ROWS, E), bf16),
            pltpu.VMEM((U, 16 * ROWS), bf16),
            pltpu.VMEM((U, E), bf16),
        ],
        flops=2 * 10**9,
    )
    got = exchange(send, BLK)
    piece = kernel(piece_body, sds((8, U + 32, E), bf16), got)
    whole = exchange(piece, BLK)
    first, second = kernel(
        final_body,
        (sds((C, U), f32), sds((U, E), f32)),
        whole,
        grid=(4,),
        in_specs=[pl.BlockSpec((2, U + 32, E), lambda j: (j, 0, 0))],
        out_specs=[
            pl.BlockSpec((512, U), lambda j: (j, 0)),
            pl.BlockSpec((64, E), lambda j: (j, 0)),
        ],
    )
    return (loss_all[0, 0], first, second)


def solution(mesh):
    finer = Mesh(mesh.devices.reshape(4, 2, 2, 4, 2), ALL)
    placed = (P(ALL, None, None), P(ALL), P(ALL), P(None, GRP), P(GRP, None))
    return jax.shard_map(
        step,
        mesh=finer,
        in_specs=placed,
        out_specs=(P(), P(None, GRP), P(GRP, None)),
        check_vma=False,
    )
```

time: 227 us -> 220 us (0.969)
  local copies, waits for them, and re-layouts: 14.9 us -> 3.05 us
  waiting for transfers between devices: 77.6 us -> 69.1 us
  Pallas kernels: 41 us -> 47.8 us
  starting transfers between devices: 46.5 us -> 53.1 us
    unnamed x36 -> x30, local copies, waits for them, and re-layouts: 14.9 us -> 2.96 us
    ppermute x18 -> x21, waiting for transfers between devices: 41.1 us -> 30.2 us  [along_y(): return lax.ppermute(block, 'y', [(i, (i + distance) % 4) for i in range(4)])]
    ppermute x4 -> x7, waiting for transfers between devices: 18.6 us -> 26.5 us  [along_z(): return lax.ppermute(block, ZC, pairs)]
    pallas_call x17, Pallas kernels: 41 us -> 47.8 us  [kernel(): pl.pallas_call(body, out_shape=outs, scratch_shapes=list(scratch), compil...]
    all_to_all x3, waiting for transfers between devices: 15.3 us -> 9.85 us  [exchange(): return lax.all_to_all(array, axis, 0, 0, tiled=True)]
    ppermute x12 -> x21, starting transfers between devices: 3.16 us -> 6.75 us  [swap(): return lax.ppermute(block, 'c', [(0, 1), (1, 0)])]
    ppermute x4 -> x7, starting transfers between devices: 5.06 us -> 8.14 us  [along_z(): return lax.ppermute(block, ZC, pairs)]
    ppermute x18 -> x21, starting transfers between devices: 21.2 us -> 22 us  [along_y(): return lax.ppermute(block, 'y', [(i, (i + distance) % 4) for i in range(4)])]
  transfers between devices with their start and end apart: 37 -> 52, of which waited for: 19 -> 18; matrix products, arithmetic and copies ran while one was open for 0% -> 0% of each run, Pallas kernels for 13% -> 18%
where the time goes in v2:
time: 220 us; the launch traced here: 217 us
  waiting for transfers between devices  69.1 us (31%)
  starting transfers between devices  53.1 us (24%)
  Pallas kernels  47.8 us (22%)
  blocking collectives  43.4 us (20%)
  local copies, waits for them, and re-layouts  3.05 us (1%)
    pallas_call x17, Pallas kernels, kernel(): pl.pallas_call(body, out_shape=outs, scratch_shapes=list(scratch), compil...  47.8 us
    all_to_all x2, blocking collectives, exchange(): return lax.all_to_all(array, axis, 0, 0, tiled=True)  43.4 us
    ppermute x21, waiting for transfers between devices, along_y(): return lax.ppermute(block, 'y', [(i, (i + distance) % 4) for i in range(4)])  30.2 us
    ppermute x7, waiting for transfers between devices, along_z(): return lax.ppermute(block, ZC, pairs)  26.5 us
    ppermute x21, starting transfers between devices, along_y(): return lax.ppermute(block, 'y', [(i, (i + distance) % 4) for i in range(4)])  22 us
    all_to_all x3, starting transfers between devices, exchange(): return lax.all_to_all(array, axis, 0, 0, tiled=True)  16.2 us
    all_to_all x3, waiting for transfers between devices, exchange(): return lax.all_to_all(array, axis, 0, 0, tiled=True)  9.85 us
    ppermute x7, starting transfers between devices, along_z(): return lax.ppermute(block, ZC, pairs)  8.14 us
  transfers between devices with their start and end apart: 52, of which 18 were waited for; matrix products, arithmetic and copies ran while one was open for 0% of the time, Pallas kernels for 18%

profile of v2, /device:TPU:6, one launch (start us, length us, event | category | flops | bytes accessed | tf_op | source)
XLA Modules:
  0.0 217.4 jit_solution(348194896712995049)
XLA Ops:
  0.6 2.0 collective-permute-start.4
  2.6 1.7 collective-permute-start.5
  4.3 13.4 %collective-permute-done.4.refs_1_ = bf16[2048,256]{1,0:T(8,128)(2,1)S(1)} collective-permute-done((bf16[2048,256]{1,0:T(8,128)(2,1)}, bf16[2048,256]{1,0:T(8,128)(2,1)S(1)}, u32[]{:S(2)}, u32[]{:S(2)}) %collective-permute-start.4) | collective-permute-done | bytes 1048608 | tf_op jit(solution)/shard_map/ppermute | solution.py:77
  18.4 2.8 %shard_map.76 = (bf16[64,2048]{1,0:T(8,128)(2,1)S(1)}, bf16[64,2048]{1,0:T(8,128)(2,1)S(1)}) custom-call(bf16[1024,2048]{1,0:T(8,128)(2,1)} %bitcast.12, s32[1,128]{1,0:T(1,128)S(1)} %bitcast.10), custom_call_target="tpu_custom_call" | custom-call | flops 100000000 | tf_op jit(solution)/shard_map/pallas_call | solution.py:54
  21.2 3.1 %collective-permute-start = (bf16[64,2048]{1,0:T(8,128)(2,1)S(1)}, bf16[64,2048]{1,0:T(8,128)(2,1)S(1)}, u32[]{:S(2)}, u32[]{:S(2)}) collective-permute-start(bf16[64,2048]{1,0:T(8,128)(2,1)S(1)} %get-tuple-element.32.a0), channel_id=1, source_target_pairs={{0,6},{2,0},{4,2},{6,4},{1,7},{3,1},{5,3},{7,5},{8,14},{10,8},{12,... | collective-permute-start | bytes 786440 | tf_op jit(solution)/shard_map/ppermute | solution.py:65
  24.3 2.0 collective-permute-start.8
  26.3 4.2 %collective-permute-done.7.refs_5_ = bf16[256,256]{1,0:T(8,128)(2,1)S(1)} collective-permute-done((bf16[256,256]{1,0:T(8,128)(2,1)S(1)}, bf16[256,256]{1,0:T(8,128)(2,1)S(1)}, u32[]{:S(2)}, u32[]{:S(2)}) %collective-permute-start.7) | collective-permute-done | bytes 131104 | tf_op jit(solution)/shard_map/ppermute | solution.py:77
  31.2 1.3 collective-permute-start.2
  32.6 4.3 %collective-permute-done.1.b1 = bf16[64,2048]{1,0:T(8,128)(2,1)S(1)} collective-permute-done((bf16[64,2048]{1,0:T(8,128)(2,1)S(1)}, bf16[64,2048]{1,0:T(8,128)(2,1)S(1)}, u32[]{:S(2)}, u32[]{:S(2)}) %collective-permute-start.1) | collective-permute-done | bytes 262176 | tf_op jit(solution)/shard_map/ppermute | solution.py:65
  36.9 4.6 %collective-permute-done.2.a3 = bf16[64,2048]{1,0:T(8,128)(2,1)S(1)} collective-permute-done((bf16[64,2048]{1,0:T(8,128)(2,1)S(1)}, bf16[64,2048]{1,0:T(8,128)(2,1)S(1)}, u32[]{:S(2)}, u32[]{:S(2)}) %collective-permute-start.2) | collective-permute-done | bytes 262176 | tf_op jit(solution)/shard_map/ppermute | solution.py:65
  41.7 5.3 %collective-permute-done.3.b3 = bf16[64,2048]{1,0:T(8,128)(2,1)S(1)} collective-permute-done((bf16[64,2048]{1,0:T(8,128)(2,1)S(1)}, bf16[64,2048]{1,0:T(8,128)(2,1)S(1)}, u32[]{:S(2)}, u32[]{:S(2)}) %collective-permute-start.3) | collective-permute-done | bytes 262176 | tf_op jit(solution)/shard_map/ppermute | solution.py:65
  47.0 3.9 %shard_map.77 = (bf16[384,2048]{1,0:T(8,128)(2,1)}, bf16[256,2048]{1,0:T(8,128)(2,1)}, f32[128,256]{1,0:T(8,128)S(1)}, f32[128,256]{1,0:T(8,128)S(1)}, f32[128,256]{1,0:T(8,128)S(1)}) custom-call(bf16[64,2048]{1,0:T(8,128)(2,1)S(1)} %get-tuple-element.32.a0, bf16[64,2048]{1,0:T(8,128)(2,1)S(1)} %get-tuple-element.33.b0, ...), custom_call_target="tpu_custom_call" | custom-call | flops 2000000000 | tf_op jit(solution)/shard_map/pallas_call | solution.py:54
  50.9 2.0 collective-permute-start.22
  52.9 1.6 collective-permute-done.11.b2
  54.6 1.8 shard_map.78
  56.5 3.2 %collective-permute-start.24 = (f32[128,256]{1,0:T(8,128)S(1)}, f32[128,256]{1,0:T(8,128)S(1)}, u32[]{:S(2)}, u32[]{:S(2)}) collective-permute-start(f32[128,256]{1,0:T(8,128)S(1)} %get-tuple-element.46), channel_id=1, source_target_pairs={{0,6},{2,0},{4,2},{6,4},{1,7},{3,1},{5,3},{7,5},{8,14},{10,8},{12,... | collective-permute-start | bytes 393224 | tf_op jit(solution)/shard_map/ppermute | solution.py:65
  59.7 3.2 %collective-permute-done.23.p2 = f32[128,256]{1,0:T(8,128)S(1)} collective-permute-done((f32[128,256]{1,0:T(8,128)S(1)}, f32[128,256]{1,0:T(8,128)S(1)}, u32[]{:S(2)}, u32[]{:S(2)}) %collective-permute-start.23) | collective-permute-done | bytes 131104 | tf_op jit(solution)/shard_map/ppermute | solution.py:65
  62.9 1.2 shard_map.81
  64.1 5.0 %all-to-all-start = ((bf16[16,128,256]{2,1,0:T(8,128)(2,1)}), bf16[16,128,256]{2,1,0:T(8,128)(2,1)S(1)}, u32[]{:S(2)}, u32[]{:S(2)}) async-start(bf16[16,128,256]{2,1,0:T(8,128)(2,1)} %get-tuple-element.49), calls=%async_computation | async-start | bytes 2097152 | tf_op jit(solution)/shard_map/all_to_all | solution.py:81
  69.1 1.5 collective-permute-start.16
  70.5 1.3 collective-permute-done.25.mate
  71.9 2.8 %collective-permute-start.26 = (bf16[256,384]{1,0:T(8,128)(2,1)S(1)}, bf16[256,384]{1,0:T(8,128)(2,1)S(1)}, u32[]{:S(2)}, u32[]{:S(2)}) collective-permute-start(bf16[256,384]{1,0:T(8,128)(2,1)S(1)} %shard_map.84.pay0), channel_id=1, source_target_pairs={{0,6},{2,0},{4,2},{6,4},{1,7},{3,1},{5,3},{7,5},{8,14},{10,8},{12,... | collective-permute-start | bytes 589832 | tf_op jit(solution)/shard_map/ppermute | solution.py:65
  75.9 1.1 shard_map.82.given.where
  77.0 6.4 %collective-permute-done.26.pay1 = bf16[256,384]{1,0:T(8,128)(2,1)S(1)} collective-permute-done((bf16[256,384]{1,0:T(8,128)(2,1)S(1)}, bf16[256,384]{1,0:T(8,128)(2,1)S(1)}, u32[]{:S(2)}, u32[]{:S(2)}) %collective-permute-start.26) | collective-permute-done | bytes 196640 | tf_op jit(solution)/shard_map/ppermute | solution.py:65
  84.0 3.0 %collective-permute-done.28.pay3 = bf16[256,384]{1,0:T(8,128)(2,1)S(1)} collective-permute-done((bf16[256,384]{1,0:T(8,128)(2,1)S(1)}, bf16[256,384]{1,0:T(8,128)(2,1)S(1)}, u32[]{:S(2)}, u32[]{:S(2)}) %collective-permute-start.28) | collective-permute-done | bytes 196640 | tf_op jit(solution)/shard_map/ppermute | solution.py:65
  87.0 3.7 %shard_map.85 = (f32[8,128]{1,0:T(8,128)S(1)}, f32[16,1,2176]{2,1,0:T(1,128)}, bf16[1024,256]{1,0:T(8,128)(2,1)}, f32[1024,128]{1,0:T(8,128)}) custom-call(s32[5]{0:T(128)S(1)} %shard_map.82.given.where, bf16[256,384]{1,0:T(8,128)(2,1)S(1)} %shard_map.84.pay0, bf16[256,384]{1,0:T(8,128)(2,1)S(1)} %collective-permute-done.26.pay1, ...), custom_call_target="tpu_custom_call" | custom-call | flops 1000000000 | tf_op jit(solution)/shard_map/pallas_call | solution.py:54
  90.7 6.9 %all-to-all-start.1 = ((f32[16,1,2176]{2,1,0:T(1,128)}), f32[16,1,2176]{2,1,0:T(1,128)S(1)}, u32[]{:S(2)}, u32[]{:S(2)}) async-start(f32[16,1,2176]{2,1,0:T(1,128)} %get-tuple-element.53), calls=%async_computation.1 | async-start | bytes 278528 | tf_op jit(solution)/shard_map/all_to_all | solution.py:81
  97.7 1.2 collective-permute-done.29.mate
  100.9 1.1 shard_map.83.where
  102.4 1.5 collective-permute-start.14
  104.7 1.5 collective-permute-start.17
  106.2 6.9 %shard_map.87 = (f32[4,128,256]{2,1,0:T(8,128)S(1)}, f32[4,128,256]{2,1,0:T(8,128)S(1)}, f32[1,128]{1,0:T(1,128)}) custom-call(s32[5]{0:T(128)S(1)} %shard_map.83.where, bf16[1024,256]{1,0:T(8,128)(2,1)} %get-tuple-element.50.tile, f32[1024,128]{1,0:T(8,128)} %get-tuple-element.51.who, bf16[16,128,256]{2,1,0:T(8,128)(2,1)} %copy-done.3, ...), custom_call_target="tpu_custom_call" | custom-call | flops 3000000000 | tf_op jit(solution)/shard_map/pallas_call | solution.py:54
  113.5 1.5 collective-permute-start.15
  115.0 6.1 %collective-permute-done.15.refs_1_ = bf16[64,2048]{1,0:T(8,128)(2,1)S(1)} collective-permute-done((bf16[64,2048]{1,0:T(8,128)(2,1)S(1)}, bf16[64,2048]{1,0:T(8,128)(2,1)S(1)}, u32[]{:S(2)}, u32[]{:S(2)}) %collective-permute-start.15) | collective-permute-done | bytes 262176 | tf_op jit(solution)/shard_map/ppermute | solution.py:77
  122.6 4.3 %all-to-all-start.2 = ((f32[4,128,256]{2,1,0:T(8,128)}), f32[4,128,256]{2,1,0:T(8,128)S(1)}, u32[]{:S(2)}, u32[]{:S(2)}) async-start(f32[4,128,256]{2,1,0:T(8,128)} %shard_map.88), calls=%async_computation.2 | async-start | bytes 1048576 | tf_op jit(solution)/shard_map/all_to_all | solution.py:81
  127.1 9.8 %all-to-all-done.2.got = f32[4,128,256]{2,1,0:T(8,128)S(1)} async-done(((f32[4,128,256]{2,1,0:T(8,128)}), f32[4,128,256]{2,1,0:T(8,128)S(1)}, u32[]{:S(2)}, u32[]{:S(2)}) %all-to-all-start.2) | async-done | bytes 524320 | tf_op jit(solution)/shard_map/all_to_all | solution.py:81
  138.5 1.2 collective-permute-start.34
  139.7 1.5 collective-permute-start.35
  141.3 2.7 %collective-permute-done.41.refs_8_ = bf16[144,256]{1,0:T(8,128)(2,1)S(1)} collective-permute-done((bf16[144,256]{1,0:T(8,128)(2,1)S(1)}, bf16[144,256]{1,0:T(8,128)(2,1)S(1)}, u32[]{:S(2)}, u32[]{:S(2)}) %collective-permute-start.41) | collective-permute-done | bytes 73760 | tf_op jit(solution)/shard_map/ppermute | solution.py:77
  144.0 1.2 collective-permute-start.42
  145.2 1.5 collective-permute-start.43
  147.3 7.3 %shard_map.79 = (bf16[256,1024]{1,0:T(8,128)(2,1)}, f32[256,1024]{1,0:T(8,128)}, bf16[1024,2048]{1,0:T(8,128)(2,1)}) custom-call(bf16[384,2048]{1,0:T(8,128)(2,1)} %get-tuple-element.34.refs_0_, bf16[128,2048]{1,0:T(8,128)(2,1)} %get-tuple-element.35.refs_1_, bf16[384,2048]{1,0:T(8,128)(2,1)} %collective-permute-done.12.refs_2_, ...), custom_call_target="tpu_custom_call" | custom-call | flops 2000000000 | tf_op jit(solution)/shard_map/pallas_call | solution.py:54
  155.8 7.4 %shard_map.80 = (bf16[256,1024]{1,0:T(8,128)(2,1)}, f32[256,1024]{1,0:T(8,128)}, bf16[1024,2048]{1,0:T(8,128)(2,1)}) custom-call(bf16[64,2048]{1,0:T(8,128)(2,1)} %copy-done.12, bf16[64,2048]{1,0:T(8,128)(2,1)} %copy-done.13, bf16[256,2048]{1,0:T(8,128)(2,1)} %copy-done.10, bf16[128,2048]{1,0:T(8,128)(2,1)} %collective-permute-done.17.refs_3_, ...), custom_call_target="tpu_custom_call" | custom-call | flops 2000000000 | tf_op jit(solution)/shard_map/pallas_call | solution.py:54
  163.3 1.2 copy-done.2
  165.6 6.2 %shard_map.90 = (bf16[8,288,256]{2,1,0:T(8,128)(2,1)S(1)}, f32[1,128]{1,0:T(1,128)}) custom-call(bf16[1024,2048]{1,0:T(8,128)(2,1)} %get-tuple-element.36.pool_a, bf16[1024,2048]{1,0:T(8,128)(2,1)} %get-tuple-element.38.pool_b, bf16[256,1024]{1,0:T(8,128)(2,1)S(1)} %copy-done.5, bf16[256,1024]{1,0:T(8,128)(2,1)S(1)} %copy-done.6, f32[256,1024]{1,0:T(8,128)S(1)} %copy-done.1, ...), custom_call_target="tpu_custom_call" | custom-call | flops 2000000000 | tf_op jit(solution)/shard_map/pallas_call | solution.py:54
  171.8 22.9 %all_to_all.25.got = bf16[8,288,256]{2,1,0:T(8,128)(2,1)S(1)} all-to-all(bf16[8,288,256]{2,1,0:T(8,128)(2,1)S(1)} %get-tuple-element.58), channel_id=1, replica_groups=mesh['x'=4,'zh'=2,'zl'=2,'y'=4,'c'=2] {'x','zh'}, dimensions={0} | all-to-all | bytes 2359296 | tf_op jit(solution)/shard_map/all_to_all | solution.py:81
  194.9 20.6 %all_to_all.26.got = bf16[8,288,256]{2,1,0:T(8,128)(2,1)S(1)} all-to-all(bf16[8,288,256]{2,1,0:T(8,128)(2,1)S(1)} %shard_map.91), channel_id=1, replica_groups=mesh['x'=4,'zh'=2,'zl'=2,'y'=4,'c'=2] {'x','zh'}, dimensions={0} | all-to-all | bytes 2359296 | tf_op jit(solution)/shard_map/all_to_all | solution.py:81
  215.5 1.9 shard_map.92
  (106 shorter events, 13.7 us)
Async XLA Ops:
  0.6 17.1 %collective-permute-start.4 = (bf16[2048,256]{1,0:T(8,128)(2,1)}, bf16[2048,256]{1,0:T(8,128)(2,1)S(1)}, u32[]{:S(2)}, u32[]{:S(2)}) collective-permute-start(bf16[2048,256]{1,0:T(8,128)(2,1)} %refs_8_.1), channel_id=1, source_target_pairs={{0,8},{1,25},{8,16},{9,1},{16,24},{17,9},{24,0},{25,17},{2,10},{3,... | collective-permute-start | bytes 3145736 | tf_op jit(solution)/shard_map/ppermute | solution.py:77
  2.6 44.4 %collective-permute-start.5 = (bf16[2048,256]{1,0:T(8,128)(2,1)}, bf16[2048,256]{1,0:T(8,128)(2,1)S(1)}, u32[]{:S(2)}, u32[]{:S(2)}) collective-permute-start(bf16[2048,256]{1,0:T(8,128)(2,1)} %refs_8_.1), channel_id=1, source_target_pairs={{0,1},{1,0},{2,3},{3,2},{4,5},{5,4},{6,7},{7,6},{8,9},{9,8},{10,11... | collective-permute-start | bytes 3145736 | tf_op jit(solution)/shard_map/ppermute | solution.py:69
  17.7 29.2 %collective-permute-start.6 = (bf16[2048,256]{1,0:T(8,128)(2,1)S(1)}, bf16[2048,256]{1,0:T(8,128)(2,1)S(1)}, u32[]{:S(2)}, u32[]{:S(2)}) collective-permute-start(bf16[2048,256]{1,0:T(8,128)(2,1)S(1)} %collective-permute-done.4.refs_1_), channel_id=1, source_target_pairs={{0,1},{1,0},{2,3},{3,2},{4,5},{5,4},{6,7},{7,6},{8,9},{9,8},{10,11... | collective-permute-start | bytes 3145736 | tf_op jit(solution)/shard_map/ppermute | solution.py:69
  21.2 11.3 %collective-permute-start = (bf16[64,2048]{1,0:T(8,128)(2,1)S(1)}, bf16[64,2048]{1,0:T(8,128)(2,1)S(1)}, u32[]{:S(2)}, u32[]{:S(2)}) collective-permute-start(bf16[64,2048]{1,0:T(8,128)(2,1)S(1)} %get-tuple-element.32.a0), channel_id=1, source_target_pairs={{0,6},{2,0},{4,2},{6,4},{1,7},{3,1},{5,3},{7,5},{8,14},{10,8},{12,... | collective-permute-start | bytes 786440 | tf_op jit(solution)/shard_map/ppermute | solution.py:65
  24.3 6.2 %collective-permute-start.7 = (bf16[256,256]{1,0:T(8,128)(2,1)S(1)}, bf16[256,256]{1,0:T(8,128)(2,1)S(1)}, u32[]{:S(2)}, u32[]{:S(2)}) collective-permute-start(bf16[256,256]{1,0:T(8,128)(2,1)S(1)} %copy-done.4), channel_id=1, source_target_pairs={{0,8},{1,25},{8,16},{9,1},{16,24},{17,9},{24,0},{25,17},{2,10},{3,... | collective-permute-start | bytes 393224 | tf_op jit(solution)/shard_map/ppermute | solution.py:77
  24.3 6.9 %collective-permute-start.8 = (bf16[256,256]{1,0:T(8,128)(2,1)S(1)}, bf16[256,256]{1,0:T(8,128)(2,1)S(1)}, u32[]{:S(2)}, u32[]{:S(2)}) collective-permute-start(bf16[256,256]{1,0:T(8,128)(2,1)S(1)} %copy-done.4), channel_id=1, source_target_pairs={{0,1},{1,0},{2,3},{3,2},{4,5},{5,4},{6,7},{7,6},{8,9},{9,8},{10,11... | collective-permute-start | bytes 393224 | tf_op jit(solution)/shard_map/ppermute | solution.py:69
  30.5 6.4 %collective-permute-start.1 = (bf16[64,2048]{1,0:T(8,128)(2,1)S(1)}, bf16[64,2048]{1,0:T(8,128)(2,1)S(1)}, u32[]{:S(2)}, u32[]{:S(2)}) collective-permute-start(bf16[64,2048]{1,0:T(8,128)(2,1)S(1)} %get-tuple-element.33.b0), channel_id=1, source_target_pairs={{0,6},{2,0},{4,2},{6,4},{1,7},{3,1},{5,3},{7,5},{8,14},{10,8},{12,... | collective-permute-start | bytes 786440 | tf_op jit(solution)/shard_map/ppermute | solution.py:65
  31.2 10.2 %collective-permute-start.2 = (bf16[64,2048]{1,0:T(8,128)(2,1)S(1)}, bf16[64,2048]{1,0:T(8,128)(2,1)S(1)}, u32[]{:S(2)}, u32[]{:S(2)}) collective-permute-start(bf16[64,2048]{1,0:T(8,128)(2,1)S(1)} %get-tuple-element.32.a0), channel_id=1, source_target_pairs={{0,2},{2,4},{4,6},{6,0},{1,3},{3,5},{5,7},{7,1},{8,10},{10,12},{12... | collective-permute-start | bytes 786440 | tf_op jit(solution)/shard_map/ppermute | solution.py:65
  32.5 14.4 %collective-permute-start.3 = (bf16[64,2048]{1,0:T(8,128)(2,1)S(1)}, bf16[64,2048]{1,0:T(8,128)(2,1)S(1)}, u32[]{:S(2)}, u32[]{:S(2)}) collective-permute-start(bf16[64,2048]{1,0:T(8,128)(2,1)S(1)} %get-tuple-element.33.b0), channel_id=1, source_target_pairs={{0,2},{2,4},{4,6},{6,0},{1,3},{3,5},{5,7},{7,1},{8,10},{10,12},{12... | collective-permute-start | bytes 786440 | tf_op jit(solution)/shard_map/ppermute | solution.py:65
  36.9 10.1 %collective-permute-start.9 = (bf16[256,256]{1,0:T(8,128)(2,1)S(1)}, bf16[256,256]{1,0:T(8,128)(2,1)S(1)}, u32[]{:S(2)}, u32[]{:S(2)}) collective-permute-start(bf16[256,256]{1,0:T(8,128)(2,1)S(1)} %collective-permute-done.7.refs_5_), channel_id=1, source_target_pairs={{0,1},{1,0},{2,3},{3,2},{4,5},{5,4},{6,7},{7,6},{8,9},{9,8},{10,11... | collective-permute-start | bytes 393224 | tf_op jit(solution)/shard_map/ppermute | solution.py:69
  41.5 11.5 %collective-permute-start.10 = (bf16[64,2048]{1,0:T(8,128)(2,1)S(1)}, bf16[64,2048]{1,0:T(8,128)(2,1)S(1)}, u32[]{:S(2)}, u32[]{:S(2)}) collective-permute-start(bf16[64,2048]{1,0:T(8,128)(2,1)S(1)} %collective-permute-done.2.a3), channel_id=1, source_target_pairs={{0,2},{2,4},{4,6},{6,0},{1,3},{3,5},{5,7},{7,1},{8,10},{10,12},{12... | collective-permute-start | bytes 786440 | tf_op jit(solution)/shard_map/ppermute | solution.py:65
  47.0 7.6 %collective-permute-start.11 = (bf16[64,2048]{1,0:T(8,128)(2,1)S(1)}, bf16[64,2048]{1,0:T(8,128)(2,1)S(1)}, u32[]{:S(2)}, u32[]{:S(2)}) collective-permute-start(bf16[64,2048]{1,0:T(8,128)(2,1)S(1)} %collective-permute-done.1.b1), channel_id=1, source_target_pairs={{0,6},{2,0},{4,2},{6,4},{1,7},{3,1},{5,3},{7,5},{8,14},{10,8},{12,... | collective-permute-start | bytes 786440 | tf_op jit(solution)/shard_map/ppermute | solution.py:65
  50.9 8.8 %collective-permute-start.22 = (f32[128,256]{1,0:T(8,128)S(1)}, f32[128,256]{1,0:T(8,128)S(1)}, u32[]{:S(2)}, u32[]{:S(2)}) collective-permute-start(f32[128,256]{1,0:T(8,128)S(1)} %get-tuple-element.44), channel_id=1, source_target_pairs={{0,2},{2,4},{4,6},{6,0},{1,3},{3,5},{5,7},{7,1},{8,10},{10,12},{12... | collective-permute-start | bytes 393224 | tf_op jit(solution)/shard_map/ppermute | solution.py:65
  56.4 6.5 %collective-permute-start.23 = (f32[128,256]{1,0:T(8,128)S(1)}, f32[128,256]{1,0:T(8,128)S(1)}, u32[]{:S(2)}, u32[]{:S(2)}) collective-permute-start(f32[128,256]{1,0:T(8,128)S(1)} %get-tuple-element.45), channel_id=1, source_target_pairs={{0,4},{2,6},{4,0},{6,2},{1,5},{3,7},{5,1},{7,3},{8,12},{10,14},{12... | collective-permute-start | bytes 393224 | tf_op jit(solution)/shard_map/ppermute | solution.py:65
  56.5 6.4 %collective-permute-start.24 = (f32[128,256]{1,0:T(8,128)S(1)}, f32[128,256]{1,0:T(8,128)S(1)}, u32[]{:S(2)}, u32[]{:S(2)}) collective-permute-start(f32[128,256]{1,0:T(8,128)S(1)} %get-tuple-element.46), channel_id=1, source_target_pairs={{0,6},{2,0},{4,2},{6,4},{1,7},{3,1},{5,3},{7,5},{8,14},{10,8},{12,... | collective-permute-start | bytes 393224 | tf_op jit(solution)/shard_map/ppermute | solution.py:65
  64.1 22.9 %all-to-all-start = ((bf16[16,128,256]{2,1,0:T(8,128)(2,1)}), bf16[16,128,256]{2,1,0:T(8,128)(2,1)S(1)}, u32[]{:S(2)}, u32[]{:S(2)}) async-start(bf16[16,128,256]{2,1,0:T(8,128)(2,1)} %get-tuple-element.49), calls=%async_computation | async-start | bytes 2097152 | tf_op jit(solution)/shard_map/all_to_all | solution.py:81
  69.1 43.9 %collective-permute-start.16 = (bf16[256,2048]{1,0:T(8,128)(2,1)}, bf16[256,2048]{1,0:T(8,128)(2,1)S(1)}, u32[]{:S(2)}, u32[]{:S(2)}) collective-permute-start(bf16[256,2048]{1,0:T(8,128)(2,1)} %get-tuple-element.37), channel_id=1, source_target_pairs={{0,8},{1,25},{8,16},{9,1},{16,24},{17,9},{24,0},{25,17},{2,10},{3,... | collective-permute-start | bytes 3145736 | tf_op jit(solution)/shard_map/ppermute | solution.py:77
  71.9 11.6 %collective-permute-start.26 = (bf16[256,384]{1,0:T(8,128)(2,1)S(1)}, bf16[256,384]{1,0:T(8,128)(2,1)S(1)}, u32[]{:S(2)}, u32[]{:S(2)}) collective-permute-start(bf16[256,384]{1,0:T(8,128)(2,1)S(1)} %shard_map.84.pay0), channel_id=1, source_target_pairs={{0,6},{2,0},{4,2},{6,4},{1,7},{3,1},{5,3},{7,5},{8,14},{10,8},{12,... | collective-permute-start | bytes 589832 | tf_op jit(solution)/shard_map/ppermute | solution.py:65
  74.7 9.3 %collective-permute-start.27 = (bf16[256,384]{1,0:T(8,128)(2,1)S(1)}, bf16[256,384]{1,0:T(8,128)(2,1)S(1)}, u32[]{:S(2)}, u32[]{:S(2)}) collective-permute-start(bf16[256,384]{1,0:T(8,128)(2,1)S(1)} %shard_map.84.pay0), channel_id=1, source_target_pairs={{0,4},{2,6},{4,0},{6,2},{1,5},{3,7},{5,1},{7,3},{8,12},{10,14},{12... | collective-permute-start | bytes 589832 | tf_op jit(solution)/shard_map/ppermute | solution.py:65
  75.1 11.8 %collective-permute-start.28 = (bf16[256,384]{1,0:T(8,128)(2,1)S(1)}, bf16[256,384]{1,0:T(8,128)(2,1)S(1)}, u32[]{:S(2)}, u32[]{:S(2)}) collective-permute-start(bf16[256,384]{1,0:T(8,128)(2,1)S(1)} %shard_map.84.pay0), channel_id=1, source_target_pairs={{0,2},{2,4},{4,6},{6,0},{1,3},{3,5},{5,7},{7,1},{8,10},{10,12},{12... | collective-permute-start | bytes 589832 | tf_op jit(solution)/shard_map/ppermute | solution.py:65
  75.8 65.4 %collective-permute-start.12 = (bf16[384,2048]{1,0:T(8,128)(2,1)}, bf16[384,2048]{1,0:T(8,128)(2,1)}, u32[]{:S(2)}, u32[]{:S(2)}) collective-permute-start(bf16[384,2048]{1,0:T(8,128)(2,1)} %get-tuple-element.34.refs_0_), channel_id=1, source_target_pairs={{0,1},{1,0},{2,3},{3,2},{4,5},{5,4},{6,7},{7,6},{8,9},{9,8},{10,11... | collective-permute-start | bytes 4718600 | tf_op jit(solution)/shard_map/ppermute | solution.py:69
  90.7 15.4 %all-to-all-start.1 = ((f32[16,1,2176]{2,1,0:T(1,128)}), f32[16,1,2176]{2,1,0:T(1,128)S(1)}, u32[]{:S(2)}, u32[]{:S(2)}) async-start(f32[16,1,2176]{2,1,0:T(1,128)} %get-tuple-element.53), calls=%async_computation.1 | async-start | bytes 278528 | tf_op jit(solution)/shard_map/all_to_all | solution.py:81
  100.0 6.1 %collective-permute-start.32 = (f32[8,128]{1,0:T(8,128)S(1)}, f32[8,128]{1,0:T(8,128)S(1)}, u32[]{:S(2)}, u32[]{:S(2)}) collective-permute-start(f32[8,128]{1,0:T(8,128)S(1)} %shard_map.86.sum0), channel_id=1, source_target_pairs={{0,2},{2,4},{4,6},{6,0},{1,3},{3,5},{5,7},{7,1},{8,10},{10,12},{12... | collective-permute-start | bytes 12296 | tf_op jit(solution)/shard_map/ppermute | solution.py:65
  102.4 11.1 %collective-permute-start.14 = (bf16[64,2048]{1,0:T(8,128)(2,1)S(1)}, bf16[64,2048]{1,0:T(8,128)(2,1)S(1)}, u32[]{:S(2)}, u32[]{:S(2)}) collective-permute-start(bf16[64,2048]{1,0:T(8,128)(2,1)S(1)} %get-tuple-element.32.a0), channel_id=1, source_target_pairs={{0,8},{1,25},{8,16},{9,1},{16,24},{17,9},{24,0},{25,17},{2,10},{3,... | collective-permute-start | bytes 786440 | tf_op jit(solution)/shard_map/ppermute | solution.py:77
  104.7 16.4 %collective-permute-start.17 = (bf16[128,2048]{1,0:T(8,128)(2,1)}, bf16[128,2048]{1,0:T(8,128)(2,1)}, u32[]{:S(2)}, u32[]{:S(2)}) collective-permute-start(bf16[128,2048]{1,0:T(8,128)(2,1)} %get-tuple-element.35.refs_1_), channel_id=1, source_target_pairs={{0,8},{1,25},{8,16},{9,1},{16,24},{17,9},{24,0},{25,17},{2,10},{3,... | collective-permute-start | bytes 1572872 | tf_op jit(solution)/shard_map/ppermute | solution.py:77
  113.0 8.6 %collective-permute-start.33 = (f32[4,128,256]{2,1,0:T(8,128)S(1)}, f32[4,128,256]{2,1,0:T(8,128)S(1)}, u32[]{:S(2)}, u32[]{:S(2)}) collective-permute-start(f32[4,128,256]{2,1,0:T(8,128)S(1)} %get-tuple-element.55), channel_id=1, source_target_pairs={{0,1},{1,0},{2,3},{3,2},{4,5},{5,4},{6,7},{7,6},{8,9},{9,8},{10,11... | collective-permute-start | bytes 1572872 | tf_op jit(solution)/shard_map/ppermute | solution.py:69
  113.0 28.1 %collective-permute-start.20 = (bf16[256,2048]{1,0:T(8,128)(2,1)S(1)}, bf16[256,2048]{1,0:T(8,128)(2,1)S(1)}, u32[]{:S(2)}, u32[]{:S(2)}) collective-permute-start(bf16[256,2048]{1,0:T(8,128)(2,1)S(1)} %collective-permute-done.16.refs_2_), channel_id=1, source_target_pairs={{0,1},{1,0},{2,3},{3,2},{4,5},{5,4},{6,7},{7,6},{8,9},{9,8},{10,11... | collective-permute-start | bytes 3145736 | tf_op jit(solution)/shard_map/ppermute | solution.py:69
  113.5 7.6 %collective-permute-start.15 = (bf16[64,2048]{1,0:T(8,128)(2,1)S(1)}, bf16[64,2048]{1,0:T(8,128)(2,1)S(1)}, u32[]{:S(2)}, u32[]{:S(2)}) collective-permute-start(bf16[64,2048]{1,0:T(8,128)(2,1)S(1)} %get-tuple-element.33.b0), channel_id=1, source_target_pairs={{0,8},{1,25},{8,16},{9,1},{16,24},{17,9},{24,0},{25,17},{2,10},{3,... | collective-permute-start | bytes 786440 | tf_op jit(solution)/shard_map/ppermute | solution.py:77
  121.1 5.8 %collective-permute-start.18 = (bf16[64,2048]{1,0:T(8,128)(2,1)S(1)}, bf16[64,2048]{1,0:T(8,128)(2,1)S(1)}, u32[]{:S(2)}, u32[]{:S(2)}) collective-permute-start(bf16[64,2048]{1,0:T(8,128)(2,1)S(1)} %collective-permute-done.14.refs_0_), channel_id=1, source_target_pairs={{0,1},{1,0},{2,3},{3,2},{4,5},{5,4},{6,7},{7,6},{8,9},{9,8},{10,11... | collective-permute-start | bytes 786440 | tf_op jit(solution)/shard_map/ppermute | solution.py:69
  121.1 17.3 %collective-permute-start.13 = (bf16[128,2048]{1,0:T(8,128)(2,1)}, bf16[128,2048]{1,0:T(8,128)(2,1)}, u32[]{:S(2)}, u32[]{:S(2)}) collective-permute-start(bf16[128,2048]{1,0:T(8,128)(2,1)} %get-tuple-element.35.refs_1_), channel_id=1, source_target_pairs={{0,1},{1,0},{2,3},{3,2},{4,5},{5,4},{6,7},{7,6},{8,9},{9,8},{10,11... | collective-permute-start | bytes 1572872 | tf_op jit(solution)/shard_map/ppermute | solution.py:69
  121.6 18.1 %collective-permute-start.21 = (bf16[128,2048]{1,0:T(8,128)(2,1)}, bf16[128,2048]{1,0:T(8,128)(2,1)}, u32[]{:S(2)}, u32[]{:S(2)}) collective-permute-start(bf16[128,2048]{1,0:T(8,128)(2,1)} %collective-permute-done.17.refs_3_), channel_id=1, source_target_pairs={{0,1},{1,0},{2,3},{3,2},{4,5},{5,4},{6,7},{7,6},{8,9},{9,8},{10,11... | collective-permute-start | bytes 1572872 | tf_op jit(solution)/shard_map/ppermute | solution.py:69
  122.6 14.3 %all-to-all-start.2 = ((f32[4,128,256]{2,1,0:T(8,128)}), f32[4,128,256]{2,1,0:T(8,128)S(1)}, u32[]{:S(2)}, u32[]{:S(2)}) async-start(f32[4,128,256]{2,1,0:T(8,128)} %shard_map.88), calls=%async_computation.2 | async-start | bytes 1048576 | tf_op jit(solution)/shard_map/all_to_all | solution.py:81
  126.9 11.2 %collective-permute-start.19 = (bf16[64,2048]{1,0:T(8,128)(2,1)S(1)}, bf16[64,2048]{1,0:T(8,128)(2,1)}, u32[]{:S(2)}, u32[]{:S(2)}) collective-permute-start(bf16[64,2048]{1,0:T(8,128)(2,1)S(1)} %collective-permute-done.15.refs_1_), channel_id=1, source_target_pairs={{0,1},{1,0},{2,3},{3,2},{4,5},{5,4},{6,7},{7,6},{8,9},{9,8},{10,11... | collective-permute-start | bytes 786440 | tf_op jit(solution)/shard_map/ppermute | solution.py:69
  138.1 5.9 %collective-permute-start.41 = (bf16[144,256]{1,0:T(8,128)(2,1)S(1)}, bf16[144,256]{1,0:T(8,128)(2,1)S(1)}, u32[]{:S(2)}, u32[]{:S(2)}) collective-permute-start(bf16[144,256]{1,0:T(8,128)(2,1)S(1)} %shard_map.89.refs_0_), channel_id=1, source_target_pairs={{0,8},{1,25},{8,16},{9,1},{16,24},{17,9},{24,0},{25,17},{2,10},{3,... | collective-permute-start | bytes 221192 | tf_op jit(solution)/shard_map/ppermute | solution.py:77
  138.5 6.7 %collective-permute-start.34 = (bf16[144,256]{1,0:T(8,128)(2,1)S(1)}, bf16[144,256]{1,0:T(8,128)(2,1)S(1)}, u32[]{:S(2)}, u32[]{:S(2)}) collective-permute-start(bf16[144,256]{1,0:T(8,128)(2,1)S(1)} %shard_map.89.refs_0_), channel_id=1, source_target_pairs={{0,6},{2,0},{4,2},{6,4},{1,7},{3,1},{5,3},{7,5},{8,14},{10,8},{12,... | collective-permute-start | bytes 221192 | tf_op jit(solution)/shard_map/ppermute | solution.py:65
  139.7 6.9 %collective-permute-start.35 = (bf16[144,256]{1,0:T(8,128)(2,1)S(1)}, bf16[144,256]{1,0:T(8,128)(2,1)S(1)}, u32[]{:S(2)}, u32[]{:S(2)}) collective-permute-start(bf16[144,256]{1,0:T(8,128)(2,1)S(1)} %shard_map.89.refs_0_), channel_id=1, source_target_pairs={{0,4},{2,6},{4,0},{6,2},{1,5},{3,7},{5,1},{7,3},{8,12},{10,14},{12... | collective-permute-start | bytes 221192 | tf_op jit(solution)/shard_map/ppermute | solution.py:65
  141.2 5.6 %collective-permute-start.36 = (bf16[144,256]{1,0:T(8,128)(2,1)S(1)}, bf16[144,256]{1,0:T(8,128)(2,1)S(1)}, u32[]{:S(2)}, u32[]{:S(2)}) collective-permute-start(bf16[144,256]{1,0:T(8,128)(2,1)S(1)} %shard_map.89.refs_0_), channel_id=1, source_target_pairs={{0,2},{2,4},{4,6},{6,0},{1,3},{3,5},{5,7},{7,1},{8,10},{10,12},{12... | collective-permute-start | bytes 221192 | tf_op jit(solution)/shard_map/ppermute | solution.py:65
  141.2 5.6 %collective-permute-start.37 = (bf16[144,256]{1,0:T(8,128)(2,1)S(1)}, bf16[144,256]{1,0:T(8,128)(2,1)S(1)}, u32[]{:S(2)}, u32[]{:S(2)}) collective-permute-start(bf16[144,256]{1,0:T(8,128)(2,1)S(1)} %shard_map.89.refs_0_), channel_id=1, source_target_pairs={{0,1},{1,0},{2,3},{3,2},{4,5},{5,4},{6,7},{7,6},{8,9},{9,8},{10,11... | collective-permute-start | bytes 221192 | tf_op jit(solution)/shard_map/ppermute | solution.py:69
  144.0 11.2 %collective-permute-start.42 = (bf16[144,256]{1,0:T(8,128)(2,1)S(1)}, bf16[144,256]{1,0:T(8,128)(2,1)S(1)}, u32[]{:S(2)}, u32[]{:S(2)}) collective-permute-start(bf16[144,256]{1,0:T(8,128)(2,1)S(1)} %collective-permute-done.41.refs_8_), channel_id=1, source_target_pairs={{0,6},{2,0},{4,2},{6,4},{1,7},{3,1},{5,3},{7,5},{8,14},{10,8},{12,... | collective-permute-start | bytes 221192 | tf_op jit(solution)/shard_map/ppermute | solution.py:65
  145.2 10.1 %collective-permute-start.43 = (bf16[144,256]{1,0:T(8,128)(2,1)S(1)}, bf16[144,256]{1,0:T(8,128)(2,1)S(1)}, u32[]{:S(2)}, u32[]{:S(2)}) collective-permute-start(bf16[144,256]{1,0:T(8,128)(2,1)S(1)} %collective-permute-done.41.refs_8_), channel_id=1, source_target_pairs={{0,4},{2,6},{4,0},{6,2},{1,5},{3,7},{5,1},{7,3},{8,12},{10,14},{12... | collective-permute-start | bytes 221192 | tf_op jit(solution)/shard_map/ppermute | solution.py:65
  146.6 9.1 %collective-permute-start.44 = (bf16[144,256]{1,0:T(8,128)(2,1)S(1)}, bf16[144,256]{1,0:T(8,128)(2,1)S(1)}, u32[]{:S(2)}, u32[]{:S(2)}) collective-permute-start(bf16[144,256]{1,0:T(8,128)(2,1)S(1)} %collective-permute-done.41.refs_8_), channel_id=1, source_target_pairs={{0,2},{2,4},{4,6},{6,0},{1,3},{3,5},{5,7},{7,1},{8,10},{10,12},{12... | collective-permute-start | bytes 221192 | tf_op jit(solution)/shard_map/ppermute | solution.py:65
  146.7 7.9 %collective-permute-start.38 = (bf16[144,256]{1,0:T(8,128)(2,1)S(1)}, bf16[144,256]{1,0:T(8,128)(2,1)S(1)}, u32[]{:S(2)}, u32[]{:S(2)}) collective-permute-start(bf16[144,256]{1,0:T(8,128)(2,1)S(1)} %collective-permute-done.34.refs_1_), channel_id=1, source_target_pairs={{0,1},{1,0},{2,3},{3,2},{4,5},{5,4},{6,7},{7,6},{8,9},{9,8},{10,11... | collective-permute-start | bytes 221192 | tf_op jit(solution)/shard_map/ppermute | solution.py:69
  146.8 8.0 %collective-permute-start.39 = (bf16[144,256]{1,0:T(8,128)(2,1)S(1)}, bf16[144,256]{1,0:T(8,128)(2,1)S(1)}, u32[]{:S(2)}, u32[]{:S(2)}) collective-permute-start(bf16[144,256]{1,0:T(8,128)(2,1)S(1)} %collective-permute-done.35.refs_2_), channel_id=1, source_target_pairs={{0,1},{1,0},{2,3},{3,2},{4,5},{5,4},{6,7},{7,6},{8,9},{9,8},{10,11... | collective-permute-start | bytes 221192 | tf_op jit(solution)/shard_map/ppermute | solution.py:69
  154.6 8.6 %collective-permute-start.45 = (bf16[144,256]{1,0:T(8,128)(2,1)S(1)}, bf16[144,256]{1,0:T(8,128)(2,1)S(1)}, u32[]{:S(2)}, u32[]{:S(2)}) collective-permute-start(bf16[144,256]{1,0:T(8,128)(2,1)S(1)} %collective-permute-done.41.refs_8_), channel_id=1, source_target_pairs={{0,1},{1,0},{2,3},{3,2},{4,5},{5,4},{6,7},{7,6},{8,9},{9,8},{10,11... | collective-permute-start | bytes 221192 | tf_op jit(solution)/shard_map/ppermute | solution.py:69
  154.8 8.5 %collective-permute-start.40 = (bf16[144,256]{1,0:T(8,128)(2,1)S(1)}, bf16[144,256]{1,0:T(8,128)(2,1)S(1)}, u32[]{:S(2)}, u32[]{:S(2)}) collective-permute-start(bf16[144,256]{1,0:T(8,128)(2,1)S(1)} %collective-permute-done.36.refs_3_), channel_id=1, source_target_pairs={{0,1},{1,0},{2,3},{3,2},{4,5},{5,4},{6,7},{7,6},{8,9},{9,8},{10,11... | collective-permute-start | bytes 221192 | tf_op jit(solution)/shard_map/ppermute | solution.py:69
  155.2 8.0 %collective-permute-start.46 = (bf16[144,256]{1,0:T(8,128)(2,1)S(1)}, bf16[144,256]{1,0:T(8,128)(2,1)S(1)}, u32[]{:S(2)}, u32[]{:S(2)}) collective-permute-start(bf16[144,256]{1,0:T(8,128)(2,1)S(1)} %collective-permute-done.42.refs_9_), channel_id=1, source_target_pairs={{0,1},{1,0},{2,3},{3,2},{4,5},{5,4},{6,7},{7,6},{8,9},{9,8},{10,11... | collective-permute-start | bytes 221192 | tf_op jit(solution)/shard_map/ppermute | solution.py:69
  155.3 8.0 %collective-permute-start.47 = (bf16[144,256]{1,0:T(8,128)(2,1)S(1)}, bf16[144,256]{1,0:T(8,128)(2,1)S(1)}, u32[]{:S(2)}, u32[]{:S(2)}) collective-permute-start(bf16[144,256]{1,0:T(8,128)(2,1)S(1)} %collective-permute-done.43.refs_10_), channel_id=1, source_target_pairs={{0,1},{1,0},{2,3},{3,2},{4,5},{5,4},{6,7},{7,6},{8,9},{9,8},{10,11... | collective-permute-start | bytes 221192 | tf_op jit(solution)/shard_map/ppermute | solution.py:69
  155.7 7.5 %collective-permute-start.48 = (bf16[144,256]{1,0:T(8,128)(2,1)S(1)}, bf16[144,256]{1,0:T(8,128)(2,1)S(1)}, u32[]{:S(2)}, u32[]{:S(2)}) collective-permute-start(bf16[144,256]{1,0:T(8,128)(2,1)S(1)} %collective-permute-done.44.refs_11_), channel_id=1, source_target_pairs={{0,1},{1,0},{2,3},{3,2},{4,5},{5,4},{6,7},{7,6},{8,9},{9,8},{10,11... | collective-permute-start | bytes 221192 | tf_op jit(solution)/shard_map/ppermute | solution.py:69
  (19 other events, 195.8 us)

commit v3 on v2

--- a/solution.py
+++ b/solution.py
@@ -192,11 +192,6 @@
     exps = jnp.exp2(scaled * (log2e / sharpness))
     row = own_row + lax.broadcasted_iota(i32, (ROWS, 1), 0)
     return jnp.concatenate([jnp.where(ids == row, 0.0, exps[:ROWS]), exps[ROWS:]], axis=0)
-
-
-def place_body(given, out):
-    for i in range(5):
-        out[i] = given[i]
 
 
 def score_body(where, pay0, pay1, pay2, pay3, cols, row_out, col_out, tile, who, acc):
@@ -230,9 +225,7 @@
         row_out[r : r + 1, :] = total
 
 
-def weight_body(
-    where, tile, who, cols, sum0, sum1, sum2, sum3, col_sums, own, mate, loss, scale, acc
-):
+def scale_body(sum0, sum1, sum2, sum3, scale):
     sums = (sum0, sum1, sum2, sum3)
     for r in range(8):
         d, m = divmod(r, 2)
@@ -242,30 +235,34 @@
             part = sums[s][at : at + 1, :]
             total = part if total is None else total + part
         scale[r * ROWS : (r + 1) * ROWS, :] = as_column(1.0 / total)
+
+
+def weight_body(where, tile, who, cols, scale, col_sums, own, mate, loss, acc):
     columns = col_sums[0]
     for i in range(1, 16):
         columns = columns + col_sums[i]
     logs = jnp.log(columns[:, :2048])
     loss[...] = jnp.full((1, 128), jnp.sum(logs) - jnp.sum(columns[:, 2048:2049]), f32)
-    for j in range(8):
-        block = cols[2 * j : 2 * j + 2].reshape(256, E)
-        scaled = dot_t(tile[...], block)
-        ids = column_ids(where[1], j)
-        here = exp_block(scaled, ids, where[0])
-        ids = ids.astype(f32)
-        by_col = 1.0 / columns[:, j * 256 : (j + 1) * 256]
+    for j in range(4):
+        block = cols[4 * j : 4 * j + 4].reshape(512, E)
         sides = [], []
-        for low in (0, 128):
-            half = here[:, low : low + 128]
-            hit = jnp.where(who[...] == ids[:, low : low + 128], 1.0, 0.0)
-            sides[0].append((half * scale[...] - hit).astype(bf16))
-            sides[1].append((half * by_col[:, low : low + 128] - hit).astype(bf16))
-        weights = jnp.concatenate(sides[0], axis=1)
-        mirror = jnp.concatenate(sides[1], axis=1)
-        part = dot(weights, block) + dot(mirror, block)
+        for half in range(2):
+            one = block[half * 256 : (half + 1) * 256]
+            ids = column_ids(where[1], 2 * j + half)
+            here = exp_block(dot_t(tile[...], one), ids, where[0])
+            ids = ids.astype(f32)
+            at = (2 * j + half) * 256
+            by_col = 1.0 / columns[:, at : at + 256]
+            for low in (0, 128):
+                part = here[:, low : low + 128]
+                hit = jnp.where(who[...] == ids[:, low : low + 128], 1.0, 0.0)
+                sides[0].append((part * scale[...] - hit).astype(bf16))
+                sides[1].append((part * by_col[:, low : low + 128] - hit).astype(bf16))
+        both = jnp.concatenate(sides[0] + sides[1], axis=1)
+        part = dot(both, jnp.concatenate([block, block], axis=0))
         if j == 0:
             acc[...] = part
-        elif j < 7:
+        elif j < 3:
             acc[...] += part
         else:
             part = acc[...] + part
@@ -462,9 +459,6 @@
         beside + tuple(swap(p) for p in beside[:3]) + (swap(beside[3]),)
     )
 
-    where = kernel(
-        place_body, sds((5,), i32), where, in_specs=[smem], out_specs=smem
-    )
     row_sums, col_sums, tile, who = kernel(
         score_body,
         (
@@ -482,9 +476,7 @@
     col_sums = exchange(col_sums, XZ)
     row_sums = kernel(pair_sum_body, sds((8, ROWS), f32), row_sums, swap(row_sums))
     row_sums = [row_sums] + [along_y(row_sums, -d) for d in (1, 2, 3)]
-    where = kernel(
-        place_body, sds((5,), i32), where, in_specs=[smem], out_specs=smem
-    )
+    scale = kernel(scale_body, sds((8 * ROWS, 128), f32), *row_sums)
     grads, mate_grads, loss = kernel(
         weight_body,
         (
@@ -492,11 +484,10 @@
             sds((4, ROWS, E), f32),
             far_sds((1, 128), f32),
         ),
-        where, kept(tile), kept(who), kept(cols), *row_sums, col_sums,
-        in_specs=[smem] + [vm] * 8,
+        where, kept(tile), kept(who), kept(cols), scale, col_sums,
+        in_specs=[smem] + [vm] * 5,
         out_specs=[vm, vm, vm],
         scratch=[
-            pltpu.VMEM((1024, 128), f32),
             pltpu.VMEM((1024, E), f32),
         ],
         flops=3 * 10**9,
@@ -515,7 +506,7 @@
     send, loss_all = kernel(
         head_body,
         (sds((8, U + 32, E), bf16), sds((1, 128), f32)),
-        kept(joined_a), kept(joined_b), hidden_a, hidden_b, slope_a, slope_b, kept(w_second), *ring,
+        kept(joined_a), kept(joined_b), kept(hidden_a), kept(hidden_b), kept(slope_a), kept(slope_b), kept(w_second), *ring,
         grid=(4,),
         in_specs=[
             pl.BlockSpec((8 * ROWS, 512), lambda j: (0, j)),

time: 220 us -> 218 us (level)
  local copies, waits for them, and re-layouts: 3.05 us -> 0.78 us
    ppermute x21, waiting for transfers between devices: 30.2 us -> 32.6 us  [along_y(): return lax.ppermute(block, 'y', [(i, (i + distance) % 4) for i in range(4)])]
    unnamed x30 -> x22, local copies, waits for them, and re-layouts: 2.96 us -> 0.69 us
    pallas_call x17 -> x16, Pallas kernels: 47.8 us -> 46.8 us  [kernel(): pl.pallas_call(body, out_shape=outs, scratch_shapes=list(scratch), compil...]
  transfers between devices with their start and end apart: 52 -> 52, of which waited for: 18 -> 18; matrix products, arithmetic and copies ran while one was open for 0% -> 0% of each run, Pallas kernels for 18% -> 17%
where the time goes in v3:
time: 218 us; the launch traced here: 216 us
  waiting for transfers between devices  71.2 us (33%)
  starting transfers between devices  52.9 us (24%)
  Pallas kernels  46.8 us (21%)
  blocking collectives  43.3 us (20%)
    pallas_call x16, Pallas kernels, kernel(): pl.pallas_call(body, out_shape=outs, scratch_shapes=list(scratch), compil...  46.8 us
    all_to_all x2, blocking collectives, exchange(): return lax.all_to_all(array, axis, 0, 0, tiled=True)  43.3 us
    ppermute x21, waiting for transfers between devices, along_y(): return lax.ppermute(block, 'y', [(i, (i + distance) % 4) for i in range(4)])  32.6 us
    ppermute x7, waiting for transfers between devices, along_z(): return lax.ppermute(block, ZC, pairs)  26.3 us
    ppermute x21, starting transfers between devices, along_y(): return lax.ppermute(block, 'y', [(i, (i + distance) % 4) for i in range(4)])  22 us
    all_to_all x3, starting transfers between devices, exchange(): return lax.all_to_all(array, axis, 0, 0, tiled=True)  15.4 us
    all_to_all x3, waiting for transfers between devices, exchange(): return lax.all_to_all(array, axis, 0, 0, tiled=True)  9.79 us
    ppermute x7, starting transfers between devices, along_z(): return lax.ppermute(block, ZC, pairs)  8.38 us
  transfers between devices with their start and end apart: 52, of which 18 were waited for; matrix products, arithmetic and copies ran while one was open for 0% of the time, Pallas kernels for 17%

profile of v3, /device:TPU:6, one launch (start us, length us, event | category | flops | bytes accessed | tf_op | source)
XLA Modules:
  0.0 215.8 jit_solution(15653517338840588186)
XLA Ops:
  0.6 2.0 collective-permute-start.4
  2.6 1.7 collective-permute-start.5
  4.3 13.4 %collective-permute-done.4.refs_1_ = bf16[2048,256]{1,0:T(8,128)(2,1)S(1)} collective-permute-done((bf16[2048,256]{1,0:T(8,128)(2,1)}, bf16[2048,256]{1,0:T(8,128)(2,1)S(1)}, u32[]{:S(2)}, u32[]{:S(2)}) %collective-permute-start.4) | collective-permute-done | bytes 1048608 | tf_op jit(solution)/shard_map/ppermute | solution.py:77
  18.4 2.8 %shard_map.76 = (bf16[64,2048]{1,0:T(8,128)(2,1)S(1)}, bf16[64,2048]{1,0:T(8,128)(2,1)S(1)}) custom-call(bf16[1024,2048]{1,0:T(8,128)(2,1)} %bitcast.12, s32[1,128]{1,0:T(1,128)S(1)} %bitcast.10), custom_call_target="tpu_custom_call" | custom-call | flops 100000000 | tf_op jit(solution)/shard_map/pallas_call | solution.py:54
  21.2 3.1 %collective-permute-start = (bf16[64,2048]{1,0:T(8,128)(2,1)S(1)}, bf16[64,2048]{1,0:T(8,128)(2,1)S(1)}, u32[]{:S(2)}, u32[]{:S(2)}) collective-permute-start(bf16[64,2048]{1,0:T(8,128)(2,1)S(1)} %get-tuple-element.32.a0), channel_id=1, source_target_pairs={{0,6},{2,0},{4,2},{6,4},{1,7},{3,1},{5,3},{7,5},{8,14},{10,8},{12,... | collective-permute-start | bytes 786440 | tf_op jit(solution)/shard_map/ppermute | solution.py:65
  24.3 2.0 collective-permute-start.8
  26.3 4.2 %collective-permute-done.7.refs_5_ = bf16[256,256]{1,0:T(8,128)(2,1)S(1)} collective-permute-done((bf16[256,256]{1,0:T(8,128)(2,1)S(1)}, bf16[256,256]{1,0:T(8,128)(2,1)S(1)}, u32[]{:S(2)}, u32[]{:S(2)}) %collective-permute-start.7) | collective-permute-done | bytes 131104 | tf_op jit(solution)/shard_map/ppermute | solution.py:77
  31.2 1.3 collective-permute-start.2
  32.6 4.3 %collective-permute-done.1.b1 = bf16[64,2048]{1,0:T(8,128)(2,1)S(1)} collective-permute-done((bf16[64,2048]{1,0:T(8,128)(2,1)S(1)}, bf16[64,2048]{1,0:T(8,128)(2,1)S(1)}, u32[]{:S(2)}, u32[]{:S(2)}) %collective-permute-start.1) | collective-permute-done | bytes 262176 | tf_op jit(solution)/shard_map/ppermute | solution.py:65
  36.9 4.6 %collective-permute-done.2.a3 = bf16[64,2048]{1,0:T(8,128)(2,1)S(1)} collective-permute-done((bf16[64,2048]{1,0:T(8,128)(2,1)S(1)}, bf16[64,2048]{1,0:T(8,128)(2,1)S(1)}, u32[]{:S(2)}, u32[]{:S(2)}) %collective-permute-start.2) | collective-permute-done | bytes 262176 | tf_op jit(solution)/shard_map/ppermute | solution.py:65
  41.7 5.3 %collective-permute-done.3.b3 = bf16[64,2048]{1,0:T(8,128)(2,1)S(1)} collective-permute-done((bf16[64,2048]{1,0:T(8,128)(2,1)S(1)}, bf16[64,2048]{1,0:T(8,128)(2,1)S(1)}, u32[]{:S(2)}, u32[]{:S(2)}) %collective-permute-start.3) | collective-permute-done | bytes 262176 | tf_op jit(solution)/shard_map/ppermute | solution.py:65
  47.0 3.9 %shard_map.77 = (bf16[384,2048]{1,0:T(8,128)(2,1)}, bf16[256,2048]{1,0:T(8,128)(2,1)}, f32[128,256]{1,0:T(8,128)S(1)}, f32[128,256]{1,0:T(8,128)S(1)}, f32[128,256]{1,0:T(8,128)S(1)}) custom-call(bf16[64,2048]{1,0:T(8,128)(2,1)S(1)} %get-tuple-element.32.a0, bf16[64,2048]{1,0:T(8,128)(2,1)S(1)} %get-tuple-element.33.b0, ...), custom_call_target="tpu_custom_call" | custom-call | flops 2000000000 | tf_op jit(solution)/shard_map/pallas_call | solution.py:54
  50.9 2.0 collective-permute-start.22
  52.9 1.6 collective-permute-done.11.b2
  54.6 1.8 shard_map.78
  56.5 3.2 %collective-permute-start.24 = (f32[128,256]{1,0:T(8,128)S(1)}, f32[128,256]{1,0:T(8,128)S(1)}, u32[]{:S(2)}, u32[]{:S(2)}) collective-permute-start(f32[128,256]{1,0:T(8,128)S(1)} %get-tuple-element.46), channel_id=1, source_target_pairs={{0,6},{2,0},{4,2},{6,4},{1,7},{3,1},{5,3},{7,5},{8,14},{10,8},{12,... | collective-permute-start | bytes 393224 | tf_op jit(solution)/shard_map/ppermute | solution.py:65
  59.7 3.2 %collective-permute-done.23.p2 = f32[128,256]{1,0:T(8,128)S(1)} collective-permute-done((f32[128,256]{1,0:T(8,128)S(1)}, f32[128,256]{1,0:T(8,128)S(1)}, u32[]{:S(2)}, u32[]{:S(2)}) %collective-permute-start.23) | collective-permute-done | bytes 131104 | tf_op jit(solution)/shard_map/ppermute | solution.py:65
  62.9 1.2 shard_map.81
  64.1 5.0 %all-to-all-start = ((bf16[16,128,256]{2,1,0:T(8,128)(2,1)}), bf16[16,128,256]{2,1,0:T(8,128)(2,1)S(1)}, u32[]{:S(2)}, u32[]{:S(2)}) async-start(bf16[16,128,256]{2,1,0:T(8,128)(2,1)} %get-tuple-element.49), calls=%async_computation | async-start | bytes 2097152 | tf_op jit(solution)/shard_map/all_to_all | solution.py:81
  69.1 1.5 collective-permute-start.16
  70.6 1.3 collective-permute-done.25.mate
  71.9 2.8 %collective-permute-start.26 = (bf16[256,384]{1,0:T(8,128)(2,1)S(1)}, bf16[256,384]{1,0:T(8,128)(2,1)S(1)}, u32[]{:S(2)}, u32[]{:S(2)}) collective-permute-start(bf16[256,384]{1,0:T(8,128)(2,1)S(1)} %shard_map.82.pay0), channel_id=1, source_target_pairs={{0,6},{2,0},{4,2},{6,4},{1,7},{3,1},{5,3},{7,5},{8,14},{10,8},{12,... | collective-permute-start | bytes 589832 | tf_op jit(solution)/shard_map/ppermute | solution.py:65
  75.9 7.5 %collective-permute-done.26.pay1 = bf16[256,384]{1,0:T(8,128)(2,1)S(1)} collective-permute-done((bf16[256,384]{1,0:T(8,128)(2,1)S(1)}, bf16[256,384]{1,0:T(8,128)(2,1)S(1)}, u32[]{:S(2)}, u32[]{:S(2)}) %collective-permute-start.26) | collective-permute-done | bytes 196640 | tf_op jit(solution)/shard_map/ppermute | solution.py:65
  84.0 3.0 %collective-permute-done.28.pay3 = bf16[256,384]{1,0:T(8,128)(2,1)S(1)} collective-permute-done((bf16[256,384]{1,0:T(8,128)(2,1)S(1)}, bf16[256,384]{1,0:T(8,128)(2,1)S(1)}, u32[]{:S(2)}, u32[]{:S(2)}) %collective-permute-start.28) | collective-permute-done | bytes 196640 | tf_op jit(solution)/shard_map/ppermute | solution.py:65
  87.0 3.7 %shard_map.83 = (f32[8,128]{1,0:T(8,128)S(1)}, f32[16,1,2176]{2,1,0:T(1,128)}, bf16[1024,256]{1,0:T(8,128)(2,1)}, f32[1024,128]{1,0:T(8,128)}) custom-call(s32[5]{0:T(128)S(1)} %stack.23.where, bf16[256,384]{1,0:T(8,128)(2,1)S(1)} %shard_map.82.pay0, bf16[256,384]{1,0:T(8,128)(2,1)S(1)} %collective-permute-done.26.pay1, ...), custom_call_target="tpu_custom_call" | custom-call | flops 1000000000 | tf_op jit(solution)/shard_map/pallas_call | solution.py:54
  90.7 6.9 %all-to-all-start.1 = ((f32[16,1,2176]{2,1,0:T(1,128)}), f32[16,1,2176]{2,1,0:T(1,128)S(1)}, u32[]{:S(2)}, u32[]{:S(2)}) async-start(f32[16,1,2176]{2,1,0:T(1,128)} %get-tuple-element.53), calls=%async_computation.1 | async-start | bytes 278528 | tf_op jit(solution)/shard_map/all_to_all | solution.py:81
  97.7 1.2 collective-permute-done.29.mate
  100.9 1.6 collective-permute-done.30.sum1
  102.5 1.5 collective-permute-start.14
  104.7 1.5 collective-permute-start.17
  106.4 6.9 %shard_map.86 = (f32[4,128,256]{2,1,0:T(8,128)S(1)}, f32[4,128,256]{2,1,0:T(8,128)S(1)}, f32[1,128]{1,0:T(1,128)}) custom-call(s32[5]{0:T(128)S(1)} %stack.23.where, bf16[1024,256]{1,0:T(8,128)(2,1)} %get-tuple-element.50.tile, f32[1024,128]{1,0:T(8,128)} %get-tuple-element.51.who, bf16[16,128,256]{2,1,0:T(8,128)(2,1)} %copy-done.1, ...), custom_call_target="tpu_custom_call" | custom-call | flops 3000000000 | tf_op jit(solution)/shard_map/pallas_call | solution.py:54
  113.8 1.5 collective-permute-start.15
  115.3 6.1 %collective-permute-done.15.refs_1_ = bf16[64,2048]{1,0:T(8,128)(2,1)S(1)} collective-permute-done((bf16[64,2048]{1,0:T(8,128)(2,1)S(1)}, bf16[64,2048]{1,0:T(8,128)(2,1)S(1)}, u32[]{:S(2)}, u32[]{:S(2)}) %collective-permute-start.15) | collective-permute-done | bytes 262176 | tf_op jit(solution)/shard_map/ppermute | solution.py:77
  122.0 0.9 shard_map.87
  122.9 3.5 %all-to-all-start.2 = ((f32[4,128,256]{2,1,0:T(8,128)}), f32[4,128,256]{2,1,0:T(8,128)S(1)}, u32[]{:S(2)}, u32[]{:S(2)}) async-start(f32[4,128,256]{2,1,0:T(8,128)} %shard_map.87), calls=%async_computation.2 | async-start | bytes 1048576 | tf_op jit(solution)/shard_map/all_to_all | solution.py:81
  126.9 9.8 %all-to-all-done.2.got = f32[4,128,256]{2,1,0:T(8,128)S(1)} async-done(((f32[4,128,256]{2,1,0:T(8,128)}), f32[4,128,256]{2,1,0:T(8,128)S(1)}, u32[]{:S(2)}, u32[]{:S(2)}) %all-to-all-start.2) | async-done | bytes 524320 | tf_op jit(solution)/shard_map/all_to_all | solution.py:81
  136.7 1.1 shard_map.88.refs_0_
  138.4 1.2 collective-permute-start.34
  139.5 1.5 collective-permute-start.35
  141.1 2.6 %collective-permute-done.41.refs_8_ = bf16[144,256]{1,0:T(8,128)(2,1)S(1)} collective-permute-done((bf16[144,256]{1,0:T(8,128)(2,1)S(1)}, bf16[144,256]{1,0:T(8,128)(2,1)S(1)}, u32[]{:S(2)}, u32[]{:S(2)}) %collective-permute-start.41) | collective-permute-done | bytes 73760 | tf_op jit(solution)/shard_map/ppermute | solution.py:77
  143.7 1.2 collective-permute-start.42
  144.9 1.5 collective-permute-start.43
  147.1 7.3 %shard_map.79 = (bf16[256,1024]{1,0:T(8,128)(2,1)}, f32[256,1024]{1,0:T(8,128)}, bf16[1024,2048]{1,0:T(8,128)(2,1)}) custom-call(bf16[384,2048]{1,0:T(8,128)(2,1)} %get-tuple-element.34.refs_0_, bf16[128,2048]{1,0:T(8,128)(2,1)} %get-tuple-element.35.refs_1_, bf16[384,2048]{1,0:T(8,128)(2,1)} %collective-permute-done.12.refs_2_, ...), custom_call_target="tpu_custom_call" | custom-call | flops 2000000000 | tf_op jit(solution)/shard_map/pallas_call | solution.py:54
  155.6 7.4 %shard_map.80 = (bf16[256,1024]{1,0:T(8,128)(2,1)}, f32[256,1024]{1,0:T(8,128)}, bf16[1024,2048]{1,0:T(8,128)(2,1)}) custom-call(bf16[64,2048]{1,0:T(8,128)(2,1)} %collective-permute-done.14.refs_0_, bf16[64,2048]{1,0:T(8,128)(2,1)} %copy-done.9, bf16[256,2048]{1,0:T(8,128)(2,1)} %copy-done.6, bf16[128,2048]{1,0:T(8,128)(2,1)} %collective-permute-done.17.refs_3_, ...), custom_call_target="tpu_custom_call" | custom-call | flops 2000000000 | tf_op jit(solution)/shard_map/pallas_call | solution.py:54
  163.1 7.3 %shard_map.89 = (bf16[8,288,256]{2,1,0:T(8,128)(2,1)S(1)}, f32[1,128]{1,0:T(1,128)}) custom-call(bf16[1024,2048]{1,0:T(8,128)(2,1)} %get-tuple-element.36.pool_a, bf16[1024,2048]{1,0:T(8,128)(2,1)} %get-tuple-element.38.pool_b, bf16[256,1024]{1,0:T(8,128)(2,1)} %get-tuple-element.39.hidden_a, bf16[256,1024]{1,0:T(8,128)(2,1)} %get-tuple-element.40.hidden_b, ...), custom_call_target="tpu_custom_call" | custom-call | flops 2000000000 | tf_op jit(solution)/shard_map/pallas_call | solution.py:54
  170.4 22.7 %all_to_all.25.got = bf16[8,288,256]{2,1,0:T(8,128)(2,1)S(1)} all-to-all(bf16[8,288,256]{2,1,0:T(8,128)(2,1)S(1)} %get-tuple-element.58), channel_id=1, replica_groups=mesh['x'=4,'zh'=2,'zl'=2,'y'=4,'c'=2] {'x','zh'}, dimensions={0} | all-to-all | bytes 2359296 | tf_op jit(solution)/shard_map/all_to_all | solution.py:81
  193.4 20.6 %all_to_all.26.got = bf16[8,288,256]{2,1,0:T(8,128)(2,1)S(1)} all-to-all(bf16[8,288,256]{2,1,0:T(8,128)(2,1)S(1)} %shard_map.90), channel_id=1, replica_groups=mesh['x'=4,'zh'=2,'zl'=2,'y'=4,'c'=2] {'x','zh'}, dimensions={0} | all-to-all | bytes 2359296 | tf_op jit(solution)/shard_map/all_to_all | solution.py:81
  213.9 1.9 shard_map.91
  (97 shorter events, 11.1 us)
Async XLA Ops:
  0.6 17.1 %collective-permute-start.4 = (bf16[2048,256]{1,0:T(8,128)(2,1)}, bf16[2048,256]{1,0:T(8,128)(2,1)S(1)}, u32[]{:S(2)}, u32[]{:S(2)}) collective-permute-start(bf16[2048,256]{1,0:T(8,128)(2,1)} %refs_8_.1), channel_id=1, source_target_pairs={{0,8},{1,25},{8,16},{9,1},{16,24},{17,9},{24,0},{25,17},{2,10},{3,... | collective-permute-start | bytes 3145736 | tf_op jit(solution)/shard_map/ppermute | solution.py:77
  2.6 44.4 %collective-permute-start.5 = (bf16[2048,256]{1,0:T(8,128)(2,1)}, bf16[2048,256]{1,0:T(8,128)(2,1)S(1)}, u32[]{:S(2)}, u32[]{:S(2)}) collective-permute-start(bf16[2048,256]{1,0:T(8,128)(2,1)} %refs_8_.1), channel_id=1, source_target_pairs={{0,1},{1,0},{2,3},{3,2},{4,5},{5,4},{6,7},{7,6},{8,9},{9,8},{10,11... | collective-permute-start | bytes 3145736 | tf_op jit(solution)/shard_map/ppermute | solution.py:69
  17.7 29.2 %collective-permute-start.6 = (bf16[2048,256]{1,0:T(8,128)(2,1)S(1)}, bf16[2048,256]{1,0:T(8,128)(2,1)S(1)}, u32[]{:S(2)}, u32[]{:S(2)}) collective-permute-start(bf16[2048,256]{1,0:T(8,128)(2,1)S(1)} %collective-permute-done.4.refs_1_), channel_id=1, source_target_pairs={{0,1},{1,0},{2,3},{3,2},{4,5},{5,4},{6,7},{7,6},{8,9},{9,8},{10,11... | collective-permute-start | bytes 3145736 | tf_op jit(solution)/shard_map/ppermute | solution.py:69
  21.2 11.3 %collective-permute-start = (bf16[64,2048]{1,0:T(8,128)(2,1)S(1)}, bf16[64,2048]{1,0:T(8,128)(2,1)S(1)}, u32[]{:S(2)}, u32[]{:S(2)}) collective-permute-start(bf16[64,2048]{1,0:T(8,128)(2,1)S(1)} %get-tuple-element.32.a0), channel_id=1, source_target_pairs={{0,6},{2,0},{4,2},{6,4},{1,7},{3,1},{5,3},{7,5},{8,14},{10,8},{12,... | collective-permute-start | bytes 786440 | tf_op jit(solution)/shard_map/ppermute | solution.py:65
  24.3 6.2 %collective-permute-start.7 = (bf16[256,256]{1,0:T(8,128)(2,1)S(1)}, bf16[256,256]{1,0:T(8,128)(2,1)S(1)}, u32[]{:S(2)}, u32[]{:S(2)}) collective-permute-start(bf16[256,256]{1,0:T(8,128)(2,1)S(1)} %copy-done.2), channel_id=1, source_target_pairs={{0,8},{1,25},{8,16},{9,1},{16,24},{17,9},{24,0},{25,17},{2,10},{3,... | collective-permute-start | bytes 393224 | tf_op jit(solution)/shard_map/ppermute | solution.py:77
  24.3 6.9 %collective-permute-start.8 = (bf16[256,256]{1,0:T(8,128)(2,1)S(1)}, bf16[256,256]{1,0:T(8,128)(2,1)S(1)}, u32[]{:S(2)}, u32[]{:S(2)}) collective-permute-start(bf16[256,256]{1,0:T(8,128)(2,1)S(1)} %copy-done.2), channel_id=1, source_target_pairs={{0,1},{1,0},{2,3},{3,2},{4,5},{5,4},{6,7},{7,6},{8,9},{9,8},{10,11... | collective-permute-start | bytes 393224 | tf_op jit(solution)/shard_map/ppermute | solution.py:69
  30.5 6.4 %collective-permute-start.1 = (bf16[64,2048]{1,0:T(8,128)(2,1)S(1)}, bf16[64,2048]{1,0:T(8,128)(2,1)S(1)}, u32[]{:S(2)}, u32[]{:S(2)}) collective-permute-start(bf16[64,2048]{1,0:T(8,128)(2,1)S(1)} %get-tuple-element.33.b0), channel_id=1, source_target_pairs={{0,6},{2,0},{4,2},{6,4},{1,7},{3,1},{5,3},{7,5},{8,14},{10,8},{12,... | collective-permute-start | bytes 786440 | tf_op jit(solution)/shard_map/ppermute | solution.py:65
  31.2 10.2 %collective-permute-start.2 = (bf16[64,2048]{1,0:T(8,128)(2,1)S(1)}, bf16[64,2048]{1,0:T(8,128)(2,1)S(1)}, u32[]{:S(2)}, u32[]{:S(2)}) collective-permute-start(bf16[64,2048]{1,0:T(8,128)(2,1)S(1)} %get-tuple-element.32.a0), channel_id=1, source_target_pairs={{0,2},{2,4},{4,6},{6,0},{1,3},{3,5},{5,7},{7,1},{8,10},{10,12},{12... | collective-permute-start | bytes 786440 | tf_op jit(solution)/shard_map/ppermute | solution.py:65
  32.5 14.4 %collective-permute-start.3 = (bf16[64,2048]{1,0:T(8,128)(2,1)S(1)}, bf16[64,2048]{1,0:T(8,128)(2,1)S(1)}, u32[]{:S(2)}, u32[]{:S(2)}) collective-permute-start(bf16[64,2048]{1,0:T(8,128)(2,1)S(1)} %get-tuple-element.33.b0), channel_id=1, source_target_pairs={{0,2},{2,4},{4,6},{6,0},{1,3},{3,5},{5,7},{7,1},{8,10},{10,12},{12... | collective-permute-start | bytes 786440 | tf_op jit(solution)/shard_map/ppermute | solution.py:65
  36.9 10.1 %collective-permute-start.9 = (bf16[256,256]{1,0:T(8,128)(2,1)S(1)}, bf16[256,256]{1,0:T(8,128)(2,1)S(1)}, u32[]{:S(2)}, u32[]{:S(2)}) collective-permute-start(bf16[256,256]{1,0:T(8,128)(2,1)S(1)} %collective-permute-done.7.refs_5_), channel_id=1, source_target_pairs={{0,1},{1,0},{2,3},{3,2},{4,5},{5,4},{6,7},{7,6},{8,9},{9,8},{10,11... | collective-permute-start | bytes 393224 | tf_op jit(solution)/shard_map/ppermute | solution.py:69
  41.5 11.5 %collective-permute-start.10 = (bf16[64,2048]{1,0:T(8,128)(2,1)S(1)}, bf16[64,2048]{1,0:T(8,128)(2,1)S(1)}, u32[]{:S(2)}, u32[]{:S(2)}) collective-permute-start(bf16[64,2048]{1,0:T(8,128)(2,1)S(1)} %collective-permute-done.2.a3), channel_id=1, source_target_pairs={{0,2},{2,4},{4,6},{6,0},{1,3},{3,5},{5,7},{7,1},{8,10},{10,12},{12... | collective-permute-start | bytes 786440 | tf_op jit(solution)/shard_map/ppermute | solution.py:65
  47.0 7.6 %collective-permute-start.11 = (bf16[64,2048]{1,0:T(8,128)(2,1)S(1)}, bf16[64,2048]{1,0:T(8,128)(2,1)S(1)}, u32[]{:S(2)}, u32[]{:S(2)}) collective-permute-start(bf16[64,2048]{1,0:T(8,128)(2,1)S(1)} %collective-permute-done.1.b1), channel_id=1, source_target_pairs={{0,6},{2,0},{4,2},{6,4},{1,7},{3,1},{5,3},{7,5},{8,14},{10,8},{12,... | collective-permute-start | bytes 786440 | tf_op jit(solution)/shard_map/ppermute | solution.py:65
  50.9 8.8 %collective-permute-start.22 = (f32[128,256]{1,0:T(8,128)S(1)}, f32[128,256]{1,0:T(8,128)S(1)}, u32[]{:S(2)}, u32[]{:S(2)}) collective-permute-start(f32[128,256]{1,0:T(8,128)S(1)} %get-tuple-element.44), channel_id=1, source_target_pairs={{0,2},{2,4},{4,6},{6,0},{1,3},{3,5},{5,7},{7,1},{8,10},{10,12},{12... | collective-permute-start | bytes 393224 | tf_op jit(solution)/shard_map/ppermute | solution.py:65
  56.4 6.5 %collective-permute-start.23 = (f32[128,256]{1,0:T(8,128)S(1)}, f32[128,256]{1,0:T(8,128)S(1)}, u32[]{:S(2)}, u32[]{:S(2)}) collective-permute-start(f32[128,256]{1,0:T(8,128)S(1)} %get-tuple-element.45), channel_id=1, source_target_pairs={{0,4},{2,6},{4,0},{6,2},{1,5},{3,7},{5,1},{7,3},{8,12},{10,14},{12... | collective-permute-start | bytes 393224 | tf_op jit(solution)/shard_map/ppermute | solution.py:65
  56.5 6.4 %collective-permute-start.24 = (f32[128,256]{1,0:T(8,128)S(1)}, f32[128,256]{1,0:T(8,128)S(1)}, u32[]{:S(2)}, u32[]{:S(2)}) collective-permute-start(f32[128,256]{1,0:T(8,128)S(1)} %get-tuple-element.46), channel_id=1, source_target_pairs={{0,6},{2,0},{4,2},{6,4},{1,7},{3,1},{5,3},{7,5},{8,14},{10,8},{12,... | collective-permute-start | bytes 393224 | tf_op jit(solution)/shard_map/ppermute | solution.py:65
  64.1 22.9 %all-to-all-start = ((bf16[16,128,256]{2,1,0:T(8,128)(2,1)}), bf16[16,128,256]{2,1,0:T(8,128)(2,1)S(1)}, u32[]{:S(2)}, u32[]{:S(2)}) async-start(bf16[16,128,256]{2,1,0:T(8,128)(2,1)} %get-tuple-element.49), calls=%async_computation | async-start | bytes 2097152 | tf_op jit(solution)/shard_map/all_to_all | solution.py:81
  69.1 44.2 %collective-permute-start.16 = (bf16[256,2048]{1,0:T(8,128)(2,1)}, bf16[256,2048]{1,0:T(8,128)(2,1)S(1)}, u32[]{:S(2)}, u32[]{:S(2)}) collective-permute-start(bf16[256,2048]{1,0:T(8,128)(2,1)} %get-tuple-element.37), channel_id=1, source_target_pairs={{0,8},{1,25},{8,16},{9,1},{16,24},{17,9},{24,0},{25,17},{2,10},{3,... | collective-permute-start | bytes 3145736 | tf_op jit(solution)/shard_map/ppermute | solution.py:77
  71.9 11.6 %collective-permute-start.26 = (bf16[256,384]{1,0:T(8,128)(2,1)S(1)}, bf16[256,384]{1,0:T(8,128)(2,1)S(1)}, u32[]{:S(2)}, u32[]{:S(2)}) collective-permute-start(bf16[256,384]{1,0:T(8,128)(2,1)S(1)} %shard_map.82.pay0), channel_id=1, source_target_pairs={{0,6},{2,0},{4,2},{6,4},{1,7},{3,1},{5,3},{7,5},{8,14},{10,8},{12,... | collective-permute-start | bytes 589832 | tf_op jit(solution)/shard_map/ppermute | solution.py:65
  74.7 9.3 %collective-permute-start.27 = (bf16[256,384]{1,0:T(8,128)(2,1)S(1)}, bf16[256,384]{1,0:T(8,128)(2,1)S(1)}, u32[]{:S(2)}, u32[]{:S(2)}) collective-permute-start(bf16[256,384]{1,0:T(8,128)(2,1)S(1)} %shard_map.82.pay0), channel_id=1, source_target_pairs={{0,4},{2,6},{4,0},{6,2},{1,5},{3,7},{5,1},{7,3},{8,12},{10,14},{12... | collective-permute-start | bytes 589832 | tf_op jit(solution)/shard_map/ppermute | solution.py:65
  75.2 11.8 %collective-permute-start.28 = (bf16[256,384]{1,0:T(8,128)(2,1)S(1)}, bf16[256,384]{1,0:T(8,128)(2,1)S(1)}, u32[]{:S(2)}, u32[]{:S(2)}) collective-permute-start(bf16[256,384]{1,0:T(8,128)(2,1)S(1)} %shard_map.82.pay0), channel_id=1, source_target_pairs={{0,2},{2,4},{4,6},{6,0},{1,3},{3,5},{5,7},{7,1},{8,10},{10,12},{12... | collective-permute-start | bytes 589832 | tf_op jit(solution)/shard_map/ppermute | solution.py:65
  75.8 65.2 %collective-permute-start.12 = (bf16[384,2048]{1,0:T(8,128)(2,1)}, bf16[384,2048]{1,0:T(8,128)(2,1)}, u32[]{:S(2)}, u32[]{:S(2)}) collective-permute-start(bf16[384,2048]{1,0:T(8,128)(2,1)} %get-tuple-element.34.refs_0_), channel_id=1, source_target_pairs={{0,1},{1,0},{2,3},{3,2},{4,5},{5,4},{6,7},{7,6},{8,9},{9,8},{10,11... | collective-permute-start | bytes 4718600 | tf_op jit(solution)/shard_map/ppermute | solution.py:69
  90.7 15.6 %all-to-all-start.1 = ((f32[16,1,2176]{2,1,0:T(1,128)}), f32[16,1,2176]{2,1,0:T(1,128)S(1)}, u32[]{:S(2)}, u32[]{:S(2)}) async-start(f32[16,1,2176]{2,1,0:T(1,128)} %get-tuple-element.53), calls=%async_computation.1 | async-start | bytes 278528 | tf_op jit(solution)/shard_map/all_to_all | solution.py:81
  99.6 5.1 %collective-permute-start.31 = (f32[8,128]{1,0:T(8,128)S(1)}, f32[8,128]{1,0:T(8,128)S(1)}, u32[]{:S(2)}, u32[]{:S(2)}) collective-permute-start(f32[8,128]{1,0:T(8,128)S(1)} %shard_map.84.sum0), channel_id=1, source_target_pairs={{0,4},{2,6},{4,0},{6,2},{1,5},{3,7},{5,1},{7,3},{8,12},{10,14},{12... | collective-permute-start | bytes 12296 | tf_op jit(solution)/shard_map/ppermute | solution.py:65
  100.0 6.2 %collective-permute-start.32 = (f32[8,128]{1,0:T(8,128)S(1)}, f32[8,128]{1,0:T(8,128)S(1)}, u32[]{:S(2)}, u32[]{:S(2)}) collective-permute-start(f32[8,128]{1,0:T(8,128)S(1)} %shard_map.84.sum0), channel_id=1, source_target_pairs={{0,2},{2,4},{4,6},{6,0},{1,3},{3,5},{5,7},{7,1},{8,10},{10,12},{12... | collective-permute-start | bytes 12296 | tf_op jit(solution)/shard_map/ppermute | solution.py:65
  102.5 11.4 %collective-permute-start.14 = (bf16[64,2048]{1,0:T(8,128)(2,1)S(1)}, bf16[64,2048]{1,0:T(8,128)(2,1)}, u32[]{:S(2)}, u32[]{:S(2)}) collective-permute-start(bf16[64,2048]{1,0:T(8,128)(2,1)S(1)} %get-tuple-element.32.a0), channel_id=1, source_target_pairs={{0,8},{1,25},{8,16},{9,1},{16,24},{17,9},{24,0},{25,17},{2,10},{3,... | collective-permute-start | bytes 786440 | tf_op jit(solution)/shard_map/ppermute | solution.py:77
  104.7 16.7 %collective-permute-start.17 = (bf16[128,2048]{1,0:T(8,128)(2,1)}, bf16[128,2048]{1,0:T(8,128)(2,1)}, u32[]{:S(2)}, u32[]{:S(2)}) collective-permute-start(bf16[128,2048]{1,0:T(8,128)(2,1)} %get-tuple-element.35.refs_1_), channel_id=1, source_target_pairs={{0,8},{1,25},{8,16},{9,1},{16,24},{17,9},{24,0},{25,17},{2,10},{3,... | collective-permute-start | bytes 1572872 | tf_op jit(solution)/shard_map/ppermute | solution.py:77
  113.3 8.6 %collective-permute-start.33 = (f32[4,128,256]{2,1,0:T(8,128)S(1)}, f32[4,128,256]{2,1,0:T(8,128)S(1)}, u32[]{:S(2)}, u32[]{:S(2)}) collective-permute-start(f32[4,128,256]{2,1,0:T(8,128)S(1)} %get-tuple-element.55), channel_id=1, source_target_pairs={{0,1},{1,0},{2,3},{3,2},{4,5},{5,4},{6,7},{7,6},{8,9},{9,8},{10,11... | collective-permute-start | bytes 1572872 | tf_op jit(solution)/shard_map/ppermute | solution.py:69
  113.3 27.7 %collective-permute-start.20 = (bf16[256,2048]{1,0:T(8,128)(2,1)S(1)}, bf16[256,2048]{1,0:T(8,128)(2,1)}, u32[]{:S(2)}, u32[]{:S(2)}) collective-permute-start(bf16[256,2048]{1,0:T(8,128)(2,1)S(1)} %collective-permute-done.16.refs_2_), channel_id=1, source_target_pairs={{0,1},{1,0},{2,3},{3,2},{4,5},{5,4},{6,7},{7,6},{8,9},{9,8},{10,11... | collective-permute-start | bytes 3145736 | tf_op jit(solution)/shard_map/ppermute | solution.py:69
  113.8 7.6 %collective-permute-start.15 = (bf16[64,2048]{1,0:T(8,128)(2,1)S(1)}, bf16[64,2048]{1,0:T(8,128)(2,1)S(1)}, u32[]{:S(2)}, u32[]{:S(2)}) collective-permute-start(bf16[64,2048]{1,0:T(8,128)(2,1)S(1)} %get-tuple-element.33.b0), channel_id=1, source_target_pairs={{0,8},{1,25},{8,16},{9,1},{16,24},{17,9},{24,0},{25,17},{2,10},{3,... | collective-permute-start | bytes 786440 | tf_op jit(solution)/shard_map/ppermute | solution.py:77
  121.4 17.0 %collective-permute-start.13 = (bf16[128,2048]{1,0:T(8,128)(2,1)}, bf16[128,2048]{1,0:T(8,128)(2,1)S(1)}, u32[]{:S(2)}, u32[]{:S(2)}) collective-permute-start(bf16[128,2048]{1,0:T(8,128)(2,1)} %get-tuple-element.35.refs_1_), channel_id=1, source_target_pairs={{0,1},{1,0},{2,3},{3,2},{4,5},{5,4},{6,7},{7,6},{8,9},{9,8},{10,11... | collective-permute-start | bytes 1572872 | tf_op jit(solution)/shard_map/ppermute | solution.py:69
  121.9 17.6 %collective-permute-start.21 = (bf16[128,2048]{1,0:T(8,128)(2,1)}, bf16[128,2048]{1,0:T(8,128)(2,1)S(1)}, u32[]{:S(2)}, u32[]{:S(2)}) collective-permute-start(bf16[128,2048]{1,0:T(8,128)(2,1)} %collective-permute-done.17.refs_3_), channel_id=1, source_target_pairs={{0,1},{1,0},{2,3},{3,2},{4,5},{5,4},{6,7},{7,6},{8,9},{9,8},{10,11... | collective-permute-start | bytes 1572872 | tf_op jit(solution)/shard_map/ppermute | solution.py:69
  122.9 13.8 %all-to-all-start.2 = ((f32[4,128,256]{2,1,0:T(8,128)}), f32[4,128,256]{2,1,0:T(8,128)S(1)}, u32[]{:S(2)}, u32[]{:S(2)}) async-start(f32[4,128,256]{2,1,0:T(8,128)} %shard_map.87), calls=%async_computation.2 | async-start | bytes 1048576 | tf_op jit(solution)/shard_map/all_to_all | solution.py:81
  126.4 11.5 %collective-permute-start.19 = (bf16[64,2048]{1,0:T(8,128)(2,1)S(1)}, bf16[64,2048]{1,0:T(8,128)(2,1)}, u32[]{:S(2)}, u32[]{:S(2)}) collective-permute-start(bf16[64,2048]{1,0:T(8,128)(2,1)S(1)} %collective-permute-done.15.refs_1_), channel_id=1, source_target_pairs={{0,1},{1,0},{2,3},{3,2},{4,5},{5,4},{6,7},{7,6},{8,9},{9,8},{10,11... | collective-permute-start | bytes 786440 | tf_op jit(solution)/shard_map/ppermute | solution.py:69
  137.8 5.9 %collective-permute-start.41 = (bf16[144,256]{1,0:T(8,128)(2,1)S(1)}, bf16[144,256]{1,0:T(8,128)(2,1)S(1)}, u32[]{:S(2)}, u32[]{:S(2)}) collective-permute-start(bf16[144,256]{1,0:T(8,128)(2,1)S(1)} %shard_map.88.refs_0_), channel_id=1, source_target_pairs={{0,8},{1,25},{8,16},{9,1},{16,24},{17,9},{24,0},{25,17},{2,10},{3,... | collective-permute-start | bytes 221192 | tf_op jit(solution)/shard_map/ppermute | solution.py:77
  138.4 6.5 %collective-permute-start.34 = (bf16[144,256]{1,0:T(8,128)(2,1)S(1)}, bf16[144,256]{1,0:T(8,128)(2,1)S(1)}, u32[]{:S(2)}, u32[]{:S(2)}) collective-permute-start(bf16[144,256]{1,0:T(8,128)(2,1)S(1)} %shard_map.88.refs_0_), channel_id=1, source_target_pairs={{0,6},{2,0},{4,2},{6,4},{1,7},{3,1},{5,3},{7,5},{8,14},{10,8},{12,... | collective-permute-start | bytes 221192 | tf_op jit(solution)/shard_map/ppermute | solution.py:65
  139.5 6.8 %collective-permute-start.35 = (bf16[144,256]{1,0:T(8,128)(2,1)S(1)}, bf16[144,256]{1,0:T(8,128)(2,1)S(1)}, u32[]{:S(2)}, u32[]{:S(2)}) collective-permute-start(bf16[144,256]{1,0:T(8,128)(2,1)S(1)} %shard_map.88.refs_0_), channel_id=1, source_target_pairs={{0,4},{2,6},{4,0},{6,2},{1,5},{3,7},{5,1},{7,3},{8,12},{10,14},{12... | collective-permute-start | bytes 221192 | tf_op jit(solution)/shard_map/ppermute | solution.py:65
  141.0 5.6 %collective-permute-start.36 = (bf16[144,256]{1,0:T(8,128)(2,1)S(1)}, bf16[144,256]{1,0:T(8,128)(2,1)S(1)}, u32[]{:S(2)}, u32[]{:S(2)}) collective-permute-start(bf16[144,256]{1,0:T(8,128)(2,1)S(1)} %shard_map.88.refs_0_), channel_id=1, source_target_pairs={{0,2},{2,4},{4,6},{6,0},{1,3},{3,5},{5,7},{7,1},{8,10},{10,12},{12... | collective-permute-start | bytes 221192 | tf_op jit(solution)/shard_map/ppermute | solution.py:65
  141.0 5.6 %collective-permute-start.37 = (bf16[144,256]{1,0:T(8,128)(2,1)S(1)}, bf16[144,256]{1,0:T(8,128)(2,1)S(1)}, u32[]{:S(2)}, u32[]{:S(2)}) collective-permute-start(bf16[144,256]{1,0:T(8,128)(2,1)S(1)} %shard_map.88.refs_0_), channel_id=1, source_target_pairs={{0,1},{1,0},{2,3},{3,2},{4,5},{5,4},{6,7},{7,6},{8,9},{9,8},{10,11... | collective-permute-start | bytes 221192 | tf_op jit(solution)/shard_map/ppermute | solution.py:69
  143.7 11.3 %collective-permute-start.42 = (bf16[144,256]{1,0:T(8,128)(2,1)S(1)}, bf16[144,256]{1,0:T(8,128)(2,1)S(1)}, u32[]{:S(2)}, u32[]{:S(2)}) collective-permute-start(bf16[144,256]{1,0:T(8,128)(2,1)S(1)} %collective-permute-done.41.refs_8_), channel_id=1, source_target_pairs={{0,6},{2,0},{4,2},{6,4},{1,7},{3,1},{5,3},{7,5},{8,14},{10,8},{12,... | collective-permute-start | bytes 221192 | tf_op jit(solution)/shard_map/ppermute | solution.py:65
  144.9 10.3 %collective-permute-start.43 = (bf16[144,256]{1,0:T(8,128)(2,1)S(1)}, bf16[144,256]{1,0:T(8,128)(2,1)S(1)}, u32[]{:S(2)}, u32[]{:S(2)}) collective-permute-start(bf16[144,256]{1,0:T(8,128)(2,1)S(1)} %collective-permute-done.41.refs_8_), channel_id=1, source_target_pairs={{0,4},{2,6},{4,0},{6,2},{1,5},{3,7},{5,1},{7,3},{8,12},{10,14},{12... | collective-permute-start | bytes 221192 | tf_op jit(solution)/shard_map/ppermute | solution.py:65
  146.3 9.2 %collective-permute-start.44 = (bf16[144,256]{1,0:T(8,128)(2,1)S(1)}, bf16[144,256]{1,0:T(8,128)(2,1)S(1)}, u32[]{:S(2)}, u32[]{:S(2)}) collective-permute-start(bf16[144,256]{1,0:T(8,128)(2,1)S(1)} %collective-permute-done.41.refs_8_), channel_id=1, source_target_pairs={{0,2},{2,4},{4,6},{6,0},{1,3},{3,5},{5,7},{7,1},{8,10},{10,12},{12... | collective-permute-start | bytes 221192 | tf_op jit(solution)/shard_map/ppermute | solution.py:65
  146.6 7.8 %collective-permute-start.38 = (bf16[144,256]{1,0:T(8,128)(2,1)S(1)}, bf16[144,256]{1,0:T(8,128)(2,1)S(1)}, u32[]{:S(2)}, u32[]{:S(2)}) collective-permute-start(bf16[144,256]{1,0:T(8,128)(2,1)S(1)} %collective-permute-done.34.refs_1_), channel_id=1, source_target_pairs={{0,1},{1,0},{2,3},{3,2},{4,5},{5,4},{6,7},{7,6},{8,9},{9,8},{10,11... | collective-permute-start | bytes 221192 | tf_op jit(solution)/shard_map/ppermute | solution.py:69
  146.6 7.9 %collective-permute-start.39 = (bf16[144,256]{1,0:T(8,128)(2,1)S(1)}, bf16[144,256]{1,0:T(8,128)(2,1)S(1)}, u32[]{:S(2)}, u32[]{:S(2)}) collective-permute-start(bf16[144,256]{1,0:T(8,128)(2,1)S(1)} %collective-permute-done.35.refs_2_), channel_id=1, source_target_pairs={{0,1},{1,0},{2,3},{3,2},{4,5},{5,4},{6,7},{7,6},{8,9},{9,8},{10,11... | collective-permute-start | bytes 221192 | tf_op jit(solution)/shard_map/ppermute | solution.py:69
  154.4 8.6 %collective-permute-start.45 = (bf16[144,256]{1,0:T(8,128)(2,1)S(1)}, bf16[144,256]{1,0:T(8,128)(2,1)S(1)}, u32[]{:S(2)}, u32[]{:S(2)}) collective-permute-start(bf16[144,256]{1,0:T(8,128)(2,1)S(1)} %collective-permute-done.41.refs_8_), channel_id=1, source_target_pairs={{0,1},{1,0},{2,3},{3,2},{4,5},{5,4},{6,7},{7,6},{8,9},{9,8},{10,11... | collective-permute-start | bytes 221192 | tf_op jit(solution)/shard_map/ppermute | solution.py:69
  154.5 8.5 %collective-permute-start.40 = (bf16[144,256]{1,0:T(8,128)(2,1)S(1)}, bf16[144,256]{1,0:T(8,128)(2,1)S(1)}, u32[]{:S(2)}, u32[]{:S(2)}) collective-permute-start(bf16[144,256]{1,0:T(8,128)(2,1)S(1)} %collective-permute-done.36.refs_3_), channel_id=1, source_target_pairs={{0,1},{1,0},{2,3},{3,2},{4,5},{5,4},{6,7},{7,6},{8,9},{9,8},{10,11... | collective-permute-start | bytes 221192 | tf_op jit(solution)/shard_map/ppermute | solution.py:69
  155.0 8.1 %collective-permute-start.46 = (bf16[144,256]{1,0:T(8,128)(2,1)S(1)}, bf16[144,256]{1,0:T(8,128)(2,1)S(1)}, u32[]{:S(2)}, u32[]{:S(2)}) collective-permute-start(bf16[144,256]{1,0:T(8,128)(2,1)S(1)} %collective-permute-done.42.refs_9_), channel_id=1, source_target_pairs={{0,1},{1,0},{2,3},{3,2},{4,5},{5,4},{6,7},{7,6},{8,9},{9,8},{10,11... | collective-permute-start | bytes 221192 | tf_op jit(solution)/shard_map/ppermute | solution.py:69
  155.1 8.0 %collective-permute-start.47 = (bf16[144,256]{1,0:T(8,128)(2,1)S(1)}, bf16[144,256]{1,0:T(8,128)(2,1)S(1)}, u32[]{:S(2)}, u32[]{:S(2)}) collective-permute-start(bf16[144,256]{1,0:T(8,128)(2,1)S(1)} %collective-permute-done.43.refs_10_), channel_id=1, source_target_pairs={{0,1},{1,0},{2,3},{3,2},{4,5},{5,4},{6,7},{7,6},{8,9},{9,8},{10,11... | collective-permute-start | bytes 221192 | tf_op jit(solution)/shard_map/ppermute | solution.py:69
  155.5 7.6 %collective-permute-start.48 = (bf16[144,256]{1,0:T(8,128)(2,1)S(1)}, bf16[144,256]{1,0:T(8,128)(2,1)S(1)}, u32[]{:S(2)}, u32[]{:S(2)}) collective-permute-start(bf16[144,256]{1,0:T(8,128)(2,1)S(1)} %collective-permute-done.44.refs_11_), channel_id=1, source_target_pairs={{0,1},{1,0},{2,3},{3,2},{4,5},{5,4},{6,7},{7,6},{8,9},{9,8},{10,11... | collective-permute-start | bytes 221192 | tf_op jit(solution)/shard_map/ppermute | solution.py:69
  (15 other events, 160.1 us)

commit v4 on v3

--- a/solution.py
+++ b/solution.py
@@ -269,20 +269,19 @@
             for r in range(8):
                 d, m = divmod(r, 2)
                 out = mate if m else own
-                out[pl.ds((where[3] + d) % 4, 1)] = part[r * ROWS : (r + 1) * ROWS].reshape(1, ROWS, E)
-
-
-def add_body(a, b, out):
-    out[...] = a[...] + b[...]
-
-
-def raw_grad_body(raw, got, loss, out):
+                out[d] = part[r * ROWS : (r + 1) * ROWS]
+
+
+def add_body(a, b, *outs):
+    for d, out in enumerate(outs):
+        out[...] = a[d] + b[d]
+
+
+def raw_grad_body(raw, g0, g1, g2, g3, loss, out):
     total = raw[...]
     length = jnp.sqrt(jnp.sum(total * total, axis=1, keepdims=True) + 1e-06)
     unit = total / length
-    grad = got[0]
-    for i in range(1, 4):
-        grad = grad + got[i]
+    grad = g0[...] + g1[...] + g2[...] + g3[...]
     grad = grad / (TOTAL * sharpness)
     along = jnp.sum(unit * grad, axis=1, keepdims=True)
     out[:ROWS, :] = ((grad - unit * along) / length).astype(bf16)
@@ -309,16 +308,12 @@
     def _():
         acc[...] = part
 
-    @pl.when(step > 0)
-    def _():
-        acc[...] += part
-
-    @pl.when(step == 3)
+    @pl.when(step == 1)
     def _():
         k = math.sqrt(2.0 / math.pi)
         n = 256
         for low in range(0, 8 * ROWS, n):
-            v = acc[low : low + n, :]
+            v = acc[low : low + n, :] + part[low : low + n, :]
             t = jnp.tanh(k * (v + 0.044715 * (v * v * v)))
             hidden[:, low : low + n] = (v * (0.5 * (1.0 + t))).astype(bf16).T
             rise = k * (1.0 + 3 * 0.044715 * (v * v))
@@ -350,9 +345,9 @@
 
     first = dot(turned[:, :rows], pool_a[...]) + dot(turned[:, rows:], pool_b[...])
     first = first.astype(bf16)
-    for i in range(2):
+    for i in range(4):
         out[i, :U, :] = first[:, i * 256 : (i + 1) * 256]
-        out[i, U:, :] = second[pl.ds(pl.multiple_of(step * 64 + i * 32, 32), 32), :]
+        out[i, U:, :] = second[pl.ds(pl.multiple_of(step * 128 + i * 32, 32), 32), :]
 
 
 def piece_body(got, out):
@@ -367,7 +362,7 @@
 
 
 def final_body(got, first, second):
-    for i in range(2):
+    for i in range(4):
         first[i * 256 : (i + 1) * 256, :] = got[i, :U, :].astype(f32)
         second[i * 32 : (i + 1) * 32, :] = got[i, U:, :].astype(f32)
 
@@ -442,13 +437,13 @@
                 far_sds((8 * ROWS, C), bf16),
             ),
             *[kept(p) for p in pools], kept(w_first),
-            grid=(4,),
-            in_specs=[pl.BlockSpec((p.shape[0], 512), lambda j: (0, j)) for p in pools]
-            + [pl.BlockSpec((512, U), lambda j: (j, 0))],
+            grid=(2,),
+            in_specs=[pl.BlockSpec((p.shape[0], 1024), lambda j: (0, j)) for p in pools]
+            + [pl.BlockSpec((1024, U), lambda j: (j, 0))],
             out_specs=[
                 pl.BlockSpec((U, 8 * ROWS), lambda j: (0, 0)),
                 pl.BlockSpec((U, 8 * ROWS), lambda j: (0, 0)),
-                pl.BlockSpec((8 * ROWS, 512), lambda j: (0, j)),
+                pl.BlockSpec((8 * ROWS, 1024), lambda j: (0, j)),
             ],
             scratch=[pltpu.VMEM((8 * ROWS, U), f32)],
             flops=2 * 10**9,
@@ -492,25 +487,22 @@
         ],
         flops=3 * 10**9,
     )
-    grads = kernel(add_body, far_sds((4, ROWS, E), f32), grads, swap(mate_grads))
-    mine = exchange(grads, "y")
-    raw_grad = kernel(raw_grad_body, sds((ROWS + 16, E), bf16), kept(raw), mine, loss)
-    z_grad = along_z(raw_grad)
-
-    def ring_of(block):
-        core = [block] + [along_y(block, -d) for d in (1, 2, 3)]
-        return core + [swap(r) for r in core]
-
-    ring = ring_of(raw_grad) + ring_of(z_grad)
+    grads = kernel(add_body, (key_part,) * 4, grads, swap(mate_grads))
+    mine = [grads[0]] + [along_y(grads[d], d) for d in (1, 2, 3)]
+    raw_grad = kernel(raw_grad_body, sds((ROWS + 16, E), bf16), kept(raw), *mine, loss)
+    ring = [raw_grad] + [along_y(raw_grad, -d) for d in (1, 2, 3)]
+    zring = [along_z(raw_grad)] + [along_z(r) for r in ring[1:]]
+    ring = ring + [swap(r) for r in ring]
+    ring = ring + zring + [swap(r) for r in zring]
     ring_spec = pl.BlockSpec((ROWS + 16, E), lambda j: (0, 0))
     send, loss_all = kernel(
         head_body,
         (sds((8, U + 32, E), bf16), sds((1, 128), f32)),
         kept(joined_a), kept(joined_b), kept(hidden_a), kept(hidden_b), kept(slope_a), kept(slope_b), kept(w_second), *ring,
-        grid=(4,),
+        grid=(2,),
         in_specs=[
-            pl.BlockSpec((8 * ROWS, 512), lambda j: (0, j)),
-            pl.BlockSpec((8 * ROWS, 512), lambda j: (0, j)),
+            pl.BlockSpec((8 * ROWS, 1024), lambda j: (0, j)),
+            pl.BlockSpec((8 * ROWS, 1024), lambda j: (0, j)),
             pl.BlockSpec((U, 8 * ROWS), lambda j: (0, 0)),
             pl.BlockSpec((U, 8 * ROWS), lambda j: (0, 0)),
             pl.BlockSpec((U, 8 * ROWS), lambda j: (0, 0)),
@@ -519,7 +511,7 @@
         ]
         + [ring_spec] * 16,
         out_specs=[
-            pl.BlockSpec((2, U + 32, E), lambda j: (j, 0, 0)),
+            pl.BlockSpec((4, U + 32, E), lambda j: (j, 0, 0)),
             pl.BlockSpec((1, 128), lambda j: (0, 0)),
         ],
         scratch=[
@@ -536,11 +528,11 @@
         final_body,
         (sds((C, U), f32), sds((U, E), f32)),
         whole,
-        grid=(4,),
-        in_specs=[pl.BlockSpec((2, U + 32, E), lambda j: (j, 0, 0))],
+        grid=(2,),
+        in_specs=[pl.BlockSpec((4, U + 32, E), lambda j: (j, 0, 0))],
         out_specs=[
-            pl.BlockSpec((512, U), lambda j: (j, 0)),
-            pl.BlockSpec((64, E), lambda j: (j, 0)),
+            pl.BlockSpec((1024, U), lambda j: (j, 0)),
+            pl.BlockSpec((128, E), lambda j: (j, 0)),
         ],
     )
     return (loss_all[0, 0], first, second)

time: 218 us -> 225 us (1.032)
  waiting for transfers between devices: 71.2 us -> 79 us
  Pallas kernels: 46.8 us -> 42.1 us
    ppermute x21, waiting for transfers between devices: 32.6 us -> 47.5 us  [along_y(): return lax.ppermute(block, 'y', [(i, (i + distance) % 4) for i in range(4)])]
    all_to_all x3 -> x2, waiting for transfers between devices: 9.79 us -> 0.01 us  [exchange(): return lax.all_to_all(array, axis, 0, 0, tiled=True)]
    pallas_call x16, Pallas kernels: 46.8 us -> 42.1 us  [kernel(): pl.pallas_call(body, out_shape=outs, scratch_shapes=list(scratch), compil...]
    all_to_all x3 -> x2, starting transfers between devices: 15.4 us -> 12.2 us  [exchange(): return lax.all_to_all(array, axis, 0, 0, tiled=True)]
    ppermute x21, starting transfers between devices: 22 us -> 25.2 us  [along_y(): return lax.ppermute(block, 'y', [(i, (i + distance) % 4) for i in range(4)])]
    ppermute x7 -> x10, waiting for transfers between devices: 26.3 us -> 28.9 us  [along_z(): return lax.ppermute(block, ZC, pairs)]
    ppermute x7 -> x10, starting transfers between devices: 8.38 us -> 8.71 us  [along_z(): return lax.ppermute(block, ZC, pairs)]
  transfers between devices with their start and end apart: 52 -> 54, of which waited for: 18 -> 24; matrix products, arithmetic and copies ran while one was open for 0% -> 0% of each run, Pallas kernels for 17% -> 15%
where the time goes in v4:
time: 225 us; the launch traced here: 222 us
  waiting for transfers between devices  79 us (35%)
  starting transfers between devices  54.7 us (24%)
  blocking collectives  43.7 us (19%)
  Pallas kernels  42.1 us (19%)
    ppermute x21, waiting for transfers between devices, along_y(): return lax.ppermute(block, 'y', [(i, (i + distance) % 4) for i in range(4)])  47.5 us
    all_to_all x2, blocking collectives, exchange(): return lax.all_to_all(array, axis, 0, 0, tiled=True)  43.7 us
    pallas_call x16, Pallas kernels, kernel(): pl.pallas_call(body, out_shape=outs, scratch_shapes=list(scratch), compil...  42.1 us
    ppermute x10, waiting for transfers between devices, along_z(): return lax.ppermute(block, ZC, pairs)  28.9 us
    ppermute x21, starting transfers between devices, along_y(): return lax.ppermute(block, 'y', [(i, (i + distance) % 4) for i in range(4)])  25.2 us
    all_to_all x2, starting transfers between devices, exchange(): return lax.all_to_all(array, axis, 0, 0, tiled=True)  12.2 us
    ppermute x10, starting transfers between devices, along_z(): return lax.ppermute(block, ZC, pairs)  8.71 us
    ppermute x21, starting transfers between devices, swap(): return lax.ppermute(block, 'c', [(0, 1), (1, 0)])  8.58 us
  transfers between devices with their start and end apart: 54, of which 24 were waited for; matrix products, arithmetic and copies ran while one was open for 0% of the time, Pallas kernels for 15%

profile of v4, /device:TPU:6, one launch (start us, length us, event | category | flops | bytes accessed | tf_op | source)
XLA Modules:
  0.0 222.3 jit_solution(7759785542728617044)
XLA Ops:
  0.6 2.0 collective-permute-start.4
  2.6 1.7 collective-permute-start.5
  4.3 13.4 %collective-permute-done.4.refs_1_ = bf16[2048,256]{1,0:T(8,128)(2,1)S(1)} collective-permute-done((bf16[2048,256]{1,0:T(8,128)(2,1)}, bf16[2048,256]{1,0:T(8,128)(2,1)S(1)}, u32[]{:S(2)}, u32[]{:S(2)}) %collective-permute-start.4) | collective-permute-done | bytes 1048608 | tf_op jit(solution)/shard_map/ppermute | solution.py:77
  18.4 2.8 %shard_map.76 = (bf16[64,2048]{1,0:T(8,128)(2,1)S(1)}, bf16[64,2048]{1,0:T(8,128)(2,1)S(1)}) custom-call(bf16[1024,2048]{1,0:T(8,128)(2,1)} %bitcast.12, s32[1,128]{1,0:T(1,128)S(1)} %bitcast.10), custom_call_target="tpu_custom_call" | custom-call | flops 100000000 | tf_op jit(solution)/shard_map/pallas_call | solution.py:54
  21.2 3.1 %collective-permute-start = (bf16[64,2048]{1,0:T(8,128)(2,1)S(1)}, bf16[64,2048]{1,0:T(8,128)(2,1)S(1)}, u32[]{:S(2)}, u32[]{:S(2)}) collective-permute-start(bf16[64,2048]{1,0:T(8,128)(2,1)S(1)} %get-tuple-element.36.a0), channel_id=1, source_target_pairs={{0,6},{2,0},{4,2},{6,4},{1,7},{3,1},{5,3},{7,5},{8,14},{10,8},{12,... | collective-permute-start | bytes 786440 | tf_op jit(solution)/shard_map/ppermute | solution.py:65
  24.3 2.0 collective-permute-start.8
  26.3 4.2 %collective-permute-done.7.refs_5_ = bf16[256,256]{1,0:T(8,128)(2,1)S(1)} collective-permute-done((bf16[256,256]{1,0:T(8,128)(2,1)S(1)}, bf16[256,256]{1,0:T(8,128)(2,1)S(1)}, u32[]{:S(2)}, u32[]{:S(2)}) %collective-permute-start.7) | collective-permute-done | bytes 131104 | tf_op jit(solution)/shard_map/ppermute | solution.py:77
  32.6 4.3 %collective-permute-done.1.b1 = bf16[64,2048]{1,0:T(8,128)(2,1)S(1)} collective-permute-done((bf16[64,2048]{1,0:T(8,128)(2,1)S(1)}, bf16[64,2048]{1,0:T(8,128)(2,1)S(1)}, u32[]{:S(2)}, u32[]{:S(2)}) %collective-permute-start.1) | collective-permute-done | bytes 262176 | tf_op jit(solution)/shard_map/ppermute | solution.py:65
  36.9 4.6 %collective-permute-done.2.a3 = bf16[64,2048]{1,0:T(8,128)(2,1)S(1)} collective-permute-done((bf16[64,2048]{1,0:T(8,128)(2,1)S(1)}, bf16[64,2048]{1,0:T(8,128)(2,1)S(1)}, u32[]{:S(2)}, u32[]{:S(2)}) %collective-permute-start.2) | collective-permute-done | bytes 262176 | tf_op jit(solution)/shard_map/ppermute | solution.py:65
  41.7 5.3 %collective-permute-done.3.b3 = bf16[64,2048]{1,0:T(8,128)(2,1)S(1)} collective-permute-done((bf16[64,2048]{1,0:T(8,128)(2,1)S(1)}, bf16[64,2048]{1,0:T(8,128)(2,1)S(1)}, u32[]{:S(2)}, u32[]{:S(2)}) %collective-permute-start.3) | collective-permute-done | bytes 262176 | tf_op jit(solution)/shard_map/ppermute | solution.py:65
  47.0 3.9 %shard_map.77 = (bf16[384,2048]{1,0:T(8,128)(2,1)}, bf16[256,2048]{1,0:T(8,128)(2,1)}, f32[128,256]{1,0:T(8,128)S(1)}, f32[128,256]{1,0:T(8,128)S(1)}, f32[128,256]{1,0:T(8,128)S(1)}) custom-call(bf16[64,2048]{1,0:T(8,128)(2,1)S(1)} %get-tuple-element.36.a0, bf16[64,2048]{1,0:T(8,128)(2,1)S(1)} %get-tuple-element.37.b0, ...), custom_call_target="tpu_custom_call" | custom-call | flops 2000000000 | tf_op jit(solution)/shard_map/pallas_call | solution.py:54
  50.9 2.0 collective-permute-start.22
  52.9 1.6 collective-permute-done.11.b2
  54.6 1.8 shard_map.78
  56.5 3.2 %collective-permute-start.24 = (f32[128,256]{1,0:T(8,128)S(1)}, f32[128,256]{1,0:T(8,128)S(1)}, u32[]{:S(2)}, u32[]{:S(2)}) collective-permute-start(f32[128,256]{1,0:T(8,128)S(1)} %get-tuple-element.50), channel_id=1, source_target_pairs={{0,6},{2,0},{4,2},{6,4},{1,7},{3,1},{5,3},{7,5},{8,14},{10,8},{12,... | collective-permute-start | bytes 393224 | tf_op jit(solution)/shard_map/ppermute | solution.py:65
  59.7 3.2 %collective-permute-done.23.p2 = f32[128,256]{1,0:T(8,128)S(1)} collective-permute-done((f32[128,256]{1,0:T(8,128)S(1)}, f32[128,256]{1,0:T(8,128)S(1)}, u32[]{:S(2)}, u32[]{:S(2)}) %collective-permute-start.23) | collective-permute-done | bytes 131104 | tf_op jit(solution)/shard_map/ppermute | solution.py:65
  64.1 5.0 %all-to-all-start = ((bf16[16,128,256]{2,1,0:T(8,128)(2,1)}), bf16[16,128,256]{2,1,0:T(8,128)(2,1)S(1)}, u32[]{:S(2)}, u32[]{:S(2)}) async-start(bf16[16,128,256]{2,1,0:T(8,128)(2,1)} %get-tuple-element.53), calls=%async_computation | async-start | bytes 2097152 | tf_op jit(solution)/shard_map/all_to_all | solution.py:81
  69.1 1.3 collective-permute-done.25.mate
  70.4 2.8 %collective-permute-start.26 = (bf16[256,384]{1,0:T(8,128)(2,1)S(1)}, bf16[256,384]{1,0:T(8,128)(2,1)S(1)}, u32[]{:S(2)}, u32[]{:S(2)}) collective-permute-start(bf16[256,384]{1,0:T(8,128)(2,1)S(1)} %shard_map.82.pay0), channel_id=1, source_target_pairs={{0,6},{2,0},{4,2},{6,4},{1,7},{3,1},{5,3},{7,5},{8,14},{10,8},{12,... | collective-permute-start | bytes 589832 | tf_op jit(solution)/shard_map/ppermute | solution.py:65
  74.3 1.5 collective-permute-start.16
  75.9 6.1 %collective-permute-done.26.pay1 = bf16[256,384]{1,0:T(8,128)(2,1)S(1)} collective-permute-done((bf16[256,384]{1,0:T(8,128)(2,1)S(1)}, bf16[256,384]{1,0:T(8,128)(2,1)S(1)}, u32[]{:S(2)}, u32[]{:S(2)}) %collective-permute-start.26) | collective-permute-done | bytes 196640 | tf_op jit(solution)/shard_map/ppermute | solution.py:65
  82.5 3.0 %collective-permute-done.28.pay3 = bf16[256,384]{1,0:T(8,128)(2,1)S(1)} collective-permute-done((bf16[256,384]{1,0:T(8,128)(2,1)S(1)}, bf16[256,384]{1,0:T(8,128)(2,1)S(1)}, u32[]{:S(2)}, u32[]{:S(2)}) %collective-permute-start.28) | collective-permute-done | bytes 196640 | tf_op jit(solution)/shard_map/ppermute | solution.py:65
  85.5 3.7 %shard_map.83 = (f32[8,128]{1,0:T(8,128)S(1)}, f32[16,1,2176]{2,1,0:T(1,128)}, bf16[1024,256]{1,0:T(8,128)(2,1)}, f32[1024,128]{1,0:T(8,128)}) custom-call(s32[5]{0:T(128)S(1)} %stack.23.where, bf16[256,384]{1,0:T(8,128)(2,1)S(1)} %shard_map.82.pay0, bf16[256,384]{1,0:T(8,128)(2,1)S(1)} %collective-permute-done.26.pay1, ...), custom_call_target="tpu_custom_call" | custom-call | flops 1000000000 | tf_op jit(solution)/shard_map/pallas_call | solution.py:54
  89.3 7.2 %all-to-all-start.1 = ((f32[16,1,2176]{2,1,0:T(1,128)}), f32[16,1,2176]{2,1,0:T(1,128)S(1)}, u32[]{:S(2)}, u32[]{:S(2)}) async-start(f32[16,1,2176]{2,1,0:T(1,128)} %get-tuple-element.57), calls=%async_computation.1 | async-start | bytes 278528 | tf_op jit(solution)/shard_map/all_to_all | solution.py:81
  99.7 1.6 collective-permute-done.30.sum1
  101.3 2.2 %collective-permute-done.31.sum2 = f32[8,128]{1,0:T(8,128)S(1)} collective-permute-done((f32[8,128]{1,0:T(8,128)S(1)}, f32[8,128]{1,0:T(8,128)S(1)}, u32[]{:S(2)}, u32[]{:S(2)}) %collective-permute-start.31) | collective-permute-done | bytes 4128 | tf_op jit(solution)/shard_map/ppermute | solution.py:65
  104.2 6.9 %shard_map.86 = (f32[4,128,256]{2,1,0:T(8,128)S(1)}, f32[4,128,256]{2,1,0:T(8,128)S(1)}, f32[1,128]{1,0:T(1,128)}) custom-call(s32[5]{0:T(128)S(1)} %stack.23.where, bf16[1024,256]{1,0:T(8,128)(2,1)} %get-tuple-element.54.tile, f32[1024,128]{1,0:T(8,128)} %get-tuple-element.55.who, bf16[16,128,256]{2,1,0:T(8,128)(2,1)} %copy-done.1, ...), custom_call_target="tpu_custom_call" | custom-call | flops 3000000000 | tf_op jit(solution)/shard_map/pallas_call | solution.py:54
  111.1 1.5 collective-permute-start.14
  112.6 1.5 collective-permute-start.17
  114.1 4.7 %collective-permute-done.14.refs_0_ = bf16[64,2048]{1,0:T(8,128)(2,1)S(1)} collective-permute-done((bf16[64,2048]{1,0:T(8,128)(2,1)S(1)}, bf16[64,2048]{1,0:T(8,128)(2,1)S(1)}, u32[]{:S(2)}, u32[]{:S(2)}) %collective-permute-start.14) | collective-permute-done | bytes 262176 | tf_op jit(solution)/shard_map/ppermute | solution.py:77
  119.0 1.5 collective-permute-start.18
  120.6 6.5 %collective-permute-done.15.refs_1_ = bf16[64,2048]{1,0:T(8,128)(2,1)S(1)} collective-permute-done((bf16[64,2048]{1,0:T(8,128)(2,1)S(1)}, bf16[64,2048]{1,0:T(8,128)(2,1)S(1)}, u32[]{:S(2)}, u32[]{:S(2)}) %collective-permute-start.15) | collective-permute-done | bytes 262176 | tf_op jit(solution)/shard_map/ppermute | solution.py:77
  128.0 2.6 %collective-permute-start.35 = (f32[128,256]{1,0:T(8,128)S(1)}, f32[128,256]{1,0:T(8,128)S(1)}, u32[]{:S(2)}, u32[]{:S(2)}) collective-permute-start(f32[128,256]{1,0:T(8,128)S(1)} %get-tuple-element.62), channel_id=1, source_target_pairs={{0,4},{2,6},{4,0},{6,2},{1,5},{3,7},{5,1},{7,3},{8,12},{10,14},{12... | collective-permute-start | bytes 393224 | tf_op jit(solution)/shard_map/ppermute | solution.py:65
  130.6 3.4 %collective-permute-done.34.g1 = f32[128,256]{1,0:T(8,128)S(1)} collective-permute-done((f32[128,256]{1,0:T(8,128)S(1)}, f32[128,256]{1,0:T(8,128)S(1)}, u32[]{:S(2)}, u32[]{:S(2)}) %collective-permute-start.34) | collective-permute-done | bytes 131104 | tf_op jit(solution)/shard_map/ppermute | solution.py:65
  134.0 1.4 collective-permute-done.35.g2
  135.4 1.4 collective-permute-start.36
  136.9 3.6 %collective-permute-done.36.g3 = f32[128,256]{1,0:T(8,128)S(1)} collective-permute-done((f32[128,256]{1,0:T(8,128)S(1)}, f32[128,256]{1,0:T(8,128)S(1)}, u32[]{:S(2)}, u32[]{:S(2)}) %collective-permute-start.36) | collective-permute-done | bytes 131104 | tf_op jit(solution)/shard_map/ppermute | solution.py:65
  142.2 2.7 %collective-permute-start.37 = (bf16[144,256]{1,0:T(8,128)(2,1)S(1)}, bf16[144,256]{1,0:T(8,128)(2,1)S(1)}, u32[]{:S(2)}, u32[]{:S(2)}) collective-permute-start(bf16[144,256]{1,0:T(8,128)(2,1)S(1)} %shard_map.88.refs_0_), channel_id=1, source_target_pairs={{0,6},{2,0},{4,2},{6,4},{1,7},{3,1},{5,3},{7,5},{8,14},{10,8},{12,... | collective-permute-start | bytes 221192 | tf_op jit(solution)/shard_map/ppermute | solution.py:65
  145.9 2.8 %collective-permute-done.37.refs_1_ = bf16[144,256]{1,0:T(8,128)(2,1)S(1)} collective-permute-done((bf16[144,256]{1,0:T(8,128)(2,1)S(1)}, bf16[144,256]{1,0:T(8,128)(2,1)S(1)}, u32[]{:S(2)}, u32[]{:S(2)}) %collective-permute-start.37) | collective-permute-done | bytes 73760 | tf_op jit(solution)/shard_map/ppermute | solution.py:65
  148.7 2.8 %collective-permute-done.38.refs_2_ = bf16[144,256]{1,0:T(8,128)(2,1)S(1)} collective-permute-done((bf16[144,256]{1,0:T(8,128)(2,1)S(1)}, bf16[144,256]{1,0:T(8,128)(2,1)S(1)}, u32[]{:S(2)}, u32[]{:S(2)}) %collective-permute-start.38) | collective-permute-done | bytes 73760 | tf_op jit(solution)/shard_map/ppermute | solution.py:65
  152.5 1.7 collective-permute-start.42
  154.3 1.8 collective-permute-start.47
  156.1 5.9 %shard_map.79 = (bf16[256,1024]{1,0:T(8,128)(2,1)}, f32[256,1024]{1,0:T(8,128)}, bf16[1024,2048]{1,0:T(8,128)(2,1)}) custom-call(bf16[384,2048]{1,0:T(8,128)(2,1)} %get-tuple-element.38.refs_0_, bf16[128,2048]{1,0:T(8,128)(2,1)} %get-tuple-element.39.refs_1_, bf16[384,2048]{1,0:T(8,128)(2,1)} %collective-permute-done.12.refs_2_, ...), custom_call_target="tpu_custom_call" | custom-call | flops 2000000000 | tf_op jit(solution)/shard_map/pallas_call | solution.py:54
  164.2 5.9 %shard_map.80 = (bf16[256,1024]{1,0:T(8,128)(2,1)}, f32[256,1024]{1,0:T(8,128)}, bf16[1024,2048]{1,0:T(8,128)(2,1)}) custom-call(bf16[64,2048]{1,0:T(8,128)(2,1)} %copy-done.12, bf16[64,2048]{1,0:T(8,128)(2,1)} %copy-done.13, bf16[256,2048]{1,0:T(8,128)(2,1)} %copy-done.6, bf16[128,2048]{1,0:T(8,128)(2,1)} %copy-done.9, bf16[64,2048]{1,0:T(8,128)(2,1)} %copy-done.14, ...), custom_call_target="tpu_custom_call" | custom-call | flops 2000000000 | tf_op jit(solution)/shard_map/pallas_call | solution.py:54
  170.2 6.7 %shard_map.89 = (bf16[8,288,256]{2,1,0:T(8,128)(2,1)S(1)}, f32[1,128]{1,0:T(1,128)}) custom-call(bf16[1024,2048]{1,0:T(8,128)(2,1)} %get-tuple-element.40.pool_a, bf16[1024,2048]{1,0:T(8,128)(2,1)} %get-tuple-element.42.pool_b, bf16[256,1024]{1,0:T(8,128)(2,1)} %get-tuple-element.43.hidden_a, bf16[256,1024]{1,0:T(8,128)(2,1)} %get-tuple-element.44.hidden_b, ...), custom_call_target="tpu_custom_call" | custom-call | flops 2000000000 | tf_op jit(solution)/shard_map/pallas_call | solution.py:54
  176.9 23.4 %all_to_all.20.got = bf16[8,288,256]{2,1,0:T(8,128)(2,1)S(1)} all-to-all(bf16[8,288,256]{2,1,0:T(8,128)(2,1)S(1)} %get-tuple-element.66), channel_id=1, replica_groups=mesh['x'=4,'zh'=2,'zl'=2,'y'=4,'c'=2] {'x','zh'}, dimensions={0} | all-to-all | bytes 2359296 | tf_op jit(solution)/shard_map/all_to_all | solution.py:81
  200.6 20.3 %all_to_all.21.got = bf16[8,288,256]{2,1,0:T(8,128)(2,1)S(1)} all-to-all(bf16[8,288,256]{2,1,0:T(8,128)(2,1)S(1)} %shard_map.90), channel_id=1, replica_groups=mesh['x'=4,'zh'=2,'zl'=2,'y'=4,'c'=2] {'x','zh'}, dimensions={0} | all-to-all | bytes 2359296 | tf_op jit(solution)/shard_map/all_to_all | solution.py:81
  220.9 1.5 shard_map.91
  (111 shorter events, 17.4 us)
Async XLA Ops:
  0.6 17.1 %collective-permute-start.4 = (bf16[2048,256]{1,0:T(8,128)(2,1)}, bf16[2048,256]{1,0:T(8,128)(2,1)S(1)}, u32[]{:S(2)}, u32[]{:S(2)}) collective-permute-start(bf16[2048,256]{1,0:T(8,128)(2,1)} %refs_8_.1), channel_id=1, source_target_pairs={{0,8},{1,25},{8,16},{9,1},{16,24},{17,9},{24,0},{25,17},{2,10},{3,... | collective-permute-start | bytes 3145736 | tf_op jit(solution)/shard_map/ppermute | solution.py:77
  2.6 44.4 %collective-permute-start.5 = (bf16[2048,256]{1,0:T(8,128)(2,1)}, bf16[2048,256]{1,0:T(8,128)(2,1)S(1)}, u32[]{:S(2)}, u32[]{:S(2)}) collective-permute-start(bf16[2048,256]{1,0:T(8,128)(2,1)} %refs_8_.1), channel_id=1, source_target_pairs={{0,1},{1,0},{2,3},{3,2},{4,5},{5,4},{6,7},{7,6},{8,9},{9,8},{10,11... | collective-permute-start | bytes 3145736 | tf_op jit(solution)/shard_map/ppermute | solution.py:69
  17.7 29.2 %collective-permute-start.6 = (bf16[2048,256]{1,0:T(8,128)(2,1)S(1)}, bf16[2048,256]{1,0:T(8,128)(2,1)S(1)}, u32[]{:S(2)}, u32[]{:S(2)}) collective-permute-start(bf16[2048,256]{1,0:T(8,128)(2,1)S(1)} %collective-permute-done.4.refs_1_), channel_id=1, source_target_pairs={{0,1},{1,0},{2,3},{3,2},{4,5},{5,4},{6,7},{7,6},{8,9},{9,8},{10,11... | collective-permute-start | bytes 3145736 | tf_op jit(solution)/shard_map/ppermute | solution.py:69
  21.2 11.3 %collective-permute-start = (bf16[64,2048]{1,0:T(8,128)(2,1)S(1)}, bf16[64,2048]{1,0:T(8,128)(2,1)S(1)}, u32[]{:S(2)}, u32[]{:S(2)}) collective-permute-start(bf16[64,2048]{1,0:T(8,128)(2,1)S(1)} %get-tuple-element.36.a0), channel_id=1, source_target_pairs={{0,6},{2,0},{4,2},{6,4},{1,7},{3,1},{5,3},{7,5},{8,14},{10,8},{12,... | collective-permute-start | bytes 786440 | tf_op jit(solution)/shard_map/ppermute | solution.py:65
  24.3 6.2 %collective-permute-start.7 = (bf16[256,256]{1,0:T(8,128)(2,1)S(1)}, bf16[256,256]{1,0:T(8,128)(2,1)S(1)}, u32[]{:S(2)}, u32[]{:S(2)}) collective-permute-start(bf16[256,256]{1,0:T(8,128)(2,1)S(1)} %copy-done.2), channel_id=1, source_target_pairs={{0,8},{1,25},{8,16},{9,1},{16,24},{17,9},{24,0},{25,17},{2,10},{3,... | collective-permute-start | bytes 393224 | tf_op jit(solution)/shard_map/ppermute | solution.py:77
  24.3 6.9 %collective-permute-start.8 = (bf16[256,256]{1,0:T(8,128)(2,1)S(1)}, bf16[256,256]{1,0:T(8,128)(2,1)S(1)}, u32[]{:S(2)}, u32[]{:S(2)}) collective-permute-start(bf16[256,256]{1,0:T(8,128)(2,1)S(1)} %copy-done.2), channel_id=1, source_target_pairs={{0,1},{1,0},{2,3},{3,2},{4,5},{5,4},{6,7},{7,6},{8,9},{9,8},{10,11... | collective-permute-start | bytes 393224 | tf_op jit(solution)/shard_map/ppermute | solution.py:69
  30.5 6.4 %collective-permute-start.1 = (bf16[64,2048]{1,0:T(8,128)(2,1)S(1)}, bf16[64,2048]{1,0:T(8,128)(2,1)S(1)}, u32[]{:S(2)}, u32[]{:S(2)}) collective-permute-start(bf16[64,2048]{1,0:T(8,128)(2,1)S(1)} %get-tuple-element.37.b0), channel_id=1, source_target_pairs={{0,6},{2,0},{4,2},{6,4},{1,7},{3,1},{5,3},{7,5},{8,14},{10,8},{12,... | collective-permute-start | bytes 786440 | tf_op jit(solution)/shard_map/ppermute | solution.py:65
  31.2 10.2 %collective-permute-start.2 = (bf16[64,2048]{1,0:T(8,128)(2,1)S(1)}, bf16[64,2048]{1,0:T(8,128)(2,1)S(1)}, u32[]{:S(2)}, u32[]{:S(2)}) collective-permute-start(bf16[64,2048]{1,0:T(8,128)(2,1)S(1)} %get-tuple-element.36.a0), channel_id=1, source_target_pairs={{0,2},{2,4},{4,6},{6,0},{1,3},{3,5},{5,7},{7,1},{8,10},{10,12},{12... | collective-permute-start | bytes 786440 | tf_op jit(solution)/shard_map/ppermute | solution.py:65
  32.5 14.4 %collective-permute-start.3 = (bf16[64,2048]{1,0:T(8,128)(2,1)S(1)}, bf16[64,2048]{1,0:T(8,128)(2,1)S(1)}, u32[]{:S(2)}, u32[]{:S(2)}) collective-permute-start(bf16[64,2048]{1,0:T(8,128)(2,1)S(1)} %get-tuple-element.37.b0), channel_id=1, source_target_pairs={{0,2},{2,4},{4,6},{6,0},{1,3},{3,5},{5,7},{7,1},{8,10},{10,12},{12... | collective-permute-start | bytes 786440 | tf_op jit(solution)/shard_map/ppermute | solution.py:65
  36.9 10.1 %collective-permute-start.9 = (bf16[256,256]{1,0:T(8,128)(2,1)S(1)}, bf16[256,256]{1,0:T(8,128)(2,1)S(1)}, u32[]{:S(2)}, u32[]{:S(2)}) collective-permute-start(bf16[256,256]{1,0:T(8,128)(2,1)S(1)} %collective-permute-done.7.refs_5_), channel_id=1, source_target_pairs={{0,1},{1,0},{2,3},{3,2},{4,5},{5,4},{6,7},{7,6},{8,9},{9,8},{10,11... | collective-permute-start | bytes 393224 | tf_op jit(solution)/shard_map/ppermute | solution.py:69
  41.5 11.5 %collective-permute-start.10 = (bf16[64,2048]{1,0:T(8,128)(2,1)S(1)}, bf16[64,2048]{1,0:T(8,128)(2,1)S(1)}, u32[]{:S(2)}, u32[]{:S(2)}) collective-permute-start(bf16[64,2048]{1,0:T(8,128)(2,1)S(1)} %collective-permute-done.2.a3), channel_id=1, source_target_pairs={{0,2},{2,4},{4,6},{6,0},{1,3},{3,5},{5,7},{7,1},{8,10},{10,12},{12... | collective-permute-start | bytes 786440 | tf_op jit(solution)/shard_map/ppermute | solution.py:65
  47.0 7.6 %collective-permute-start.11 = (bf16[64,2048]{1,0:T(8,128)(2,1)S(1)}, bf16[64,2048]{1,0:T(8,128)(2,1)S(1)}, u32[]{:S(2)}, u32[]{:S(2)}) collective-permute-start(bf16[64,2048]{1,0:T(8,128)(2,1)S(1)} %collective-permute-done.1.b1), channel_id=1, source_target_pairs={{0,6},{2,0},{4,2},{6,4},{1,7},{3,1},{5,3},{7,5},{8,14},{10,8},{12,... | collective-permute-start | bytes 786440 | tf_op jit(solution)/shard_map/ppermute | solution.py:65
  50.9 8.8 %collective-permute-start.22 = (f32[128,256]{1,0:T(8,128)S(1)}, f32[128,256]{1,0:T(8,128)S(1)}, u32[]{:S(2)}, u32[]{:S(2)}) collective-permute-start(f32[128,256]{1,0:T(8,128)S(1)} %get-tuple-element.48), channel_id=1, source_target_pairs={{0,2},{2,4},{4,6},{6,0},{1,3},{3,5},{5,7},{7,1},{8,10},{10,12},{12... | collective-permute-start | bytes 393224 | tf_op jit(solution)/shard_map/ppermute | solution.py:65
  56.4 6.5 %collective-permute-start.23 = (f32[128,256]{1,0:T(8,128)S(1)}, f32[128,256]{1,0:T(8,128)S(1)}, u32[]{:S(2)}, u32[]{:S(2)}) collective-permute-start(f32[128,256]{1,0:T(8,128)S(1)} %get-tuple-element.49), channel_id=1, source_target_pairs={{0,4},{2,6},{4,0},{6,2},{1,5},{3,7},{5,1},{7,3},{8,12},{10,14},{12... | collective-permute-start | bytes 393224 | tf_op jit(solution)/shard_map/ppermute | solution.py:65
  56.5 6.4 %collective-permute-start.24 = (f32[128,256]{1,0:T(8,128)S(1)}, f32[128,256]{1,0:T(8,128)S(1)}, u32[]{:S(2)}, u32[]{:S(2)}) collective-permute-start(f32[128,256]{1,0:T(8,128)S(1)} %get-tuple-element.50), channel_id=1, source_target_pairs={{0,6},{2,0},{4,2},{6,4},{1,7},{3,1},{5,3},{7,5},{8,14},{10,8},{12,... | collective-permute-start | bytes 393224 | tf_op jit(solution)/shard_map/ppermute | solution.py:65
  64.1 21.4 %all-to-all-start = ((bf16[16,128,256]{2,1,0:T(8,128)(2,1)}), bf16[16,128,256]{2,1,0:T(8,128)(2,1)S(1)}, u32[]{:S(2)}, u32[]{:S(2)}) async-start(bf16[16,128,256]{2,1,0:T(8,128)(2,1)} %get-tuple-element.53), calls=%async_computation | async-start | bytes 2097152 | tf_op jit(solution)/shard_map/all_to_all | solution.py:81
  70.4 11.6 %collective-permute-start.26 = (bf16[256,384]{1,0:T(8,128)(2,1)S(1)}, bf16[256,384]{1,0:T(8,128)(2,1)S(1)}, u32[]{:S(2)}, u32[]{:S(2)}) collective-permute-start(bf16[256,384]{1,0:T(8,128)(2,1)S(1)} %shard_map.82.pay0), channel_id=1, source_target_pairs={{0,6},{2,0},{4,2},{6,4},{1,7},{3,1},{5,3},{7,5},{8,14},{10,8},{12,... | collective-permute-start | bytes 589832 | tf_op jit(solution)/shard_map/ppermute | solution.py:65
  73.2 9.3 %collective-permute-start.27 = (bf16[256,384]{1,0:T(8,128)(2,1)S(1)}, bf16[256,384]{1,0:T(8,128)(2,1)S(1)}, u32[]{:S(2)}, u32[]{:S(2)}) collective-permute-start(bf16[256,384]{1,0:T(8,128)(2,1)S(1)} %shard_map.82.pay0), channel_id=1, source_target_pairs={{0,4},{2,6},{4,0},{6,2},{1,5},{3,7},{5,1},{7,3},{8,12},{10,14},{12... | collective-permute-start | bytes 589832 | tf_op jit(solution)/shard_map/ppermute | solution.py:65
  73.7 11.8 %collective-permute-start.28 = (bf16[256,384]{1,0:T(8,128)(2,1)S(1)}, bf16[256,384]{1,0:T(8,128)(2,1)S(1)}, u32[]{:S(2)}, u32[]{:S(2)}) collective-permute-start(bf16[256,384]{1,0:T(8,128)(2,1)S(1)} %shard_map.82.pay0), channel_id=1, source_target_pairs={{0,2},{2,4},{4,6},{6,0},{1,3},{3,5},{5,7},{7,1},{8,10},{10,12},{12... | collective-permute-start | bytes 589832 | tf_op jit(solution)/shard_map/ppermute | solution.py:65
  74.3 44.6 %collective-permute-start.16 = (bf16[256,2048]{1,0:T(8,128)(2,1)}, bf16[256,2048]{1,0:T(8,128)(2,1)S(1)}, u32[]{:S(2)}, u32[]{:S(2)}) collective-permute-start(bf16[256,2048]{1,0:T(8,128)(2,1)} %get-tuple-element.41), channel_id=1, source_target_pairs={{0,8},{1,25},{8,16},{9,1},{16,24},{17,9},{24,0},{25,17},{2,10},{3,... | collective-permute-start | bytes 3145736 | tf_op jit(solution)/shard_map/ppermute | solution.py:77
  89.3 14.9 %all-to-all-start.1 = ((f32[16,1,2176]{2,1,0:T(1,128)}), f32[16,1,2176]{2,1,0:T(1,128)S(1)}, u32[]{:S(2)}, u32[]{:S(2)}) async-start(f32[16,1,2176]{2,1,0:T(1,128)} %get-tuple-element.57), calls=%async_computation.1 | async-start | bytes 278528 | tf_op jit(solution)/shard_map/all_to_all | solution.py:81
  98.4 5.1 %collective-permute-start.31 = (f32[8,128]{1,0:T(8,128)S(1)}, f32[8,128]{1,0:T(8,128)S(1)}, u32[]{:S(2)}, u32[]{:S(2)}) collective-permute-start(f32[8,128]{1,0:T(8,128)S(1)} %shard_map.84.sum0), channel_id=1, source_target_pairs={{0,4},{2,6},{4,0},{6,2},{1,5},{3,7},{5,1},{7,3},{8,12},{10,14},{12... | collective-permute-start | bytes 12296 | tf_op jit(solution)/shard_map/ppermute | solution.py:65
  98.8 5.1 %collective-permute-start.32 = (f32[8,128]{1,0:T(8,128)S(1)}, f32[8,128]{1,0:T(8,128)S(1)}, u32[]{:S(2)}, u32[]{:S(2)}) collective-permute-start(f32[8,128]{1,0:T(8,128)S(1)} %shard_map.84.sum0), channel_id=1, source_target_pairs={{0,2},{2,4},{4,6},{6,0},{1,3},{3,5},{5,7},{7,1},{8,10},{10,12},{12... | collective-permute-start | bytes 12296 | tf_op jit(solution)/shard_map/ppermute | solution.py:65
  99.7 46.2 %collective-permute-start.12 = (bf16[384,2048]{1,0:T(8,128)(2,1)}, bf16[384,2048]{1,0:T(8,128)(2,1)}, u32[]{:S(2)}, u32[]{:S(2)}) collective-permute-start(bf16[384,2048]{1,0:T(8,128)(2,1)} %get-tuple-element.38.refs_0_), channel_id=1, source_target_pairs={{0,1},{1,0},{2,3},{3,2},{4,5},{5,4},{6,7},{7,6},{8,9},{9,8},{10,11... | collective-permute-start | bytes 4718600 | tf_op jit(solution)/shard_map/ppermute | solution.py:69
  111.1 9.3 %collective-permute-start.33 = (f32[4,128,256]{2,1,0:T(8,128)S(1)}, f32[4,128,256]{2,1,0:T(8,128)S(1)}, u32[]{:S(2)}, u32[]{:S(2)}) collective-permute-start(f32[4,128,256]{2,1,0:T(8,128)S(1)} %get-tuple-element.59), channel_id=1, source_target_pairs={{0,1},{1,0},{2,3},{3,2},{4,5},{5,4},{6,7},{7,6},{8,9},{9,8},{10,11... | collective-permute-start | bytes 1572872 | tf_op jit(solution)/shard_map/ppermute | solution.py:69
  111.1 7.6 %collective-permute-start.14 = (bf16[64,2048]{1,0:T(8,128)(2,1)S(1)}, bf16[64,2048]{1,0:T(8,128)(2,1)S(1)}, u32[]{:S(2)}, u32[]{:S(2)}) collective-permute-start(bf16[64,2048]{1,0:T(8,128)(2,1)S(1)} %get-tuple-element.36.a0), channel_id=1, source_target_pairs={{0,8},{1,25},{8,16},{9,1},{16,24},{17,9},{24,0},{25,17},{2,10},{3,... | collective-permute-start | bytes 786440 | tf_op jit(solution)/shard_map/ppermute | solution.py:77
  112.6 18.0 %collective-permute-start.17 = (bf16[128,2048]{1,0:T(8,128)(2,1)S(1)}, bf16[128,2048]{1,0:T(8,128)(2,1)S(1)}, u32[]{:S(2)}, u32[]{:S(2)}) collective-permute-start(bf16[128,2048]{1,0:T(8,128)(2,1)S(1)} %copy-done.8), channel_id=1, source_target_pairs={{0,8},{1,25},{8,16},{9,1},{16,24},{17,9},{24,0},{25,17},{2,10},{3,... | collective-permute-start | bytes 1572872 | tf_op jit(solution)/shard_map/ppermute | solution.py:77
  118.7 8.4 %collective-permute-start.15 = (bf16[64,2048]{1,0:T(8,128)(2,1)S(1)}, bf16[64,2048]{1,0:T(8,128)(2,1)S(1)}, u32[]{:S(2)}, u32[]{:S(2)}) collective-permute-start(bf16[64,2048]{1,0:T(8,128)(2,1)S(1)} %get-tuple-element.37.b0), channel_id=1, source_target_pairs={{0,8},{1,25},{8,16},{9,1},{16,24},{17,9},{24,0},{25,17},{2,10},{3,... | collective-permute-start | bytes 786440 | tf_op jit(solution)/shard_map/ppermute | solution.py:77
  119.0 9.0 %collective-permute-start.18 = (bf16[64,2048]{1,0:T(8,128)(2,1)S(1)}, bf16[64,2048]{1,0:T(8,128)(2,1)S(1)}, u32[]{:S(2)}, u32[]{:S(2)}) collective-permute-start(bf16[64,2048]{1,0:T(8,128)(2,1)S(1)} %collective-permute-done.14.refs_0_), channel_id=1, source_target_pairs={{0,1},{1,0},{2,3},{3,2},{4,5},{5,4},{6,7},{7,6},{8,9},{9,8},{10,11... | collective-permute-start | bytes 786440 | tf_op jit(solution)/shard_map/ppermute | solution.py:69
  120.5 42.7 %collective-permute-start.20 = (bf16[256,2048]{1,0:T(8,128)(2,1)S(1)}, bf16[256,2048]{1,0:T(8,128)(2,1)S(1)}, u32[]{:S(2)}, u32[]{:S(2)}) collective-permute-start(bf16[256,2048]{1,0:T(8,128)(2,1)S(1)} %collective-permute-done.16.refs_2_), channel_id=1, source_target_pairs={{0,1},{1,0},{2,3},{3,2},{4,5},{5,4},{6,7},{7,6},{8,9},{9,8},{10,11... | collective-permute-start | bytes 3145736 | tf_op jit(solution)/shard_map/ppermute | solution.py:69
  127.1 6.9 %collective-permute-start.34 = (f32[128,256]{1,0:T(8,128)S(1)}, f32[128,256]{1,0:T(8,128)S(1)}, u32[]{:S(2)}, u32[]{:S(2)}) collective-permute-start(f32[128,256]{1,0:T(8,128)S(1)} %get-tuple-element.61), channel_id=1, source_target_pairs={{0,2},{2,4},{4,6},{6,0},{1,3},{3,5},{5,7},{7,1},{8,10},{10,12},{12... | collective-permute-start | bytes 393224 | tf_op jit(solution)/shard_map/ppermute | solution.py:65
  128.0 7.4 %collective-permute-start.35 = (f32[128,256]{1,0:T(8,128)S(1)}, f32[128,256]{1,0:T(8,128)S(1)}, u32[]{:S(2)}, u32[]{:S(2)}) collective-permute-start(f32[128,256]{1,0:T(8,128)S(1)} %get-tuple-element.62), channel_id=1, source_target_pairs={{0,4},{2,6},{4,0},{6,2},{1,5},{3,7},{5,1},{7,3},{8,12},{10,14},{12... | collective-permute-start | bytes 393224 | tf_op jit(solution)/shard_map/ppermute | solution.py:65
  130.6 14.3 %collective-permute-start.13 = (bf16[128,2048]{1,0:T(8,128)(2,1)S(1)}, bf16[128,2048]{1,0:T(8,128)(2,1)S(1)}, u32[]{:S(2)}, u32[]{:S(2)}) collective-permute-start(bf16[128,2048]{1,0:T(8,128)(2,1)S(1)} %copy-done.8), channel_id=1, source_target_pairs={{0,1},{1,0},{2,3},{3,2},{4,5},{5,4},{6,7},{7,6},{8,9},{9,8},{10,11... | collective-permute-start | bytes 1572872 | tf_op jit(solution)/shard_map/ppermute | solution.py:69
  134.0 10.9 %collective-permute-start.21 = (bf16[128,2048]{1,0:T(8,128)(2,1)S(1)}, bf16[128,2048]{1,0:T(8,128)(2,1)S(1)}, u32[]{:S(2)}, u32[]{:S(2)}) collective-permute-start(bf16[128,2048]{1,0:T(8,128)(2,1)S(1)} %collective-permute-done.17.refs_3_), channel_id=1, source_target_pairs={{0,1},{1,0},{2,3},{3,2},{4,5},{5,4},{6,7},{7,6},{8,9},{9,8},{10,11... | collective-permute-start | bytes 1572872 | tf_op jit(solution)/shard_map/ppermute | solution.py:69
  142.2 6.5 %collective-permute-start.37 = (bf16[144,256]{1,0:T(8,128)(2,1)S(1)}, bf16[144,256]{1,0:T(8,128)(2,1)S(1)}, u32[]{:S(2)}, u32[]{:S(2)}) collective-permute-start(bf16[144,256]{1,0:T(8,128)(2,1)S(1)} %shard_map.88.refs_0_), channel_id=1, source_target_pairs={{0,6},{2,0},{4,2},{6,4},{1,7},{3,1},{5,3},{7,5},{8,14},{10,8},{12,... | collective-permute-start | bytes 221192 | tf_op jit(solution)/shard_map/ppermute | solution.py:65
  144.9 6.6 %collective-permute-start.38 = (bf16[144,256]{1,0:T(8,128)(2,1)S(1)}, bf16[144,256]{1,0:T(8,128)(2,1)S(1)}, u32[]{:S(2)}, u32[]{:S(2)}) collective-permute-start(bf16[144,256]{1,0:T(8,128)(2,1)S(1)} %shard_map.88.refs_0_), channel_id=1, source_target_pairs={{0,4},{2,6},{4,0},{6,2},{1,5},{3,7},{5,1},{7,3},{8,12},{10,14},{12... | collective-permute-start | bytes 221192 | tf_op jit(solution)/shard_map/ppermute | solution.py:65
  145.0 7.3 %collective-permute-start.39 = (bf16[144,256]{1,0:T(8,128)(2,1)S(1)}, bf16[144,256]{1,0:T(8,128)(2,1)S(1)}, u32[]{:S(2)}, u32[]{:S(2)}) collective-permute-start(bf16[144,256]{1,0:T(8,128)(2,1)S(1)} %shard_map.88.refs_0_), channel_id=1, source_target_pairs={{0,2},{2,4},{4,6},{6,0},{1,3},{3,5},{5,7},{7,1},{8,10},{10,12},{12... | collective-permute-start | bytes 221192 | tf_op jit(solution)/shard_map/ppermute | solution.py:65
  145.9 6.6 %collective-permute-start.40 = (bf16[144,256]{1,0:T(8,128)(2,1)S(1)}, bf16[144,256]{1,0:T(8,128)(2,1)S(1)}, u32[]{:S(2)}, u32[]{:S(2)}) collective-permute-start(bf16[144,256]{1,0:T(8,128)(2,1)S(1)} %shard_map.88.refs_0_), channel_id=1, source_target_pairs={{0,1},{1,0},{2,3},{3,2},{4,5},{5,4},{6,7},{7,6},{8,9},{9,8},{10,11... | collective-permute-start | bytes 221192 | tf_op jit(solution)/shard_map/ppermute | solution.py:69
  148.7 5.6 %collective-permute-start.44 = (bf16[144,256]{1,0:T(8,128)(2,1)S(1)}, bf16[144,256]{1,0:T(8,128)(2,1)S(1)}, u32[]{:S(2)}, u32[]{:S(2)}) collective-permute-start(bf16[144,256]{1,0:T(8,128)(2,1)S(1)} %shard_map.88.refs_0_), channel_id=1, source_target_pairs={{0,8},{1,25},{8,16},{9,1},{16,24},{17,9},{24,0},{25,17},{2,10},{3,... | collective-permute-start | bytes 221192 | tf_op jit(solution)/shard_map/ppermute | solution.py:77
  152.2 10.4 %collective-permute-start.45 = (bf16[144,256]{1,0:T(8,128)(2,1)S(1)}, bf16[144,256]{1,0:T(8,128)(2,1)S(1)}, u32[]{:S(2)}, u32[]{:S(2)}) collective-permute-start(bf16[144,256]{1,0:T(8,128)(2,1)S(1)} %collective-permute-done.37.refs_1_), channel_id=1, source_target_pairs={{0,8},{1,25},{8,16},{9,1},{16,24},{17,9},{24,0},{25,17},{2,10},{3,... | collective-permute-start | bytes 221192 | tf_op jit(solution)/shard_map/ppermute | solution.py:77
  152.5 9.5 %collective-permute-start.42 = (bf16[144,256]{1,0:T(8,128)(2,1)S(1)}, bf16[144,256]{1,0:T(8,128)(2,1)S(1)}, u32[]{:S(2)}, u32[]{:S(2)}) collective-permute-start(bf16[144,256]{1,0:T(8,128)(2,1)S(1)} %collective-permute-done.38.refs_2_), channel_id=1, source_target_pairs={{0,1},{1,0},{2,3},{3,2},{4,5},{5,4},{6,7},{7,6},{8,9},{9,8},{10,11... | collective-permute-start | bytes 221192 | tf_op jit(solution)/shard_map/ppermute | solution.py:69
  154.3 8.4 %collective-permute-start.46 = (bf16[144,256]{1,0:T(8,128)(2,1)S(1)}, bf16[144,256]{1,0:T(8,128)(2,1)S(1)}, u32[]{:S(2)}, u32[]{:S(2)}) collective-permute-start(bf16[144,256]{1,0:T(8,128)(2,1)S(1)} %collective-permute-done.38.refs_2_), channel_id=1, source_target_pairs={{0,8},{1,25},{8,16},{9,1},{16,24},{17,9},{24,0},{25,17},{2,10},{3,... | collective-permute-start | bytes 221192 | tf_op jit(solution)/shard_map/ppermute | solution.py:77
  154.3 8.8 %collective-permute-start.47 = (bf16[144,256]{1,0:T(8,128)(2,1)S(1)}, bf16[144,256]{1,0:T(8,128)(2,1)S(1)}, u32[]{:S(2)}, u32[]{:S(2)}) collective-permute-start(bf16[144,256]{1,0:T(8,128)(2,1)S(1)} %collective-permute-done.39.refs_3_), channel_id=1, source_target_pairs={{0,8},{1,25},{8,16},{9,1},{16,24},{17,9},{24,0},{25,17},{2,10},{3,... | collective-permute-start | bytes 221192 | tf_op jit(solution)/shard_map/ppermute | solution.py:77
  162.0 8.1 %collective-permute-start.43 = (bf16[144,256]{1,0:T(8,128)(2,1)S(1)}, bf16[144,256]{1,0:T(8,128)(2,1)S(1)}, u32[]{:S(2)}, u32[]{:S(2)}) collective-permute-start(bf16[144,256]{1,0:T(8,128)(2,1)S(1)} %collective-permute-done.39.refs_3_), channel_id=1, source_target_pairs={{0,1},{1,0},{2,3},{3,2},{4,5},{5,4},{6,7},{7,6},{8,9},{9,8},{10,11... | collective-permute-start | bytes 221192 | tf_op jit(solution)/shard_map/ppermute | solution.py:69
  162.6 7.5 %collective-permute-start.48 = (bf16[144,256]{1,0:T(8,128)(2,1)S(1)}, bf16[144,256]{1,0:T(8,128)(2,1)S(1)}, u32[]{:S(2)}, u32[]{:S(2)}) collective-permute-start(bf16[144,256]{1,0:T(8,128)(2,1)S(1)} %collective-permute-done.44.refs_8_), channel_id=1, source_target_pairs={{0,1},{1,0},{2,3},{3,2},{4,5},{5,4},{6,7},{7,6},{8,9},{9,8},{10,11... | collective-permute-start | bytes 221192 | tf_op jit(solution)/shard_map/ppermute | solution.py:69
  162.7 7.4 %collective-permute-start.49 = (bf16[144,256]{1,0:T(8,128)(2,1)S(1)}, bf16[144,256]{1,0:T(8,128)(2,1)S(1)}, u32[]{:S(2)}, u32[]{:S(2)}) collective-permute-start(bf16[144,256]{1,0:T(8,128)(2,1)S(1)} %collective-permute-done.45.refs_9_), channel_id=1, source_target_pairs={{0,1},{1,0},{2,3},{3,2},{4,5},{5,4},{6,7},{7,6},{8,9},{9,8},{10,11... | collective-permute-start | bytes 221192 | tf_op jit(solution)/shard_map/ppermute | solution.py:69
  163.1 7.0 %collective-permute-start.50 = (bf16[144,256]{1,0:T(8,128)(2,1)S(1)}, bf16[144,256]{1,0:T(8,128)(2,1)S(1)}, u32[]{:S(2)}, u32[]{:S(2)}) collective-permute-start(bf16[144,256]{1,0:T(8,128)(2,1)S(1)} %collective-permute-done.46.refs_10_), channel_id=1, source_target_pairs={{0,1},{1,0},{2,3},{3,2},{4,5},{5,4},{6,7},{7,6},{8,9},{9,8},{10,11... | collective-permute-start | bytes 221192 | tf_op jit(solution)/shard_map/ppermute | solution.py:69
  163.2 6.9 %collective-permute-start.51 = (bf16[144,256]{1,0:T(8,128)(2,1)S(1)}, bf16[144,256]{1,0:T(8,128)(2,1)S(1)}, u32[]{:S(2)}, u32[]{:S(2)}) collective-permute-start(bf16[144,256]{1,0:T(8,128)(2,1)S(1)} %collective-permute-done.47.refs_11_), channel_id=1, source_target_pairs={{0,1},{1,0},{2,3},{3,2},{4,5},{5,4},{6,7},{7,6},{8,9},{9,8},{10,11... | collective-permute-start | bytes 221192 | tf_op jit(solution)/shard_map/ppermute | solution.py:69
  (22 other events, 317.6 us)

commit v5 on v4

--- a/solution.py
+++ b/solution.py
@@ -136,13 +136,27 @@
 
 
 def near_body(a0, b0, a1, b1, a3, b3, *refs):
-    weights, (near, ring, p0, p1, p3) = refs[:8], refs[8:]
+    weights, (near, ring, p0, p1, p3, acc) = refs[:8], refs[8:]
+    step = pl.program_id(0)
     for i, piece in enumerate((a0, b0, a1, b1, a3, b3)):
         near[i * HALF : (i + 1) * HALF, :] = piece[...]
     ring[...] = near[ROWS:, :]
-    part = forward_sum(near[...], weights)
-    for i, out in enumerate((p0, p1, p3)):
-        out[...] = part[i * ROWS : (i + 1) * ROWS]
+    parts = [dot(near[...], w1[...]) for w1 in weights[:4]]
+
+    @pl.when(step == 0)
+    def _():
+        for i, part in enumerate(parts):
+            acc[:, i * U : (i + 1) * U] = part
+
+    @pl.when(step == 1)
+    def _():
+        total = None
+        for i, part in enumerate(parts):
+            hidden = gelu(acc[:, i * U : (i + 1) * U] + part).astype(bf16)
+            keys = dot(hidden, weights[4 + i][...])
+            total = keys if total is None else total + keys
+        for i, out in enumerate((p0, p1, p3)):
+            out[...] = total[i * ROWS : (i + 1) * ROWS]
 
 
 def far_body(a2, b2, *refs):
@@ -409,6 +423,16 @@
         near_body,
         (far_sds((6 * HALF, C), bf16), far_sds((4 * HALF, C), bf16)) + (key_part,) * 3,
         a0, b0, a1, b1, a3, b3, *weights,
+        grid=(2,),
+        in_specs=[pl.BlockSpec((HALF, C // 2), lambda j: (0, j))] * 6
+        + [pl.BlockSpec((C // 2, U), lambda j: (j, 0))] * 4
+        + [pl.BlockSpec((U, E), lambda j: (0, 0))] * 4,
+        out_specs=[
+            pl.BlockSpec((6 * HALF, C // 2), lambda j: (0, j)),
+            pl.BlockSpec((4 * HALF, C // 2), lambda j: (0, j)),
+        ]
+        + [pl.BlockSpec((ROWS, E), lambda j: (0, 0))] * 3,
+        scratch=[pltpu.VMEM((6 * HALF, 4 * U), f32)],
         flops=2 * 10**9,
     )
     q1, q3 = along_y(p1, 1), along_y(p3, -1)
@@ -428,7 +452,7 @@
     own = (near, far)
     beside = (along_z(a0), along_z(b0), along_z(near_ring), along_z(far))
 
-    def rows_of(pools):
+    def rows_of(name, pools):
         return kernel(
             slope_body,
             (
@@ -436,7 +460,7 @@
                 far_sds((U, 8 * ROWS), f32),
                 far_sds((8 * ROWS, C), bf16),
             ),
-            *[kept(p) for p in pools], kept(w_first),
+            *(pools if name == "slopez" else [kept(p) for p in pools]), kept(w_first),
             grid=(2,),
             in_specs=[pl.BlockSpec((p.shape[0], 1024), lambda j: (0, j)) for p in pools]
             + [pl.BlockSpec((1024, U), lambda j: (j, 0))],
@@ -449,9 +473,12 @@
             flops=2 * 10**9,
         )
 
-    hidden_a, slope_a, joined_a = rows_of(own + (swap(near), swap(far)))
+    hidden_a, slope_a, joined_a = rows_of("slope", own + (swap(near), swap(far)))
     hidden_b, slope_b, joined_b = rows_of(
-        beside + tuple(swap(p) for p in beside[:3]) + (swap(beside[3]),)
+        "slopez",
+        beside
+        + tuple(swap(p) for p in beside[:3])
+        + (swap(beside[3]),),
     )
 
     row_sums, col_sums, tile, who = kernel(

time: 225 us -> 224 us (level)
  no operation moved by 1% of the time
where the time goes in v5:
time: 224 us; the launch traced here: 221 us
  waiting for transfers between devices  78.4 us (35%)
  starting transfers between devices  54.9 us (25%)
  blocking collectives  44 us (20%)
  Pallas kernels  41.9 us (19%)
    ppermute x21, waiting for transfers between devices, along_y(): return lax.ppermute(block, 'y', [(i, (i + distance) % 4) for i in range(4)])  46.9 us
    all_to_all x2, blocking collectives, exchange(): return lax.all_to_all(array, axis, 0, 0, tiled=True)  44 us
    pallas_call x16, Pallas kernels, kernel(): pl.pallas_call(body, out_shape=outs, scratch_shapes=list(scratch), compil...  41.9 us
    ppermute x10, waiting for transfers between devices, along_z(): return lax.ppermute(block, ZC, pairs)  28.9 us
    ppermute x21, starting transfers between devices, along_y(): return lax.ppermute(block, 'y', [(i, (i + distance) % 4) for i in range(4)])  25.3 us
    all_to_all x2, starting transfers between devices, exchange(): return lax.all_to_all(array, axis, 0, 0, tiled=True)  12.4 us
    ppermute x10, starting transfers between devices, along_z(): return lax.ppermute(block, ZC, pairs)  8.7 us
    ppermute x21, starting transfers between devices, swap(): return lax.ppermute(block, 'c', [(0, 1), (1, 0)])  8.58 us
  transfers between devices with their start and end apart: 54, of which 24 were waited for; matrix products, arithmetic and copies ran while one was open for 0% of the time, Pallas kernels for 15%

profile of v5, /device:TPU:6, one launch (start us, length us, event | category | flops | bytes accessed | tf_op | source)
XLA Modules:
  0.0 221.4 jit_solution(2375257113600704448)
XLA Ops:
  0.6 2.0 collective-permute-start.4
  2.6 1.7 collective-permute-start.5
  4.3 13.4 %collective-permute-done.4.refs_1_ = bf16[2048,256]{1,0:T(8,128)(2,1)S(1)} collective-permute-done((bf16[2048,256]{1,0:T(8,128)(2,1)}, bf16[2048,256]{1,0:T(8,128)(2,1)S(1)}, u32[]{:S(2)}, u32[]{:S(2)}) %collective-permute-start.4) | collective-permute-done | bytes 1048608 | tf_op jit(solution)/shard_map/ppermute | solution.py:77
  18.4 2.8 %shard_map.76 = (bf16[64,2048]{1,0:T(8,128)(2,1)S(1)}, bf16[64,2048]{1,0:T(8,128)(2,1)S(1)}) custom-call(bf16[1024,2048]{1,0:T(8,128)(2,1)} %bitcast.12, s32[1,128]{1,0:T(1,128)S(1)} %bitcast.10), custom_call_target="tpu_custom_call" | custom-call | flops 100000000 | tf_op jit(solution)/shard_map/pallas_call | solution.py:54
  21.2 3.1 %collective-permute-start = (bf16[64,2048]{1,0:T(8,128)(2,1)S(1)}, bf16[64,2048]{1,0:T(8,128)(2,1)S(1)}, u32[]{:S(2)}, u32[]{:S(2)}) collective-permute-start(bf16[64,2048]{1,0:T(8,128)(2,1)S(1)} %get-tuple-element.36.a0), channel_id=1, source_target_pairs={{0,6},{2,0},{4,2},{6,4},{1,7},{3,1},{5,3},{7,5},{8,14},{10,8},{12,... | collective-permute-start | bytes 786440 | tf_op jit(solution)/shard_map/ppermute | solution.py:65
  24.3 2.0 collective-permute-start.8
  26.3 4.2 %collective-permute-done.7.refs_5_ = bf16[256,256]{1,0:T(8,128)(2,1)S(1)} collective-permute-done((bf16[256,256]{1,0:T(8,128)(2,1)S(1)}, bf16[256,256]{1,0:T(8,128)(2,1)S(1)}, u32[]{:S(2)}, u32[]{:S(2)}) %collective-permute-start.7) | collective-permute-done | bytes 131104 | tf_op jit(solution)/shard_map/ppermute | solution.py:77
  32.6 4.3 %collective-permute-done.1.b1 = bf16[64,2048]{1,0:T(8,128)(2,1)S(1)} collective-permute-done((bf16[64,2048]{1,0:T(8,128)(2,1)S(1)}, bf16[64,2048]{1,0:T(8,128)(2,1)S(1)}, u32[]{:S(2)}, u32[]{:S(2)}) %collective-permute-start.1) | collective-permute-done | bytes 262176 | tf_op jit(solution)/shard_map/ppermute | solution.py:65
  36.9 4.6 %collective-permute-done.2.a3 = bf16[64,2048]{1,0:T(8,128)(2,1)S(1)} collective-permute-done((bf16[64,2048]{1,0:T(8,128)(2,1)S(1)}, bf16[64,2048]{1,0:T(8,128)(2,1)S(1)}, u32[]{:S(2)}, u32[]{:S(2)}) %collective-permute-start.2) | collective-permute-done | bytes 262176 | tf_op jit(solution)/shard_map/ppermute | solution.py:65
  41.7 5.3 %collective-permute-done.3.b3 = bf16[64,2048]{1,0:T(8,128)(2,1)S(1)} collective-permute-done((bf16[64,2048]{1,0:T(8,128)(2,1)S(1)}, bf16[64,2048]{1,0:T(8,128)(2,1)S(1)}, u32[]{:S(2)}, u32[]{:S(2)}) %collective-permute-start.3) | collective-permute-done | bytes 262176 | tf_op jit(solution)/shard_map/ppermute | solution.py:65
  47.0 4.1 %shard_map.77 = (bf16[384,2048]{1,0:T(8,128)(2,1)}, bf16[256,2048]{1,0:T(8,128)(2,1)}, f32[128,256]{1,0:T(8,128)S(1)}, f32[128,256]{1,0:T(8,128)S(1)}, f32[128,256]{1,0:T(8,128)S(1)}) custom-call(bf16[64,2048]{1,0:T(8,128)(2,1)S(1)} %get-tuple-element.36.a0, bf16[64,2048]{1,0:T(8,128)(2,1)S(1)} %get-tuple-element.37.b0, ...), custom_call_target="tpu_custom_call" | custom-call | flops 2000000000 | tf_op jit(solution)/shard_map/pallas_call | solution.py:54
  51.1 2.0 collective-permute-start.22
  53.1 1.3 collective-permute-done.11.b2
  54.4 1.8 shard_map.78
  56.4 3.2 %collective-permute-start.24 = (f32[128,256]{1,0:T(8,128)S(1)}, f32[128,256]{1,0:T(8,128)S(1)}, u32[]{:S(2)}, u32[]{:S(2)}) collective-permute-start(f32[128,256]{1,0:T(8,128)S(1)} %get-tuple-element.50), channel_id=1, source_target_pairs={{0,6},{2,0},{4,2},{6,4},{1,7},{3,1},{5,3},{7,5},{8,14},{10,8},{12,... | collective-permute-start | bytes 393224 | tf_op jit(solution)/shard_map/ppermute | solution.py:65
  59.6 3.1 %collective-permute-done.23.p2 = f32[128,256]{1,0:T(8,128)S(1)} collective-permute-done((f32[128,256]{1,0:T(8,128)S(1)}, f32[128,256]{1,0:T(8,128)S(1)}, u32[]{:S(2)}, u32[]{:S(2)}) %collective-permute-start.23) | collective-permute-done | bytes 131104 | tf_op jit(solution)/shard_map/ppermute | solution.py:65
  63.9 5.1 %all-to-all-start = ((bf16[16,128,256]{2,1,0:T(8,128)(2,1)}), bf16[16,128,256]{2,1,0:T(8,128)(2,1)S(1)}, u32[]{:S(2)}, u32[]{:S(2)}) async-start(bf16[16,128,256]{2,1,0:T(8,128)(2,1)} %get-tuple-element.53), calls=%async_computation | async-start | bytes 2097152 | tf_op jit(solution)/shard_map/all_to_all | solution.py:81
  69.1 1.3 collective-permute-done.25.mate
  70.4 2.8 %collective-permute-start.26 = (bf16[256,384]{1,0:T(8,128)(2,1)S(1)}, bf16[256,384]{1,0:T(8,128)(2,1)S(1)}, u32[]{:S(2)}, u32[]{:S(2)}) collective-permute-start(bf16[256,384]{1,0:T(8,128)(2,1)S(1)} %shard_map.82.pay0), channel_id=1, source_target_pairs={{0,6},{2,0},{4,2},{6,4},{1,7},{3,1},{5,3},{7,5},{8,14},{10,8},{12,... | collective-permute-start | bytes 589832 | tf_op jit(solution)/shard_map/ppermute | solution.py:65
  74.3 1.5 collective-permute-start.16
  75.9 6.1 %collective-permute-done.26.pay1 = bf16[256,384]{1,0:T(8,128)(2,1)S(1)} collective-permute-done((bf16[256,384]{1,0:T(8,128)(2,1)S(1)}, bf16[256,384]{1,0:T(8,128)(2,1)S(1)}, u32[]{:S(2)}, u32[]{:S(2)}) %collective-permute-start.26) | collective-permute-done | bytes 196640 | tf_op jit(solution)/shard_map/ppermute | solution.py:65
  82.5 2.9 %collective-permute-done.28.pay3 = bf16[256,384]{1,0:T(8,128)(2,1)S(1)} collective-permute-done((bf16[256,384]{1,0:T(8,128)(2,1)S(1)}, bf16[256,384]{1,0:T(8,128)(2,1)S(1)}, u32[]{:S(2)}, u32[]{:S(2)}) %collective-permute-start.28) | collective-permute-done | bytes 196640 | tf_op jit(solution)/shard_map/ppermute | solution.py:65
  85.4 3.7 %shard_map.83 = (f32[8,128]{1,0:T(8,128)S(1)}, f32[16,1,2176]{2,1,0:T(1,128)}, bf16[1024,256]{1,0:T(8,128)(2,1)}, f32[1024,128]{1,0:T(8,128)}) custom-call(s32[5]{0:T(128)S(1)} %stack.23.where, bf16[256,384]{1,0:T(8,128)(2,1)S(1)} %shard_map.82.pay0, bf16[256,384]{1,0:T(8,128)(2,1)S(1)} %collective-permute-done.26.pay1, ...), custom_call_target="tpu_custom_call" | custom-call | flops 1000000000 | tf_op jit(solution)/shard_map/pallas_call | solution.py:54
  89.1 7.2 %all-to-all-start.1 = ((f32[16,1,2176]{2,1,0:T(1,128)}), f32[16,1,2176]{2,1,0:T(1,128)S(1)}, u32[]{:S(2)}, u32[]{:S(2)}) async-start(f32[16,1,2176]{2,1,0:T(1,128)} %get-tuple-element.57), calls=%async_computation.1 | async-start | bytes 278528 | tf_op jit(solution)/shard_map/all_to_all | solution.py:81
  99.6 1.6 collective-permute-done.30.sum1
  101.1 2.4 %collective-permute-done.31.sum2 = f32[8,128]{1,0:T(8,128)S(1)} collective-permute-done((f32[8,128]{1,0:T(8,128)S(1)}, f32[8,128]{1,0:T(8,128)S(1)}, u32[]{:S(2)}, u32[]{:S(2)}) %collective-permute-start.31) | collective-permute-done | bytes 4128 | tf_op jit(solution)/shard_map/ppermute | solution.py:65
  104.0 6.9 %shard_map.86 = (f32[4,128,256]{2,1,0:T(8,128)S(1)}, f32[4,128,256]{2,1,0:T(8,128)S(1)}, f32[1,128]{1,0:T(1,128)}) custom-call(s32[5]{0:T(128)S(1)} %stack.23.where, bf16[1024,256]{1,0:T(8,128)(2,1)} %get-tuple-element.54.tile, f32[1024,128]{1,0:T(8,128)} %get-tuple-element.55.who, bf16[16,128,256]{2,1,0:T(8,128)(2,1)} %copy-done.1, ...), custom_call_target="tpu_custom_call" | custom-call | flops 3000000000 | tf_op jit(solution)/shard_map/pallas_call | solution.py:54
  111.0 1.5 collective-permute-start.14
  112.4 1.5 collective-permute-start.17
  113.9 4.7 %collective-permute-done.14.refs_0_ = bf16[64,2048]{1,0:T(8,128)(2,1)S(1)} collective-permute-done((bf16[64,2048]{1,0:T(8,128)(2,1)S(1)}, bf16[64,2048]{1,0:T(8,128)(2,1)S(1)}, u32[]{:S(2)}, u32[]{:S(2)}) %collective-permute-start.14) | collective-permute-done | bytes 262176 | tf_op jit(solution)/shard_map/ppermute | solution.py:77
  118.8 1.5 collective-permute-start.18
  120.5 6.5 %collective-permute-done.15.refs_1_ = bf16[64,2048]{1,0:T(8,128)(2,1)S(1)} collective-permute-done((bf16[64,2048]{1,0:T(8,128)(2,1)S(1)}, bf16[64,2048]{1,0:T(8,128)(2,1)S(1)}, u32[]{:S(2)}, u32[]{:S(2)}) %collective-permute-start.15) | collective-permute-done | bytes 262176 | tf_op jit(solution)/shard_map/ppermute | solution.py:77
  127.8 2.6 %collective-permute-start.35 = (f32[128,256]{1,0:T(8,128)S(1)}, f32[128,256]{1,0:T(8,128)S(1)}, u32[]{:S(2)}, u32[]{:S(2)}) collective-permute-start(f32[128,256]{1,0:T(8,128)S(1)} %get-tuple-element.62), channel_id=1, source_target_pairs={{0,4},{2,6},{4,0},{6,2},{1,5},{3,7},{5,1},{7,3},{8,12},{10,14},{12... | collective-permute-start | bytes 393224 | tf_op jit(solution)/shard_map/ppermute | solution.py:65
  130.5 3.4 %collective-permute-done.34.g1 = f32[128,256]{1,0:T(8,128)S(1)} collective-permute-done((f32[128,256]{1,0:T(8,128)S(1)}, f32[128,256]{1,0:T(8,128)S(1)}, u32[]{:S(2)}, u32[]{:S(2)}) %collective-permute-start.34) | collective-permute-done | bytes 131104 | tf_op jit(solution)/shard_map/ppermute | solution.py:65
  133.9 1.4 collective-permute-done.35.g2
  135.3 1.4 collective-permute-start.36
  136.7 3.6 %collective-permute-done.36.g3 = f32[128,256]{1,0:T(8,128)S(1)} collective-permute-done((f32[128,256]{1,0:T(8,128)S(1)}, f32[128,256]{1,0:T(8,128)S(1)}, u32[]{:S(2)}, u32[]{:S(2)}) %collective-permute-start.36) | collective-permute-done | bytes 131104 | tf_op jit(solution)/shard_map/ppermute | solution.py:65
  142.1 2.7 %collective-permute-start.37 = (bf16[144,256]{1,0:T(8,128)(2,1)S(1)}, bf16[144,256]{1,0:T(8,128)(2,1)S(1)}, u32[]{:S(2)}, u32[]{:S(2)}) collective-permute-start(bf16[144,256]{1,0:T(8,128)(2,1)S(1)} %shard_map.88.refs_0_), channel_id=1, source_target_pairs={{0,6},{2,0},{4,2},{6,4},{1,7},{3,1},{5,3},{7,5},{8,14},{10,8},{12,... | collective-permute-start | bytes 221192 | tf_op jit(solution)/shard_map/ppermute | solution.py:65
  145.7 2.8 %collective-permute-done.37.refs_1_ = bf16[144,256]{1,0:T(8,128)(2,1)S(1)} collective-permute-done((bf16[144,256]{1,0:T(8,128)(2,1)S(1)}, bf16[144,256]{1,0:T(8,128)(2,1)S(1)}, u32[]{:S(2)}, u32[]{:S(2)}) %collective-permute-start.37) | collective-permute-done | bytes 73760 | tf_op jit(solution)/shard_map/ppermute | solution.py:65
  148.6 2.8 %collective-permute-done.38.refs_2_ = bf16[144,256]{1,0:T(8,128)(2,1)S(1)} collective-permute-done((bf16[144,256]{1,0:T(8,128)(2,1)S(1)}, bf16[144,256]{1,0:T(8,128)(2,1)S(1)}, u32[]{:S(2)}, u32[]{:S(2)}) %collective-permute-start.38) | collective-permute-done | bytes 73760 | tf_op jit(solution)/shard_map/ppermute | solution.py:65
  152.3 1.7 collective-permute-start.42
  154.1 1.8 collective-permute-start.47
  156.0 5.9 %shard_map.79 = (bf16[256,1024]{1,0:T(8,128)(2,1)}, f32[256,1024]{1,0:T(8,128)}, bf16[1024,2048]{1,0:T(8,128)(2,1)}) custom-call(bf16[384,2048]{1,0:T(8,128)(2,1)} %get-tuple-element.38.refs_0_, bf16[128,2048]{1,0:T(8,128)(2,1)} %get-tuple-element.39.refs_1_, bf16[384,2048]{1,0:T(8,128)(2,1)} %collective-permute-done.12.refs_2_, ...), custom_call_target="tpu_custom_call" | custom-call | flops 2000000000 | tf_op jit(solution)/shard_map/pallas_call | solution.py:54
  163.4 5.4 %shard_map.80 = (bf16[256,1024]{1,0:T(8,128)(2,1)}, f32[256,1024]{1,0:T(8,128)}, bf16[1024,2048]{1,0:T(8,128)(2,1)}) custom-call(bf16[64,2048]{1,0:T(8,128)(2,1)S(1)} %collective-permute-done.14.refs_0_, bf16[64,2048]{1,0:T(8,128)(2,1)S(1)} %collective-permute-done.15.refs_1_, bf16[256,2048]{1,0:T(8,128)(2,1)S(1)} %collective-permute-done.16.refs_2_, ...), custom_call_target="tpu_custom_call" | custom-call | flops 2000000000 | tf_op jit(solution)/shard_map/pallas_call | solution.py:54
  168.9 6.8 %shard_map.89 = (bf16[8,288,256]{2,1,0:T(8,128)(2,1)S(1)}, f32[1,128]{1,0:T(1,128)}) custom-call(bf16[1024,2048]{1,0:T(8,128)(2,1)} %get-tuple-element.40.pool_a, bf16[1024,2048]{1,0:T(8,128)(2,1)} %get-tuple-element.42.pool_b, bf16[256,1024]{1,0:T(8,128)(2,1)} %get-tuple-element.43.hidden_a, bf16[256,1024]{1,0:T(8,128)(2,1)} %get-tuple-element.44.hidden_b, ...), custom_call_target="tpu_custom_call" | custom-call | flops 2000000000 | tf_op jit(solution)/shard_map/pallas_call | solution.py:54
  175.7 23.4 %all_to_all.20.got = bf16[8,288,256]{2,1,0:T(8,128)(2,1)S(1)} all-to-all(bf16[8,288,256]{2,1,0:T(8,128)(2,1)S(1)} %get-tuple-element.66), channel_id=1, replica_groups=mesh['x'=4,'zh'=2,'zl'=2,'y'=4,'c'=2] {'x','zh'}, dimensions={0} | all-to-all | bytes 2359296 | tf_op jit(solution)/shard_map/all_to_all | solution.py:81
  199.3 20.6 %all_to_all.21.got = bf16[8,288,256]{2,1,0:T(8,128)(2,1)S(1)} all-to-all(bf16[8,288,256]{2,1,0:T(8,128)(2,1)S(1)} %shard_map.90), channel_id=1, replica_groups=mesh['x'=4,'zh'=2,'zl'=2,'y'=4,'c'=2] {'x','zh'}, dimensions={0} | all-to-all | bytes 2359296 | tf_op jit(solution)/shard_map/all_to_all | solution.py:81
  219.9 1.5 shard_map.91
  (95 shorter events, 16.8 us)
Async XLA Ops:
  0.6 17.1 %collective-permute-start.4 = (bf16[2048,256]{1,0:T(8,128)(2,1)}, bf16[2048,256]{1,0:T(8,128)(2,1)S(1)}, u32[]{:S(2)}, u32[]{:S(2)}) collective-permute-start(bf16[2048,256]{1,0:T(8,128)(2,1)} %refs_8_.1), channel_id=1, source_target_pairs={{0,8},{1,25},{8,16},{9,1},{16,24},{17,9},{24,0},{25,17},{2,10},{3,... | collective-permute-start | bytes 3145736 | tf_op jit(solution)/shard_map/ppermute | solution.py:77
  2.6 44.4 %collective-permute-start.5 = (bf16[2048,256]{1,0:T(8,128)(2,1)}, bf16[2048,256]{1,0:T(8,128)(2,1)S(1)}, u32[]{:S(2)}, u32[]{:S(2)}) collective-permute-start(bf16[2048,256]{1,0:T(8,128)(2,1)} %refs_8_.1), channel_id=1, source_target_pairs={{0,1},{1,0},{2,3},{3,2},{4,5},{5,4},{6,7},{7,6},{8,9},{9,8},{10,11... | collective-permute-start | bytes 3145736 | tf_op jit(solution)/shard_map/ppermute | solution.py:69
  17.7 29.2 %collective-permute-start.6 = (bf16[2048,256]{1,0:T(8,128)(2,1)S(1)}, bf16[2048,256]{1,0:T(8,128)(2,1)S(1)}, u32[]{:S(2)}, u32[]{:S(2)}) collective-permute-start(bf16[2048,256]{1,0:T(8,128)(2,1)S(1)} %collective-permute-done.4.refs_1_), channel_id=1, source_target_pairs={{0,1},{1,0},{2,3},{3,2},{4,5},{5,4},{6,7},{7,6},{8,9},{9,8},{10,11... | collective-permute-start | bytes 3145736 | tf_op jit(solution)/shard_map/ppermute | solution.py:69
  21.2 11.3 %collective-permute-start = (bf16[64,2048]{1,0:T(8,128)(2,1)S(1)}, bf16[64,2048]{1,0:T(8,128)(2,1)S(1)}, u32[]{:S(2)}, u32[]{:S(2)}) collective-permute-start(bf16[64,2048]{1,0:T(8,128)(2,1)S(1)} %get-tuple-element.36.a0), channel_id=1, source_target_pairs={{0,6},{2,0},{4,2},{6,4},{1,7},{3,1},{5,3},{7,5},{8,14},{10,8},{12,... | collective-permute-start | bytes 786440 | tf_op jit(solution)/shard_map/ppermute | solution.py:65
  24.3 6.2 %collective-permute-start.7 = (bf16[256,256]{1,0:T(8,128)(2,1)S(1)}, bf16[256,256]{1,0:T(8,128)(2,1)S(1)}, u32[]{:S(2)}, u32[]{:S(2)}) collective-permute-start(bf16[256,256]{1,0:T(8,128)(2,1)S(1)} %copy-done.2), channel_id=1, source_target_pairs={{0,8},{1,25},{8,16},{9,1},{16,24},{17,9},{24,0},{25,17},{2,10},{3,... | collective-permute-start | bytes 393224 | tf_op jit(solution)/shard_map/ppermute | solution.py:77
  24.3 6.9 %collective-permute-start.8 = (bf16[256,256]{1,0:T(8,128)(2,1)S(1)}, bf16[256,256]{1,0:T(8,128)(2,1)S(1)}, u32[]{:S(2)}, u32[]{:S(2)}) collective-permute-start(bf16[256,256]{1,0:T(8,128)(2,1)S(1)} %copy-done.2), channel_id=1, source_target_pairs={{0,1},{1,0},{2,3},{3,2},{4,5},{5,4},{6,7},{7,6},{8,9},{9,8},{10,11... | collective-permute-start | bytes 393224 | tf_op jit(solution)/shard_map/ppermute | solution.py:69
  30.5 6.4 %collective-permute-start.1 = (bf16[64,2048]{1,0:T(8,128)(2,1)S(1)}, bf16[64,2048]{1,0:T(8,128)(2,1)S(1)}, u32[]{:S(2)}, u32[]{:S(2)}) collective-permute-start(bf16[64,2048]{1,0:T(8,128)(2,1)S(1)} %get-tuple-element.37.b0), channel_id=1, source_target_pairs={{0,6},{2,0},{4,2},{6,4},{1,7},{3,1},{5,3},{7,5},{8,14},{10,8},{12,... | collective-permute-start | bytes 786440 | tf_op jit(solution)/shard_map/ppermute | solution.py:65
  31.2 10.2 %collective-permute-start.2 = (bf16[64,2048]{1,0:T(8,128)(2,1)S(1)}, bf16[64,2048]{1,0:T(8,128)(2,1)S(1)}, u32[]{:S(2)}, u32[]{:S(2)}) collective-permute-start(bf16[64,2048]{1,0:T(8,128)(2,1)S(1)} %get-tuple-element.36.a0), channel_id=1, source_target_pairs={{0,2},{2,4},{4,6},{6,0},{1,3},{3,5},{5,7},{7,1},{8,10},{10,12},{12... | collective-permute-start | bytes 786440 | tf_op jit(solution)/shard_map/ppermute | solution.py:65
  32.5 14.4 %collective-permute-start.3 = (bf16[64,2048]{1,0:T(8,128)(2,1)S(1)}, bf16[64,2048]{1,0:T(8,128)(2,1)S(1)}, u32[]{:S(2)}, u32[]{:S(2)}) collective-permute-start(bf16[64,2048]{1,0:T(8,128)(2,1)S(1)} %get-tuple-element.37.b0), channel_id=1, source_target_pairs={{0,2},{2,4},{4,6},{6,0},{1,3},{3,5},{5,7},{7,1},{8,10},{10,12},{12... | collective-permute-start | bytes 786440 | tf_op jit(solution)/shard_map/ppermute | solution.py:65
  36.9 10.1 %collective-permute-start.9 = (bf16[256,256]{1,0:T(8,128)(2,1)S(1)}, bf16[256,256]{1,0:T(8,128)(2,1)S(1)}, u32[]{:S(2)}, u32[]{:S(2)}) collective-permute-start(bf16[256,256]{1,0:T(8,128)(2,1)S(1)} %collective-permute-done.7.refs_5_), channel_id=1, source_target_pairs={{0,1},{1,0},{2,3},{3,2},{4,5},{5,4},{6,7},{7,6},{8,9},{9,8},{10,11... | collective-permute-start | bytes 393224 | tf_op jit(solution)/shard_map/ppermute | solution.py:69
  41.5 11.6 %collective-permute-start.10 = (bf16[64,2048]{1,0:T(8,128)(2,1)S(1)}, bf16[64,2048]{1,0:T(8,128)(2,1)S(1)}, u32[]{:S(2)}, u32[]{:S(2)}) collective-permute-start(bf16[64,2048]{1,0:T(8,128)(2,1)S(1)} %collective-permute-done.2.a3), channel_id=1, source_target_pairs={{0,2},{2,4},{4,6},{6,0},{1,3},{3,5},{5,7},{7,1},{8,10},{10,12},{12... | collective-permute-start | bytes 786440 | tf_op jit(solution)/shard_map/ppermute | solution.py:65
  47.0 7.4 %collective-permute-start.11 = (bf16[64,2048]{1,0:T(8,128)(2,1)S(1)}, bf16[64,2048]{1,0:T(8,128)(2,1)S(1)}, u32[]{:S(2)}, u32[]{:S(2)}) collective-permute-start(bf16[64,2048]{1,0:T(8,128)(2,1)S(1)} %collective-permute-done.1.b1), channel_id=1, source_target_pairs={{0,6},{2,0},{4,2},{6,4},{1,7},{3,1},{5,3},{7,5},{8,14},{10,8},{12,... | collective-permute-start | bytes 786440 | tf_op jit(solution)/shard_map/ppermute | solution.py:65
  51.1 8.6 %collective-permute-start.22 = (f32[128,256]{1,0:T(8,128)S(1)}, f32[128,256]{1,0:T(8,128)S(1)}, u32[]{:S(2)}, u32[]{:S(2)}) collective-permute-start(f32[128,256]{1,0:T(8,128)S(1)} %get-tuple-element.48), channel_id=1, source_target_pairs={{0,2},{2,4},{4,6},{6,0},{1,3},{3,5},{5,7},{7,1},{8,10},{10,12},{12... | collective-permute-start | bytes 393224 | tf_op jit(solution)/shard_map/ppermute | solution.py:65
  56.2 6.5 %collective-permute-start.23 = (f32[128,256]{1,0:T(8,128)S(1)}, f32[128,256]{1,0:T(8,128)S(1)}, u32[]{:S(2)}, u32[]{:S(2)}) collective-permute-start(f32[128,256]{1,0:T(8,128)S(1)} %get-tuple-element.49), channel_id=1, source_target_pairs={{0,4},{2,6},{4,0},{6,2},{1,5},{3,7},{5,1},{7,3},{8,12},{10,14},{12... | collective-permute-start | bytes 393224 | tf_op jit(solution)/shard_map/ppermute | solution.py:65
  56.4 6.3 %collective-permute-start.24 = (f32[128,256]{1,0:T(8,128)S(1)}, f32[128,256]{1,0:T(8,128)S(1)}, u32[]{:S(2)}, u32[]{:S(2)}) collective-permute-start(f32[128,256]{1,0:T(8,128)S(1)} %get-tuple-element.50), channel_id=1, source_target_pairs={{0,6},{2,0},{4,2},{6,4},{1,7},{3,1},{5,3},{7,5},{8,14},{10,8},{12,... | collective-permute-start | bytes 393224 | tf_op jit(solution)/shard_map/ppermute | solution.py:65
  63.9 21.4 %all-to-all-start = ((bf16[16,128,256]{2,1,0:T(8,128)(2,1)}), bf16[16,128,256]{2,1,0:T(8,128)(2,1)S(1)}, u32[]{:S(2)}, u32[]{:S(2)}) async-start(bf16[16,128,256]{2,1,0:T(8,128)(2,1)} %get-tuple-element.53), calls=%async_computation | async-start | bytes 2097152 | tf_op jit(solution)/shard_map/all_to_all | solution.py:81
  70.4 11.5 %collective-permute-start.26 = (bf16[256,384]{1,0:T(8,128)(2,1)S(1)}, bf16[256,384]{1,0:T(8,128)(2,1)S(1)}, u32[]{:S(2)}, u32[]{:S(2)}) collective-permute-start(bf16[256,384]{1,0:T(8,128)(2,1)S(1)} %shard_map.82.pay0), channel_id=1, source_target_pairs={{0,6},{2,0},{4,2},{6,4},{1,7},{3,1},{5,3},{7,5},{8,14},{10,8},{12,... | collective-permute-start | bytes 589832 | tf_op jit(solution)/shard_map/ppermute | solution.py:65
  73.2 9.3 %collective-permute-start.27 = (bf16[256,384]{1,0:T(8,128)(2,1)S(1)}, bf16[256,384]{1,0:T(8,128)(2,1)S(1)}, u32[]{:S(2)}, u32[]{:S(2)}) collective-permute-start(bf16[256,384]{1,0:T(8,128)(2,1)S(1)} %shard_map.82.pay0), channel_id=1, source_target_pairs={{0,4},{2,6},{4,0},{6,2},{1,5},{3,7},{5,1},{7,3},{8,12},{10,14},{12... | collective-permute-start | bytes 589832 | tf_op jit(solution)/shard_map/ppermute | solution.py:65
  73.5 11.8 %collective-permute-start.28 = (bf16[256,384]{1,0:T(8,128)(2,1)S(1)}, bf16[256,384]{1,0:T(8,128)(2,1)S(1)}, u32[]{:S(2)}, u32[]{:S(2)}) collective-permute-start(bf16[256,384]{1,0:T(8,128)(2,1)S(1)} %shard_map.82.pay0), channel_id=1, source_target_pairs={{0,2},{2,4},{4,6},{6,0},{1,3},{3,5},{5,7},{7,1},{8,10},{10,12},{12... | collective-permute-start | bytes 589832 | tf_op jit(solution)/shard_map/ppermute | solution.py:65
  74.3 44.5 %collective-permute-start.16 = (bf16[256,2048]{1,0:T(8,128)(2,1)}, bf16[256,2048]{1,0:T(8,128)(2,1)S(1)}, u32[]{:S(2)}, u32[]{:S(2)}) collective-permute-start(bf16[256,2048]{1,0:T(8,128)(2,1)} %get-tuple-element.41), channel_id=1, source_target_pairs={{0,8},{1,25},{8,16},{9,1},{16,24},{17,9},{24,0},{25,17},{2,10},{3,... | collective-permute-start | bytes 3145736 | tf_op jit(solution)/shard_map/ppermute | solution.py:77
  89.1 14.9 %all-to-all-start.1 = ((f32[16,1,2176]{2,1,0:T(1,128)}), f32[16,1,2176]{2,1,0:T(1,128)S(1)}, u32[]{:S(2)}, u32[]{:S(2)}) async-start(f32[16,1,2176]{2,1,0:T(1,128)} %get-tuple-element.57), calls=%async_computation.1 | async-start | bytes 278528 | tf_op jit(solution)/shard_map/all_to_all | solution.py:81
  98.4 5.1 %collective-permute-start.31 = (f32[8,128]{1,0:T(8,128)S(1)}, f32[8,128]{1,0:T(8,128)S(1)}, u32[]{:S(2)}, u32[]{:S(2)}) collective-permute-start(f32[8,128]{1,0:T(8,128)S(1)} %shard_map.84.sum0), channel_id=1, source_target_pairs={{0,4},{2,6},{4,0},{6,2},{1,5},{3,7},{5,1},{7,3},{8,12},{10,14},{12... | collective-permute-start | bytes 12296 | tf_op jit(solution)/shard_map/ppermute | solution.py:65
  98.7 5.1 %collective-permute-start.32 = (f32[8,128]{1,0:T(8,128)S(1)}, f32[8,128]{1,0:T(8,128)S(1)}, u32[]{:S(2)}, u32[]{:S(2)}) collective-permute-start(f32[8,128]{1,0:T(8,128)S(1)} %shard_map.84.sum0), channel_id=1, source_target_pairs={{0,2},{2,4},{4,6},{6,0},{1,3},{3,5},{5,7},{7,1},{8,10},{10,12},{12... | collective-permute-start | bytes 12296 | tf_op jit(solution)/shard_map/ppermute | solution.py:65
  99.6 46.2 %collective-permute-start.12 = (bf16[384,2048]{1,0:T(8,128)(2,1)}, bf16[384,2048]{1,0:T(8,128)(2,1)}, u32[]{:S(2)}, u32[]{:S(2)}) collective-permute-start(bf16[384,2048]{1,0:T(8,128)(2,1)} %get-tuple-element.38.refs_0_), channel_id=1, source_target_pairs={{0,1},{1,0},{2,3},{3,2},{4,5},{5,4},{6,7},{7,6},{8,9},{9,8},{10,11... | collective-permute-start | bytes 4718600 | tf_op jit(solution)/shard_map/ppermute | solution.py:69
  111.0 9.3 %collective-permute-start.33 = (f32[4,128,256]{2,1,0:T(8,128)S(1)}, f32[4,128,256]{2,1,0:T(8,128)S(1)}, u32[]{:S(2)}, u32[]{:S(2)}) collective-permute-start(f32[4,128,256]{2,1,0:T(8,128)S(1)} %get-tuple-element.59), channel_id=1, source_target_pairs={{0,1},{1,0},{2,3},{3,2},{4,5},{5,4},{6,7},{7,6},{8,9},{9,8},{10,11... | collective-permute-start | bytes 1572872 | tf_op jit(solution)/shard_map/ppermute | solution.py:69
  111.0 7.6 %collective-permute-start.14 = (bf16[64,2048]{1,0:T(8,128)(2,1)S(1)}, bf16[64,2048]{1,0:T(8,128)(2,1)S(1)}, u32[]{:S(2)}, u32[]{:S(2)}) collective-permute-start(bf16[64,2048]{1,0:T(8,128)(2,1)S(1)} %get-tuple-element.36.a0), channel_id=1, source_target_pairs={{0,8},{1,25},{8,16},{9,1},{16,24},{17,9},{24,0},{25,17},{2,10},{3,... | collective-permute-start | bytes 786440 | tf_op jit(solution)/shard_map/ppermute | solution.py:77
  112.4 18.0 %collective-permute-start.17 = (bf16[128,2048]{1,0:T(8,128)(2,1)S(1)}, bf16[128,2048]{1,0:T(8,128)(2,1)S(1)}, u32[]{:S(2)}, u32[]{:S(2)}) collective-permute-start(bf16[128,2048]{1,0:T(8,128)(2,1)S(1)} %copy-done.6), channel_id=1, source_target_pairs={{0,8},{1,25},{8,16},{9,1},{16,24},{17,9},{24,0},{25,17},{2,10},{3,... | collective-permute-start | bytes 1572872 | tf_op jit(solution)/shard_map/ppermute | solution.py:77
  118.6 8.4 %collective-permute-start.15 = (bf16[64,2048]{1,0:T(8,128)(2,1)S(1)}, bf16[64,2048]{1,0:T(8,128)(2,1)S(1)}, u32[]{:S(2)}, u32[]{:S(2)}) collective-permute-start(bf16[64,2048]{1,0:T(8,128)(2,1)S(1)} %get-tuple-element.37.b0), channel_id=1, source_target_pairs={{0,8},{1,25},{8,16},{9,1},{16,24},{17,9},{24,0},{25,17},{2,10},{3,... | collective-permute-start | bytes 786440 | tf_op jit(solution)/shard_map/ppermute | solution.py:77
  118.8 9.0 %collective-permute-start.18 = (bf16[64,2048]{1,0:T(8,128)(2,1)S(1)}, bf16[64,2048]{1,0:T(8,128)(2,1)S(1)}, u32[]{:S(2)}, u32[]{:S(2)}) collective-permute-start(bf16[64,2048]{1,0:T(8,128)(2,1)S(1)} %collective-permute-done.14.refs_0_), channel_id=1, source_target_pairs={{0,1},{1,0},{2,3},{3,2},{4,5},{5,4},{6,7},{7,6},{8,9},{9,8},{10,11... | collective-permute-start | bytes 786440 | tf_op jit(solution)/shard_map/ppermute | solution.py:69
  120.3 42.7 %collective-permute-start.20 = (bf16[256,2048]{1,0:T(8,128)(2,1)S(1)}, bf16[256,2048]{1,0:T(8,128)(2,1)S(1)}, u32[]{:S(2)}, u32[]{:S(2)}) collective-permute-start(bf16[256,2048]{1,0:T(8,128)(2,1)S(1)} %collective-permute-done.16.refs_2_), channel_id=1, source_target_pairs={{0,1},{1,0},{2,3},{3,2},{4,5},{5,4},{6,7},{7,6},{8,9},{9,8},{10,11... | collective-permute-start | bytes 3145736 | tf_op jit(solution)/shard_map/ppermute | solution.py:69
  127.0 6.9 %collective-permute-start.34 = (f32[128,256]{1,0:T(8,128)S(1)}, f32[128,256]{1,0:T(8,128)S(1)}, u32[]{:S(2)}, u32[]{:S(2)}) collective-permute-start(f32[128,256]{1,0:T(8,128)S(1)} %get-tuple-element.61), channel_id=1, source_target_pairs={{0,2},{2,4},{4,6},{6,0},{1,3},{3,5},{5,7},{7,1},{8,10},{10,12},{12... | collective-permute-start | bytes 393224 | tf_op jit(solution)/shard_map/ppermute | solution.py:65
  127.8 7.4 %collective-permute-start.35 = (f32[128,256]{1,0:T(8,128)S(1)}, f32[128,256]{1,0:T(8,128)S(1)}, u32[]{:S(2)}, u32[]{:S(2)}) collective-permute-start(f32[128,256]{1,0:T(8,128)S(1)} %get-tuple-element.62), channel_id=1, source_target_pairs={{0,4},{2,6},{4,0},{6,2},{1,5},{3,7},{5,1},{7,3},{8,12},{10,14},{12... | collective-permute-start | bytes 393224 | tf_op jit(solution)/shard_map/ppermute | solution.py:65
  130.5 14.3 %collective-permute-start.13 = (bf16[128,2048]{1,0:T(8,128)(2,1)S(1)}, bf16[128,2048]{1,0:T(8,128)(2,1)S(1)}, u32[]{:S(2)}, u32[]{:S(2)}) collective-permute-start(bf16[128,2048]{1,0:T(8,128)(2,1)S(1)} %copy-done.6), channel_id=1, source_target_pairs={{0,1},{1,0},{2,3},{3,2},{4,5},{5,4},{6,7},{7,6},{8,9},{9,8},{10,11... | collective-permute-start | bytes 1572872 | tf_op jit(solution)/shard_map/ppermute | solution.py:69
  133.9 10.9 %collective-permute-start.21 = (bf16[128,2048]{1,0:T(8,128)(2,1)S(1)}, bf16[128,2048]{1,0:T(8,128)(2,1)S(1)}, u32[]{:S(2)}, u32[]{:S(2)}) collective-permute-start(bf16[128,2048]{1,0:T(8,128)(2,1)S(1)} %collective-permute-done.17.refs_3_), channel_id=1, source_target_pairs={{0,1},{1,0},{2,3},{3,2},{4,5},{5,4},{6,7},{7,6},{8,9},{9,8},{10,11... | collective-permute-start | bytes 1572872 | tf_op jit(solution)/shard_map/ppermute | solution.py:69
  142.1 6.5 %collective-permute-start.37 = (bf16[144,256]{1,0:T(8,128)(2,1)S(1)}, bf16[144,256]{1,0:T(8,128)(2,1)S(1)}, u32[]{:S(2)}, u32[]{:S(2)}) collective-permute-start(bf16[144,256]{1,0:T(8,128)(2,1)S(1)} %shard_map.88.refs_0_), channel_id=1, source_target_pairs={{0,6},{2,0},{4,2},{6,4},{1,7},{3,1},{5,3},{7,5},{8,14},{10,8},{12,... | collective-permute-start | bytes 221192 | tf_op jit(solution)/shard_map/ppermute | solution.py:65
  144.8 6.7 %collective-permute-start.38 = (bf16[144,256]{1,0:T(8,128)(2,1)S(1)}, bf16[144,256]{1,0:T(8,128)(2,1)S(1)}, u32[]{:S(2)}, u32[]{:S(2)}) collective-permute-start(bf16[144,256]{1,0:T(8,128)(2,1)S(1)} %shard_map.88.refs_0_), channel_id=1, source_target_pairs={{0,4},{2,6},{4,0},{6,2},{1,5},{3,7},{5,1},{7,3},{8,12},{10,14},{12... | collective-permute-start | bytes 221192 | tf_op jit(solution)/shard_map/ppermute | solution.py:65
  144.8 7.3 %collective-permute-start.39 = (bf16[144,256]{1,0:T(8,128)(2,1)S(1)}, bf16[144,256]{1,0:T(8,128)(2,1)S(1)}, u32[]{:S(2)}, u32[]{:S(2)}) collective-permute-start(bf16[144,256]{1,0:T(8,128)(2,1)S(1)} %shard_map.88.refs_0_), channel_id=1, source_target_pairs={{0,2},{2,4},{4,6},{6,0},{1,3},{3,5},{5,7},{7,1},{8,10},{10,12},{12... | collective-permute-start | bytes 221192 | tf_op jit(solution)/shard_map/ppermute | solution.py:65
  145.7 6.6 %collective-permute-start.40 = (bf16[144,256]{1,0:T(8,128)(2,1)S(1)}, bf16[144,256]{1,0:T(8,128)(2,1)S(1)}, u32[]{:S(2)}, u32[]{:S(2)}) collective-permute-start(bf16[144,256]{1,0:T(8,128)(2,1)S(1)} %shard_map.88.refs_0_), channel_id=1, source_target_pairs={{0,1},{1,0},{2,3},{3,2},{4,5},{5,4},{6,7},{7,6},{8,9},{9,8},{10,11... | collective-permute-start | bytes 221192 | tf_op jit(solution)/shard_map/ppermute | solution.py:69
  148.6 5.6 %collective-permute-start.44 = (bf16[144,256]{1,0:T(8,128)(2,1)S(1)}, bf16[144,256]{1,0:T(8,128)(2,1)S(1)}, u32[]{:S(2)}, u32[]{:S(2)}) collective-permute-start(bf16[144,256]{1,0:T(8,128)(2,1)S(1)} %shard_map.88.refs_0_), channel_id=1, source_target_pairs={{0,8},{1,25},{8,16},{9,1},{16,24},{17,9},{24,0},{25,17},{2,10},{3,... | collective-permute-start | bytes 221192 | tf_op jit(solution)/shard_map/ppermute | solution.py:77
  152.0 10.4 %collective-permute-start.45 = (bf16[144,256]{1,0:T(8,128)(2,1)S(1)}, bf16[144,256]{1,0:T(8,128)(2,1)S(1)}, u32[]{:S(2)}, u32[]{:S(2)}) collective-permute-start(bf16[144,256]{1,0:T(8,128)(2,1)S(1)} %collective-permute-done.37.refs_1_), channel_id=1, source_target_pairs={{0,8},{1,25},{8,16},{9,1},{16,24},{17,9},{24,0},{25,17},{2,10},{3,... | collective-permute-start | bytes 221192 | tf_op jit(solution)/shard_map/ppermute | solution.py:77
  152.3 9.6 %collective-permute-start.42 = (bf16[144,256]{1,0:T(8,128)(2,1)S(1)}, bf16[144,256]{1,0:T(8,128)(2,1)S(1)}, u32[]{:S(2)}, u32[]{:S(2)}) collective-permute-start(bf16[144,256]{1,0:T(8,128)(2,1)S(1)} %collective-permute-done.38.refs_2_), channel_id=1, source_target_pairs={{0,1},{1,0},{2,3},{3,2},{4,5},{5,4},{6,7},{7,6},{8,9},{9,8},{10,11... | collective-permute-start | bytes 221192 | tf_op jit(solution)/shard_map/ppermute | solution.py:69
  154.1 8.4 %collective-permute-start.46 = (bf16[144,256]{1,0:T(8,128)(2,1)S(1)}, bf16[144,256]{1,0:T(8,128)(2,1)S(1)}, u32[]{:S(2)}, u32[]{:S(2)}) collective-permute-start(bf16[144,256]{1,0:T(8,128)(2,1)S(1)} %collective-permute-done.38.refs_2_), channel_id=1, source_target_pairs={{0,8},{1,25},{8,16},{9,1},{16,24},{17,9},{24,0},{25,17},{2,10},{3,... | collective-permute-start | bytes 221192 | tf_op jit(solution)/shard_map/ppermute | solution.py:77
  154.1 8.8 %collective-permute-start.47 = (bf16[144,256]{1,0:T(8,128)(2,1)S(1)}, bf16[144,256]{1,0:T(8,128)(2,1)S(1)}, u32[]{:S(2)}, u32[]{:S(2)}) collective-permute-start(bf16[144,256]{1,0:T(8,128)(2,1)S(1)} %collective-permute-done.39.refs_3_), channel_id=1, source_target_pairs={{0,8},{1,25},{8,16},{9,1},{16,24},{17,9},{24,0},{25,17},{2,10},{3,... | collective-permute-start | bytes 221192 | tf_op jit(solution)/shard_map/ppermute | solution.py:77
  161.9 7.0 %collective-permute-start.43 = (bf16[144,256]{1,0:T(8,128)(2,1)S(1)}, bf16[144,256]{1,0:T(8,128)(2,1)S(1)}, u32[]{:S(2)}, u32[]{:S(2)}) collective-permute-start(bf16[144,256]{1,0:T(8,128)(2,1)S(1)} %collective-permute-done.39.refs_3_), channel_id=1, source_target_pairs={{0,1},{1,0},{2,3},{3,2},{4,5},{5,4},{6,7},{7,6},{8,9},{9,8},{10,11... | collective-permute-start | bytes 221192 | tf_op jit(solution)/shard_map/ppermute | solution.py:69
  162.4 6.5 %collective-permute-start.48 = (bf16[144,256]{1,0:T(8,128)(2,1)S(1)}, bf16[144,256]{1,0:T(8,128)(2,1)S(1)}, u32[]{:S(2)}, u32[]{:S(2)}) collective-permute-start(bf16[144,256]{1,0:T(8,128)(2,1)S(1)} %collective-permute-done.44.refs_8_), channel_id=1, source_target_pairs={{0,1},{1,0},{2,3},{3,2},{4,5},{5,4},{6,7},{7,6},{8,9},{9,8},{10,11... | collective-permute-start | bytes 221192 | tf_op jit(solution)/shard_map/ppermute | solution.py:69
  162.5 6.4 %collective-permute-start.49 = (bf16[144,256]{1,0:T(8,128)(2,1)S(1)}, bf16[144,256]{1,0:T(8,128)(2,1)S(1)}, u32[]{:S(2)}, u32[]{:S(2)}) collective-permute-start(bf16[144,256]{1,0:T(8,128)(2,1)S(1)} %collective-permute-done.45.refs_9_), channel_id=1, source_target_pairs={{0,1},{1,0},{2,3},{3,2},{4,5},{5,4},{6,7},{7,6},{8,9},{9,8},{10,11... | collective-permute-start | bytes 221192 | tf_op jit(solution)/shard_map/ppermute | solution.py:69
  162.9 6.0 %collective-permute-start.50 = (bf16[144,256]{1,0:T(8,128)(2,1)S(1)}, bf16[144,256]{1,0:T(8,128)(2,1)S(1)}, u32[]{:S(2)}, u32[]{:S(2)}) collective-permute-start(bf16[144,256]{1,0:T(8,128)(2,1)S(1)} %collective-permute-done.46.refs_10_), channel_id=1, source_target_pairs={{0,1},{1,0},{2,3},{3,2},{4,5},{5,4},{6,7},{7,6},{8,9},{9,8},{10,11... | collective-permute-start | bytes 221192 | tf_op jit(solution)/shard_map/ppermute | solution.py:69
  163.0 5.9 %collective-permute-start.51 = (bf16[144,256]{1,0:T(8,128)(2,1)S(1)}, bf16[144,256]{1,0:T(8,128)(2,1)S(1)}, u32[]{:S(2)}, u32[]{:S(2)}) collective-permute-start(bf16[144,256]{1,0:T(8,128)(2,1)S(1)} %collective-permute-done.47.refs_11_), channel_id=1, source_target_pairs={{0,1},{1,0},{2,3},{3,2},{4,5},{5,4},{6,7},{7,6},{8,9},{9,8},{10,11... | collective-permute-start | bytes 221192 | tf_op jit(solution)/shard_map/ppermute | solution.py:69
  (14 other events, 86.4 us)
